TPU v7x, 8 devices: a whole 2x2x1 slice. The times are simulated.
8 devices in a mesh: batch: 1 (over z), row: 2 (over y), col: 4 (over x, core).
Axes of the slice: x: 2, y: 2, z: 1, core: 2. Of those that a mesh axis runs over, the one named last changes fastest.
Arguments:
- a_mat: bfloat16 [16384, 512], P(('batch', 'row'), 'col')
Outputs:
- output: bfloat16 [16384, 16384], P(('batch', 'row'), 'col')
All inputs are finite; a program needn't handle non-finite values.
Results may differ from a plain program's by a relative error of at most 0.001.
Values are sent between devices in bfloat16 or wider.
A program may use at most 1 GiB of HBM per device.

v0:
```python
import jax
import jax.numpy as jnp
from jax import lax
from jax.sharding import PartitionSpec as P

BLOCK = 256


def lower_part(row_panel, col_panel, row_step, row_pos, col_step, col_pos):
    row_blocks = row_panel.shape[0] // BLOCK
    col_blocks = col_panel.shape[0] // BLOCK
    col_total = col_panel.shape[0]
    band_size = max(1, row_blocks // 8)
    col_local = jnp.arange(col_total)
    col_index = ((col_local // BLOCK) * col_step + col_pos) * BLOCK + col_local % BLOCK
    pieces = []
    for first_blk in range(0, row_blocks, band_size):
        last_blk = min(first_blk + band_size, row_blocks)
        col_width = BLOCK * min(col_blocks, (last_blk * row_step - 1) // col_step + 1)
        product = lax.dot_general(row_panel[first_blk * BLOCK:last_blk * BLOCK], col_panel[:col_width], (((1,), (1,)), ((), ())), preferred_element_type=jnp.float32)
        row_local = jnp.arange(first_blk * BLOCK, last_blk * BLOCK)
        row_index = ((row_local // BLOCK) * row_step + row_pos) * BLOCK + row_local % BLOCK
        kept_vals = jnp.where(row_index[:, None] >= col_index[None, :col_width], product, 0.0).astype(jnp.bfloat16)
        pieces.append(jnp.pad(kept_vals, ((0, 0), (0, col_total - col_width))))
    return jnp.concatenate(pieces, axis=0)


def solution(mesh):
    row_count = mesh.shape['row']
    col_count = mesh.shape['col']

    def local_fn(a_local):
        local_rows, m_local = a_local.shape
        n_total = local_rows * row_count
        row_pos = lax.axis_index('row')
        col_pos = lax.axis_index('col')
        row_panel = lax.all_gather(a_local, 'col', axis=1, tiled=True)
        gathered = lax.all_gather(a_local.reshape(local_rows // BLOCK, BLOCK, m_local), 'row', axis=1)
        grouped = gathered.reshape(n_total // (BLOCK * col_count), col_count, BLOCK, m_local)
        swapped = lax.all_to_all(grouped, 'col', 1, 3, tiled=True)
        col_panel = swapped.reshape(n_total // col_count, m_local * col_count)
        return lower_part(row_panel, col_panel, row_count, row_pos, col_count, col_pos)

    part_spec = P(('batch', 'row'), 'col')
    return jax.shard_map(local_fn, mesh=mesh, in_specs=(part_spec,), out_specs=part_spec, check_vma=False)
```

profile of v0, /device:TPU:0, one launch (start us, length us, event | category | flops | bytes accessed | tf_op | source)
XLA Modules:
  0.0 305.5 jit_solution(7360151584337444951)
XLA Ops:
  6.5 0.0 all-gather.5.cloned.1.call-start
  6.5 0.7 all-gather.5.cloned.1.call-update
  7.3 0.0 all-gather.3.cloned.1.call-start
  7.3 0.7 all-gather.3.cloned.1.call-update
  8.0 57.9 %all-gather.5.cloned.1.call-done = bf16[32,2,256,128]{3,2,1,0:T(8,128)(2,1)} async-done(((bf16[32,1,256,128]{3,2,1,0:T(8,128)(2,1)}), bf16[32,2,256,128]{3,2,1,0:T(8,128)(2,1)}) %all-gather.5.cloned.1.call-update) | async-done | bytes 4194320 | tf_op jit(solution)/shard_map/all_gather | solution.py:38
  65.9 4.7 %copy.10 = bf16[16,4,256,128]{3,2,0,1:T(8,128)(2,1)} copy(bf16[16,4,256,128]{3,2,1,0:T(8,128)(2,1)} %bitcast.58) | data formatting | bytes 8388608 | tf_op jit(solution)/shard_map/reshape | solution.py:39
  70.6 4.9 %all-to-all-start = ((bf16[16,4,256,128]{3,2,0,1:T(8,128)(2,1)}), bf16[16,4,256,128]{3,2,0,1:T(8,128)(2,1)}, u32[]{:S(2)}, u32[]{:S(2)}) async-start(bf16[16,4,256,128]{3,2,0,1:T(8,128)(2,1)} %copy.10), calls=%async_computation | async-start | bytes 8388608 | tf_op jit(solution)/shard_map/all_to_all | solution.py:40
  75.5 0.0 copy-start.8
  75.6 90.8 %all-to-all-done = bf16[16,4,256,128]{3,2,0,1:T(8,128)(2,1)} async-done(((bf16[16,4,256,128]{3,2,0,1:T(8,128)(2,1)}), bf16[16,4,256,128]{3,2,0,1:T(8,128)(2,1)}, u32[]{:S(2)}, u32[]{:S(2)}) %all-to-all-start) | async-done | bytes 4194336 | tf_op jit(solution)/shard_map/all_to_all | solution.py:40
  166.4 1.9 slice.118
  168.3 2.3 slice.121
  170.6 2.7 slice.124
  173.3 3.1 %slice.127 = bf16[8,1,256,4,128]{4,2,0,3,1:T(8,128)(2,1)} slice(bf16[16,1,256,4,128]{4,2,0,3,1:T(8,128)(2,1)} %bitcast.3), slice={[0:8], [0:1], [0:256], [0:4], [0:128]} | slice | bytes 4194304 | tf_op jit(solution)/shard_map/slice | solution.py:20
  176.5 3.6 %slice.130 = bf16[10,1,256,4,128]{4,2,0,3,1:T(8,128)(2,1)} slice(bf16[16,1,256,4,128]{4,2,0,3,1:T(8,128)(2,1)} %bitcast.3), slice={[0:10], [0:1], [0:256], [0:4], [0:128]} | slice | bytes 5242880 | tf_op jit(solution)/shard_map/slice | solution.py:20
  180.0 0.0 copy-done.8
  180.0 2.1 slice.133
  182.1 4.3 %slice.136 = bf16[14,1,256,4,128]{4,2,0,3,1:T(8,128)(2,1)} slice(bf16[16,1,256,4,128]{4,2,0,3,1:T(8,128)(2,1)} %bitcast.3), slice={[0:14], [0:1], [0:256], [0:4], [0:128]} | slice | bytes 7340032 | tf_op jit(solution)/shard_map/slice | solution.py:20
  186.4 7.8 %copy.18 = bf16[16,1,256,4,128]{2,0,4,3,1:T(8,128)(2,1)} copy(bf16[16,1,256,4,128]{4,2,0,3,1:T(8,128)(2,1)} %bitcast.3) | data formatting | bytes 8388608 | tf_op jit(solution)/shard_map/all_to_all | solution.py:40
  194.2 2.3 copy.11
  196.5 3.0 copy.12
  199.5 3.8 %copy.13 = bf16[6,1,256,4,128]{4,3,2,0,1:T(4,128)(2,1)} copy(bf16[6,1,256,4,128]{4,2,0,3,1:T(8,128)(2,1)} %slice.124) | data formatting | bytes 3145728 | tf_op jit(solution)/shard_map/slice | solution.py:20
  203.3 4.6 %copy.14 = bf16[8,1,256,4,128]{2,0,4,3,1:T(8,128)(2,1)} copy(bf16[8,1,256,4,128]{4,2,0,3,1:T(8,128)(2,1)} %slice.127) | data formatting | bytes 4194304 | tf_op jit(solution)/shard_map/slice | solution.py:20
  207.9 3.8 %copy.22 = bf16[64,8,8,256]{3,1,2,0:T(8,128)(2,1)} copy(bf16[64,8,8,256]{3,2,1,0:T(8,128)(2,1)} %bitcast.56) | data formatting | bytes 4194304
  211.7 5.3 %copy.15 = bf16[10,1,256,4,128]{4,3,2,0,1:T(4,128)(2,1)} copy(bf16[10,1,256,4,128]{4,2,0,3,1:T(8,128)(2,1)} %slice.130) | data formatting | bytes 5242880 | tf_op jit(solution)/shard_map/slice | solution.py:20
  217.0 4.1 %copy.16 = bf16[12,1,256,4,128]{4,3,2,0,1:T(4,128)(2,1)} copy(bf16[12,1,256,4,128]{4,2,0,3,1:T(8,128)(2,1)S(1)} %slice.133) | data formatting | bytes 6291456 | tf_op jit(solution)/shard_map/slice | solution.py:20
  221.1 0.0 copy-done.1
  221.1 4.7 %copy.17 = bf16[14,1,256,4,128]{4,3,2,0,1:T(4,128)(2,1)} copy(bf16[14,1,256,4,128]{4,2,0,3,1:T(8,128)(2,1)S(1)} %copy-done.1) | data formatting | bytes 7340032 | tf_op jit(solution)/shard_map/slice | solution.py:20
  225.8 0.0 copy-done
  225.8 4.2 %copy.26 = bf16[64,8,16,256]{3,1,2,0:T(8,128)(2,1)} copy(bf16[64,8,16,256]{3,2,1,0:T(8,128)(2,1)S(1)} %bitcast.54) | data formatting | bytes 8388608
  230.0 0.0 copy-done.7
  230.0 0.0 slice-done
  230.0 2.1 select_convert_fusion.7
  232.1 4.5 %pad_dynamic-update-slice_fusion.6 = bf16[8192,4096]{1,0:T(8,128)(2,1)} fusion(bf16[1024,512]{1,0:T(8,128)(2,1)S(1)} %select_convert_fusion.7), kind=kLoop, calls=%fused_computation.12 | loop fusion | bytes 9437184
  236.6 0.0 copy-done.6
  236.6 0.0 slice-done.1
  236.6 2.5 select_convert_fusion.6
  239.1 0.0 copy-start.5
  239.1 0.0 slice-start.2
  239.1 4.4 %pad_dynamic-update-slice_fusion.5 = bf16[8192,4096]{1,0:T(8,128)(2,1)} fusion(bf16[8192,4096]{1,0:T(8,128)(2,1)} %pad_dynamic-update-slice_fusion.6, bf16[1024,1024]{1,0:T(8,128)(2,1)S(1)} %select_convert_fusion.6), kind=kLoop, calls=%fused_computation.11 | loop fusion | bytes 10485760
  243.5 0.0 copy-done.5
  243.5 0.0 slice-done.2
  243.5 3.1 %select_convert_fusion.5 = bf16[1024,1536]{1,0:T(8,128)(2,1)S(1)} fusion(s32[1536]{0:T(1024)S(1)} %slice-done.2, s32[1024]{0:T(1024)S(1)} %get-tuple-element.7, bf16[192,8,4,128]{3,2,1,0:T(4,128)(2,1)S(1)} %bitcast.63, bf16[8192,512]{1,0:T(8,128)(2,1)} %all-gather.3.cloned.1.call-done), kind=kOutput, calls=%fused_computation.13 | convolution fusion | flops 1615331328 | bytes 5777408 | tf_op jit(solution)/shard_map/dot_general | solution.py:20
  246.5 0.0 copy-start.4
  246.5 0.0 slice-start.3
  246.6 4.5 %pad_dynamic-update-slice_fusion.4 = bf16[8192,4096]{1,0:T(8,128)(2,1)} fusion(bf16[8192,4096]{1,0:T(8,128)(2,1)} %pad_dynamic-update-slice_fusion.5, bf16[1024,1536]{1,0:T(8,128)(2,1)S(1)} %select_convert_fusion.5), kind=kLoop, calls=%fused_computation.10 | loop fusion | bytes 11534336
  251.0 0.0 copy-done.4
  251.0 0.0 slice-done.3
  251.0 3.6 %select_convert_fusion.4 = bf16[1024,2048]{1,0:T(8,128)(2,1)S(1)} fusion(s32[2048]{0:T(1024)S(1)} %slice-done.3, s32[1024]{0:T(1024)S(1)} %get-tuple-element.8, bf16[2048,512]{0,1:T(8,128)(2,1)S(1)} %bitcast.62, bf16[8192,512]{1,0:T(8,128)(2,1)} %all-gather.3.cloned.1.call-done), kind=kOutput, calls=%fused_computation.9 | convolution fusion | flops 2153775104 | bytes 7352320 | tf_op jit(solution)/shard_map/dot_general | solution.py:20
  254.6 0.0 copy-start.3
  254.6 0.0 slice-start.4
  254.6 4.2 %pad_dynamic-update-slice_fusion.3 = bf16[8192,4096]{1,0:T(8,128)(2,1)} fusion(bf16[8192,4096]{1,0:T(8,128)(2,1)} %pad_dynamic-update-slice_fusion.4, bf16[1024,2048]{1,0:T(8,128)(2,1)S(1)} %select_convert_fusion.4), kind=kLoop, calls=%fused_computation.8 | loop fusion | bytes 12582912
  258.9 0.0 copy-done.3
  258.9 0.0 slice-done.4
  258.9 4.1 %select_convert_fusion.3 = bf16[1024,2560]{1,0:T(8,128)(2,1)S(1)} fusion(s32[2560]{0:T(1024)S(1)} %slice-done.4, s32[1024]{0:T(1024)S(1)} %get-tuple-element.9, bf16[320,8,4,128]{3,2,1,0:T(4,128)(2,1)S(1)} %bitcast.61, bf16[8192,512]{1,0:T(8,128)(2,1)} %all-gather.3.cloned.1.call-done), kind=kOutput, calls=%fused_computation.3 | convolution fusion | flops 2692218880 | bytes 8927232 | tf_op jit(solution)/shard_map/dot_general | solution.py:20
  263.0 0.0 copy-start.2
  263.0 0.0 slice-start.5
  263.0 4.6 %pad_dynamic-update-slice_fusion.2 = bf16[8192,4096]{1,0:T(8,128)(2,1)} fusion(bf16[8192,4096]{1,0:T(8,128)(2,1)} %pad_dynamic-update-slice_fusion.3, bf16[1024,2560]{1,0:T(8,128)(2,1)S(1)} %select_convert_fusion.3), kind=kLoop, calls=%fused_computation.7 | loop fusion | bytes 13631488
  267.6 0.0 copy-done.2
  267.6 0.0 slice-done.5
  267.6 5.3 %select_convert_fusion.2 = bf16[1024,3072]{1,0:T(8,128)(2,1)S(1)} fusion(s32[3072]{0:T(1024)S(1)} %slice-done.5, s32[1024]{0:T(1024)S(1)} %get-tuple-element.10, bf16[384,8,4,128]{3,2,1,0:T(4,128)(2,1)S(1)} %bitcast.60, bf16[8192,512]{1,0:T(8,128)(2,1)} %all-gather.3.cloned.1.call-done), kind=kOutput, calls=%fused_computation.2 | convolution fusion | flops 3230662656 | bytes 10502144 | tf_op jit(solution)/shard_map/dot_general | solution.py:20
  272.9 4.3 %pad_dynamic-update-slice_fusion.1 = bf16[8192,4096]{1,0:T(8,128)(2,1)} fusion(bf16[8192,4096]{1,0:T(8,128)(2,1)} %pad_dynamic-update-slice_fusion.2, bf16[1024,3072]{1,0:T(8,128)(2,1)S(1)} %select_convert_fusion.2), kind=kLoop, calls=%fused_computation.6 | loop fusion | bytes 14680064
  277.2 6.4 %select_convert_fusion.1 = bf16[1024,3584]{1,0:T(8,128)(2,1)S(1)} fusion(s32[3584]{0:T(1024)S(1)} %bitcast.66, s32[1024]{0:T(1024)S(1)} %get-tuple-element.11, bf16[448,8,4,128]{3,2,1,0:T(4,128)(2,1)} %bitcast.59, bf16[8192,512]{1,0:T(8,128)(2,1)} %all-gather.3.cloned.1.call-done), kind=kOutput, calls=%fused_computation.1 | convolution fusion | flops 3769106432 | bytes 12077056 | tf_op jit(solution)/shard_map/dot_general | solution.py:20
  283.6 4.7 %pad_dynamic-update-slice_fusion = bf16[8192,4096]{1,0:T(8,128)(2,1)} fusion(bf16[8192,4096]{1,0:T(8,128)(2,1)} %pad_dynamic-update-slice_fusion.1, bf16[1024,3584]{1,0:T(8,128)(2,1)S(1)} %select_convert_fusion.1), kind=kLoop, calls=%fused_computation.5 | loop fusion | bytes 15728640
  288.2 10.4 %fusion = bf16[8192,4096]{1,0:T(8,128)(2,1)} fusion(bf16[8192,4096]{1,0:T(8,128)(2,1)} %pad_dynamic-update-slice_fusion, s32[4096]{0:T(1024)S(1)} %copy-done.9, s32[1024]{0:T(1024)S(1)} %get-tuple-element.12, bf16[4096,512]{0,1:T(8,128)(2,1)} %bitcast.57, bf16[8192,512]{1,0:T(8,128)(2,1)} %all-gather.3.cloned.1.call-done), kind=kOutput, calls=%fused_computation.4 | convolution fusion | flops 4307550208 | bytes 13651968 | tf_op jit(solution)/shard_map/dot_general | solution.py:20
  (14 shorter events, 0.1 us)
Async XLA Ops:
  6.5 59.4 %all-gather.5.cloned.1.call-start = ((), (), s32[]{:S(2)}) async-start(), calls=%async_computation.2 | async-start | bytes 6291456 | tf_op jit(solution)/shard_map/all_gather | solution.py:38
  7.3 222.8 %all-gather.3.cloned.1.call-start = ((), (), s32[]{:S(2)}) async-start(), calls=%async_computation.1 | async-start | bytes 10485760 | tf_op jit(solution)/shard_map/all_gather | solution.py:37
  70.6 95.8 %all-to-all-start = ((bf16[16,4,256,128]{3,2,0,1:T(8,128)(2,1)}), bf16[16,4,256,128]{3,2,0,1:T(8,128)(2,1)}, u32[]{:S(2)}, u32[]{:S(2)}) async-start(bf16[16,4,256,128]{3,2,0,1:T(8,128)(2,1)} %copy.10), calls=%async_computation | async-start | bytes 8388608 | tf_op jit(solution)/shard_map/all_to_all | solution.py:40
  75.5 104.5 %copy-start.8 = (s32[4096]{0:T(1024)}, s32[4096]{0:T(1024)S(1)}, u32[]{:S(2)}) copy-start(s32[4096]{0:T(1024)S(1)} %fusion.30) | copy-start | bytes 49156
  207.9 13.2 %copy-start.1 = (bf16[14,1,256,4,128]{4,2,0,3,1:T(8,128)(2,1)S(1)}, bf16[14,1,256,4,128]{4,2,0,3,1:T(8,128)(2,1)}, u32[]{:S(2)}) copy-start(bf16[14,1,256,4,128]{4,2,0,3,1:T(8,128)(2,1)} %slice.136) | copy-start | bytes 11010052
  217.0 8.8 %copy-start = (bf16[16,1,256,4,128]{2,0,4,3,1:T(8,128)(2,1)S(1)}, bf16[16,1,256,4,128]{2,0,4,3,1:T(8,128)(2,1)}, u32[]{:S(2)}) copy-start(bf16[16,1,256,4,128]{2,0,4,3,1:T(8,128)(2,1)} %copy.18) | copy-start | bytes 12582916
  221.1 8.9 %copy-start.7 = (bf16[2,1,256,4,128]{4,3,2,0,1:T(4,128)(2,1)S(1)}, bf16[2,1,256,4,128]{4,3,2,0,1:T(4,128)(2,1)}, u32[]{:S(2)}) copy-start(bf16[2,1,256,4,128]{4,3,2,0,1:T(4,128)(2,1)} %copy.11) | copy-start | bytes 1572868
  221.1 8.9 %slice-start = ((s32[4096]{0:T(1024)}), s32[512]{0:T(512)S(1)}, s32[]{:S(2)}) async-start(s32[4096]{0:T(1024)} %copy-done.8), calls=%async_computation.3 | async-start | bytes 4096 | tf_op jit(solution)/shard_map/slice | solution.py:23
  230.0 6.5 %copy-start.6 = (bf16[4,1,256,4,128]{4,3,2,0,1:T(4,128)(2,1)S(1)}, bf16[4,1,256,4,128]{4,3,2,0,1:T(4,128)(2,1)}, u32[]{:S(2)}) copy-start(bf16[4,1,256,4,128]{4,3,2,0,1:T(4,128)(2,1)} %copy.12) | copy-start | bytes 3145732
  230.0 6.6 %slice-start.1 = ((s32[4096]{0:T(1024)}), s32[1024]{0:T(1024)S(1)}, s32[]{:S(2)}) async-start(s32[4096]{0:T(1024)} %copy-done.8), calls=%async_computation.4 | async-start | bytes 8192 | tf_op jit(solution)/shard_map/slice | solution.py:23
  239.1 4.4 %copy-start.5 = (bf16[6,1,256,4,128]{4,3,2,0,1:T(4,128)(2,1)S(1)}, bf16[6,1,256,4,128]{4,3,2,0,1:T(4,128)(2,1)}, u32[]{:S(2)}) copy-start(bf16[6,1,256,4,128]{4,3,2,0,1:T(4,128)(2,1)} %copy.13) | copy-start | bytes 4718596
  239.1 4.4 %slice-start.2 = ((s32[4096]{0:T(1024)}), s32[1536]{0:T(1024)S(1)}, s32[]{:S(2)}) async-start(s32[4096]{0:T(1024)} %copy-done.8), calls=%async_computation.5 | async-start | bytes 16384 | tf_op jit(solution)/shard_map/slice | solution.py:23
  246.5 4.5 %copy-start.4 = (bf16[64,8,8,256]{3,1,2,0:T(8,128)(2,1)S(1)}, bf16[64,8,8,256]{3,1,2,0:T(8,128)(2,1)}, u32[]{:S(2)}) copy-start(bf16[64,8,8,256]{3,1,2,0:T(8,128)(2,1)} %copy.22) | copy-start | bytes 6291460
  246.5 4.5 %slice-start.3 = ((s32[4096]{0:T(1024)}), s32[2048]{0:T(1024)S(1)}, s32[]{:S(2)}) async-start(s32[4096]{0:T(1024)} %copy-done.8), calls=%async_computation.6 | async-start | bytes 16384 | tf_op jit(solution)/shard_map/slice | solution.py:23
  254.6 4.3 %copy-start.3 = (bf16[10,1,256,4,128]{4,3,2,0,1:T(4,128)(2,1)S(1)}, bf16[10,1,256,4,128]{4,3,2,0,1:T(4,128)(2,1)}, u32[]{:S(2)}) copy-start(bf16[10,1,256,4,128]{4,3,2,0,1:T(4,128)(2,1)} %copy.15) | copy-start | bytes 7864324
  254.6 4.3 %slice-start.4 = ((s32[4096]{0:T(1024)}), s32[2560]{0:T(1024)S(1)}, s32[]{:S(2)}) async-start(s32[4096]{0:T(1024)} %copy-done.8), calls=%async_computation.7 | async-start | bytes 24576 | tf_op jit(solution)/shard_map/slice | solution.py:23
  263.0 4.6 %copy-start.2 = (bf16[12,1,256,4,128]{4,3,2,0,1:T(4,128)(2,1)S(1)}, bf16[12,1,256,4,128]{4,3,2,0,1:T(4,128)(2,1)}, u32[]{:S(2)}) copy-start(bf16[12,1,256,4,128]{4,3,2,0,1:T(4,128)(2,1)} %copy.16) | copy-start | bytes 9437188
  263.0 4.6 %slice-start.5 = ((s32[4096]{0:T(1024)}), s32[3072]{0:T(1024)S(1)}, s32[]{:S(2)}) async-start(s32[4096]{0:T(1024)} %copy-done.8), calls=%async_computation.8 | async-start | bytes 24576 | tf_op jit(solution)/shard_map/slice | solution.py:23
  272.9 4.3 %copy-start.9 = (s32[4096]{0:T(1024)S(1)}, s32[4096]{0:T(1024)}, u32[]{:S(2)}) copy-start(s32[4096]{0:T(1024)} %copy-done.8) | copy-start | bytes 49156
Sparse Core Ops, SparseCore 0:
  8.8 57.0 all-gather.4
  67.4 100.2 all-gather.2
where the time goes:
time: 307 us; the launch traced here: 306 us
  waiting for transfers between devices  150 us (49%)
  local copies, waits for them, and re-layouts  99.4 us (32%)
  matrix products  37.4 us (12%)
  between operations  13.6 us (4%)
  starting transfers between devices  4.94 us (2%)
    all_to_all x1, waiting for transfers between devices, local_fn(): swapped = lax.all_to_all(grouped, 'col', 1, 3, tiled=True)  90.8 us
    all_gather x1, waiting for transfers between devices, local_fn(): lax.all_gather(a_local.reshape(local_rows // BLOCK, BLOCK, m_local), 'row...  57.9 us
    slice x14, local copies, waits for them, and re-layouts, lower_part(): col_panel[:col_width]  47.8 us
    unnamed x29, local copies, waits for them, and re-layouts  39.1 us
    dot_general x8, matrix products, lower_part(): lax.dot_general(row_panel[first_blk * BLOCK:last_blk * BLOCK], col_panel[...  37.4 us
    all_to_all x1, local copies, waits for them, and re-layouts, local_fn(): swapped = lax.all_to_all(grouped, 'col', 1, 3, tiled=True)  7.83 us
  transfers between devices with their start and end apart: 3, of which 2 were waited for; matrix products, arithmetic and copies ran while one was open for 22% of the time, Pallas kernels for 0%

commit v1 on v0

v1 whole, which is shorter than its diff:
```python
import functools
import jax
import jax.numpy as jnp
from jax import lax
from jax.experimental import pallas as pl
from jax.experimental.pallas import tpu as pltpu
from jax.sharding import PartitionSpec as P

BLOCK = 256
K_DIM = 512
PIECE = 128
NM = 16
CH = 4
NC = NM // CH
NBUF = 3
AXES = ('row', 'col')


def flat(y, x, k):
    return y * 4 + x * 2 + k


ALL = [(y, x, k) for y in range(2) for x in range(2) for k in range(2)]
PERM_PARTNER = [(flat(y, x, k), flat(y, x, 1 - k)) for y, x, k in ALL]
PERM_X = [(flat(y, x, k), flat(y, 1 - x, k)) for y, x, k in ALL]
PERM_YA = [(flat(y, x, y), flat(1 - y, x, y)) for y in range(2) for x in range(2)]
PERM_YB = [(flat(y, x, 1 - y), flat(1 - y, x, y)) for y in range(2) for x in range(2)]


def positions():
    y = lax.axis_index('row')
    col = lax.axis_index('col')
    return y, col // 2, col % 2, col


def zero_kernel(c_ref, zbuf, sem):
    zbuf[...] = jnp.zeros_like(zbuf)
    copies = []
    for i in range(NC):
        for j in range(i + 1, NC):
            cp = pltpu.make_async_copy(zbuf, c_ref.at[pl.ds(CH * i, CH), :, :, pl.ds(j * CH * BLOCK, CH * BLOCK)], sem)
            cp.start()
            copies.append(cp)
    for cp in copies:
        cp.wait()


def lookup(job, values):
    out = jnp.int32(values[-1]) if values else jnp.int32(0)
    for n in range(len(values) - 2, -1, -1):
        out = jnp.where(job == n, jnp.int32(values[n]), out)
    return out


def stage_kernel(jobs_m, jobs_u, n_in, srcs, *refs):
    ins = refs[:n_in]
    c_ref = refs[n_in + 1]
    panels, obuf, lsem, osem, seen = refs[n_in + 2:]
    y, x, k, col = positions()
    matched = k == y
    cp = jnp.where(matched, 0, 2)

    def load(panel, chunk, start):
        for p in range(4):
            ref, kind = ins[srcs[(panel, chunk, p)][0]], srcs[(panel, chunk, p)][1]
            if kind == 'local':
                s = x if panel == 0 else 1 - x
                src = ref.at[pl.ds(CH * chunk, CH), s]
            elif kind == 'full':
                src = ref.at[pl.ds(CH * chunk, CH)]
            else:
                src = ref
            pltpu.make_async_copy(src, panels.at[panel, pl.ds(CH * chunk, CH), :, pl.ds(p * PIECE, PIECE)], lsem.at[panel * NC + chunk]).start()

    def need(jobs, is_matched):
        order = []
        for rp, i, j in jobs:
            for item in ((rp, i), (0 if is_matched else 2, j)):
                if item not in order:
                    order.append(item)
        return order

    for n in range(3 * NC):
        seen[n] = 0

    @pl.when(matched)
    def _():
        for panel, chunk in need(jobs_m, True):
            load(panel, chunk, True)

    @pl.when(jnp.logical_not(matched))
    def _():
        for panel, chunk in need(jobs_u, False):
            load(panel, chunk, True)

    n_jobs = jnp.where(matched, len(jobs_m), len(jobs_u))

    def ensure(panel, chunk):
        idx = panel * NC + chunk

        @pl.when(seen[idx] == 0)
        def _():
            ref = panels.at[panel, pl.ds(CH * chunk, CH)]
            pltpu.make_async_copy(ref, ref, lsem.at[idx]).wait()
            seen[idx] = 1

    def out_copy(b, rp, i, j):
        s = jnp.where(rp == 0, x, 1 - x)
        return pltpu.make_async_copy(obuf.at[b], c_ref.at[pl.ds(CH * i, CH), s, :, pl.ds(pl.multiple_of(j * CH * BLOCK, CH * BLOCK), CH * BLOCK)], osem.at[b])

    def body(job, _):
        def pick(f):
            vm = lookup(job, [f(v) for v in jobs_m])
            vu = lookup(job, [f(v) for v in jobs_u])
            return jnp.where(matched, vm, vu)
        rp = pick(lambda v: v[0])
        i = pick(lambda v: v[1])
        j = pick(lambda v: v[2])
        b = lax.rem(job, NBUF)
        ensure(rp, i)
        ensure(cp, j)

        @pl.when(job >= NBUF)
        def _():
            out_copy(b, rp, i, j).wait()

        @pl.when(i != j)
        def _():
            rows = panels[rp, pl.ds(CH * i, CH)].reshape(CH * BLOCK, K_DIM)
            cols = panels[cp, pl.ds(CH * j, CH)].reshape(CH * BLOCK, K_DIM)
            prod = lax.dot_general(rows, cols, (((1,), (1,)), ((), ())), preferred_element_type=jnp.float32)
            obuf[b] = prod.astype(jnp.bfloat16).reshape(CH, BLOCK, CH * BLOCK)

        @pl.when(i == j)
        def _():
            s = jnp.where(rp == 0, x, 1 - x)
            for q in range(CH):
                rows = panels[rp, pl.ds(CH * i + q, CH - q)].reshape((CH - q) * BLOCK, K_DIM)
                cols = panels[cp, CH * j + q]
                prod = lax.dot_general(rows, cols, (((1,), (1,)), ((), ())), preferred_element_type=jnp.float32)
                row_id = lax.broadcasted_iota(jnp.int32, (BLOCK, BLOCK), 0) + (2 * s + y) * BLOCK
                col_id = lax.broadcasted_iota(jnp.int32, (BLOCK, BLOCK), 1) + col * BLOCK
                head = jnp.where(row_id >= col_id, prod[:BLOCK], 0.0)
                obuf[b, q, :, q * BLOCK:(q + 1) * BLOCK] = head.astype(jnp.bfloat16)
                if q + 1 < CH:
                    obuf[b, q + 1:, :, q * BLOCK:(q + 1) * BLOCK] = prod[BLOCK:].astype(jnp.bfloat16).reshape(CH - q - 1, BLOCK, BLOCK)
                if q:
                    obuf[b, :q, :, q * BLOCK:(q + 1) * BLOCK] = jnp.zeros((q, BLOCK, BLOCK), jnp.bfloat16)
        out_copy(b, rp, i, j).start()
        return 0

    lax.fori_loop(0, n_jobs, body, 0)
    for b in range(NBUF):
        @pl.when(n_jobs > b)
        def _():
            out_copy(b, 0, 0, 0).wait()


def run_stage(c, jobs_m, jobs_u, arrays, srcs):
    any_spec = pl.BlockSpec(memory_space=pl.ANY)
    tiles = max(sum(10 if i == j else 16 for _, i, j in jobs) for jobs in (jobs_m, jobs_u))
    flops = tiles * 2 * BLOCK * BLOCK * K_DIM
    return pl.pallas_call(
        functools.partial(stage_kernel, jobs_m, jobs_u, len(arrays), srcs),
        out_shape=jax.ShapeDtypeStruct(c.shape, c.dtype),
        in_specs=[any_spec] * (len(arrays) + 1),
        out_specs=any_spec,
        input_output_aliases={len(arrays): 0},
        scratch_shapes=[
            pltpu.VMEM((3, NM, BLOCK, K_DIM), jnp.bfloat16),
            pltpu.VMEM((NBUF, CH, BLOCK, CH * BLOCK), jnp.bfloat16),
            pltpu.SemaphoreType.DMA((3 * NC,)),
            pltpu.SemaphoreType.DMA((NBUF,)),
            pltpu.SMEM((3 * NC,), jnp.int32),
        ],
        compiler_params=pltpu.CompilerParams(vmem_limit_bytes=48 * 1024 * 1024),
        cost_estimate=pl.CostEstimate(flops=flops, bytes_accessed=tiles * BLOCK * BLOCK * 2, transcendentals=0),
    )(*arrays, c)


def solution(mesh):
    def local_fn(a):
        y, x, k, col = positions()
        a4 = a.reshape(NM, 2, BLOCK, PIECE)
        same = lax.dynamic_index_in_dim(a4, x, 1, keepdims=False)
        other = lax.dynamic_index_in_dim(a4, 1 - x, 1, keepdims=False)
        part = lax.ppermute(a, AXES, PERM_PARTNER).reshape(NM, 2, BLOCK, PIECE)
        xa = lax.ppermute(other, AXES, PERM_X)
        y0a = lax.ppermute(same, AXES, PERM_YA)
        y0b = lax.ppermute(same, AXES, PERM_YB)
        xb = [None] * NC
        for u in range(NC):
            i = NC - 1 - u
            xb[i] = lax.ppermute(same[CH * i:CH * (i + 1)], AXES, PERM_X)
        xap = lax.ppermute(xa, AXES, PERM_PARTNER)
        y2a, y2b, xbp = [None] * NC, [None] * NC, [None] * NC
        for u in range(NC):
            y2a[u] = lax.ppermute(xa[CH * u:CH * (u + 1)], AXES, PERM_YA)
            y2b[u] = lax.ppermute(xa[CH * u:CH * (u + 1)], AXES, PERM_YB)
            i = NC - 1 - u
            xbp[i] = lax.ppermute(xb[i], AXES, PERM_PARTNER)

        any_spec = pl.BlockSpec(memory_space=pl.ANY)
        c = pl.pallas_call(
            zero_kernel,
            out_shape=jax.ShapeDtypeStruct((NM, 2, BLOCK, NM * BLOCK), jnp.bfloat16),
            out_specs=any_spec,
            scratch_shapes=[pltpu.VMEM((CH, 2, BLOCK, CH * BLOCK), jnp.bfloat16), pltpu.SemaphoreType.DMA],
            cost_estimate=pl.CostEstimate(flops=9_000_000_000, bytes_accessed=24 << 20, transcendentals=0),
        )()

        def sources(arrays):
            srcs = {}
            names = {id(v): n for n, v in enumerate(arrays)}

            def put(key, arr, kind):
                if id(arr) in names:
                    srcs[key] = (names[id(arr)], kind)
            for ch in range(NC):
                for panel in (0, 1):
                    put((panel, ch, 0), a4, 'local')
                    put((panel, ch, 1), part, 'local')
                put((0, ch, 2), xa, 'full')
                put((0, ch, 3), xap, 'full')
                put((1, ch, 2), xb[ch], 'chunk')
                put((1, ch, 3), xbp[ch], 'chunk')
                put((2, ch, 0), y0a, 'full')
                put((2, ch, 1), y0b, 'full')
                put((2, ch, 2), y2a[ch], 'chunk')
                put((2, ch, 3), y2b[ch], 'chunk')
            return srcs

        base = [a4, part, xa, xap]
        jobs0 = [(0, i, j) for i in range(NC) for j in range(i + 1)]
        c = run_stage(c, jobs0, [], base, sources(base))
        for u in range(NC):
            i_new = NC - 1 - u
            jobs_m = [(1, i_new, j) for j in range(i_new + 1)]
            jobs_u = [(0, i, u) for i in range(u, NC)]
            for i in range(i_new, NC):
                js = range(min(u, i) + 1) if i == i_new else ([u] if u <= i else [])
                jobs_u += [(1, i, j) for j in js]
            arrays = base + [y0a, y0b] + xb[i_new:] + xbp[i_new:] + y2a[:u + 1] + y2b[:u + 1]
            c = run_stage(c, jobs_m, jobs_u, arrays, sources(arrays))
        return c.reshape(2 * NM * BLOCK, NM * BLOCK)

    spec = P(('batch', 'row'), 'col')
    return jax.shard_map(local_fn, mesh=mesh, in_specs=(spec,), out_specs=spec, check_vma=False)
```

time: 307 us -> 124 us (0.40)
  the two profiles are of different devices: /device:TPU:0 before, /device:TPU:1 now
where the time goes in v1:
time: 124 us
  starting transfers between devices  47 us (38%)
  Pallas kernels  43.2 us (35%)
  waiting for transfers between devices  29.1 us (23%)
  local copies, waits for them, and re-layouts  4.11 us (3%)
    pallas_call x5, Pallas kernels, run_stage(): pl.pallas_call(functools.partial(stage_kernel, jobs_m, jobs_u, len(arrays...  34.5 us
    ppermute x4, waiting for transfers between devices, local_fn(): xb[i] = lax.ppermute(same[CH * i:CH * (i + 1)], AXES, PERM_X)  25.1 us
    ppermute x4, starting transfers between devices, local_fn(): xbp[i] = lax.ppermute(xb[i], AXES, PERM_PARTNER)  17.8 us
    ppermute x4, starting transfers between devices, local_fn(): y2b[u] = lax.ppermute(xa[CH * u:CH * (u + 1)], AXES, PERM_YB)  11 us
    pallas_call x1, Pallas kernels, local_fn(): pl.pallas_call(zero_kernel, out_shape=jax.ShapeDtypeStruct((NM, 2, BLOCK,...  8.72 us
    ppermute x4, starting transfers between devices, local_fn(): y2a[u] = lax.ppermute(xa[CH * u:CH * (u + 1)], AXES, PERM_YA)  5.17 us
    ppermute x1, waiting for transfers between devices, local_fn(): y0a = lax.ppermute(same, AXES, PERM_YA)  3.25 us
    unnamed x7, local copies, waits for them, and re-layouts  3.11 us
  transfers between devices with their start and end apart: 21, of which 3 were waited for; matrix products, arithmetic and copies ran while one was open for 1% of the time, Pallas kernels for 30%

profile of v1, /device:TPU:1, one launch (start us, length us, event | category | flops | bytes accessed | tf_op | source)
XLA Modules:
  0.0 123.8 jit_solution(974293141982784028)
XLA Ops:
  0.0 0.0 copy-start
  0.0 3.1 %dynamic-slice_bitcast_fusion.2 = (bf16[16,1,256,128]{3,2,0,1:T(8,128)(2,1)S(1)}, bf16[16,256,128]{2,1,0:T(8,128)(2,1)}, bf16[16,256,128]{2,1,0:T(8,128)(2,1)S(1)}) fusion(bf16[16,2,256,128]{3,2,1,0:T(8,128)(2,1)} %bitcast.18, s32[]{:T(128)S(6)} %select_n.14, s32[]{:T(128)S(6)} %select_n.13), kind=kLoop, calls=%fused_computation.2 | loop fusion | bytes 5242888
  3.1 2.0 %collective-permute-start.1 = (bf16[16,256,128]{2,1,0:T(8,128)(2,1)S(1)}, bf16[16,256,128]{2,1,0:T(8,128)(2,1)S(1)}, u32[]{:S(2)}, u32[]{:S(2)}) collective-permute-start(bf16[16,256,128]{2,1,0:T(8,128)(2,1)S(1)} %get-tuple-element.7), channel_id=1, source_target_pairs={{0,2},{1,3},{2,0},{3,1},{4,6},{5,7},{6,4},{7,5}} | collective-permute-start | bytes 3145736 | tf_op jit(solution)/shard_map/ppermute | solution.py:188
  5.1 1.0 collective-permute-start
  6.1 0.9 slice_bitcast_fusion
  7.0 0.0 collective-permute-start.8
  7.0 1.5 %collective-permute-start.7 = (bf16[4,256,128]{2,1,0:T(8,128)(2,1)}, bf16[4,256,128]{2,1,0:T(8,128)(2,1)}, u32[]{:S(2)}, u32[]{:S(2)}) collective-permute-start(bf16[4,256,128]{2,1,0:T(8,128)(2,1)} %get-tuple-element.13), channel_id=1, source_target_pairs={{0,2},{1,3},{2,0},{3,1},{4,6},{5,7},{6,4},{7,5}} | collective-permute-start | bytes 786440 | tf_op jit(solution)/shard_map/ppermute | solution.py:194
  8.5 0.0 collective-permute-start.6
  8.5 25.1 %collective-permute-done.8.refs_6_.refs_7_.refs_8_.refs_9_ = bf16[4,256,128]{2,1,0:T(8,128)(2,1)S(1)} collective-permute-done((bf16[4,256,128]{2,1,0:T(8,128)(2,1)S(1)}, bf16[4,256,128]{2,1,0:T(8,128)(2,1)S(1)}, u32[]{:S(2)}, u32[]{:S(2)}) %collective-permute-start.8) | collective-permute-done | bytes 262176 | tf_op jit(solution)/shard_map/ppermute | solution.py:194
  33.6 1.2 collective-permute-start.5
  34.8 0.0 collective-permute-done.1.refs_2_
  34.8 2.9 %collective-permute-start.2 = (bf16[16,256,128]{2,1,0:T(8,128)(2,1)S(1)}, bf16[16,256,128]{2,1,0:T(8,128)(2,1)}, u32[]{:S(2)}, u32[]{:S(2)}) collective-permute-start(bf16[16,256,128]{2,1,0:T(8,128)(2,1)S(1)} %collective-permute-done.1.refs_2_), channel_id=1, source_target_pairs={{0,1},{1,0},{2,3},{3,2},{4,5},{5,4},{6,7},{7,6}} | collective-permute-start | bytes 3145736 | tf_op jit(solution)/shard_map/ppermute | solution.py:195
  37.8 8.7 %shard_map.17.refs_4_ = bf16[16,2,256,4096]{3,2,1,0:T(8,128)(2,1)} custom-call(), custom_call_target="tpu_custom_call" | custom-call | flops 8999999488 | bytes 25165824 | tf_op jit(solution)/shard_map/pallas_call | solution.py:204
  46.5 0.0 collective-permute-done.7.refs_6_.refs_7_.refs_8_
  46.5 3.0 %collective-permute-start.4 = (bf16[16,256,128]{2,1,0:T(8,128)(2,1)}, bf16[16,256,128]{2,1,0:T(8,128)(2,1)S(1)}, u32[]{:S(2)}, u32[]{:S(2)}) collective-permute-start(bf16[16,256,128]{2,1,0:T(8,128)(2,1)} %get-tuple-element.6), channel_id=1, source_target_pairs={{1,4},{3,6},{4,1},{6,3}} | collective-permute-start | bytes 3145736 | tf_op jit(solution)/shard_map/ppermute | solution.py:190
  49.5 0.0 collective-permute-done.6.refs_6_.refs_7_
  49.5 1.3 %collective-permute-start.3 = (bf16[16,256,128]{2,1,0:T(8,128)(2,1)}, bf16[16,256,128]{2,1,0:T(8,128)(2,1)S(1)}, u32[]{:S(2)}, u32[]{:S(2)}) collective-permute-start(bf16[16,256,128]{2,1,0:T(8,128)(2,1)} %get-tuple-element.6), channel_id=1, source_target_pairs={{0,4},{2,6},{5,1},{7,3}} | collective-permute-start | bytes 3145736 | tf_op jit(solution)/shard_map/ppermute | solution.py:189
  50.8 0.1 fusion
  50.9 0.0 collective-permute-done.5.refs_6_
  51.0 1.7 %collective-permute-start.12 = (bf16[4,256,128]{2,1,0:T(8,128)(2,1)S(1)}, bf16[4,256,128]{2,1,0:T(8,128)(2,1)S(1)}, u32[]{:S(2)}, u32[]{:S(2)}) collective-permute-start(bf16[4,256,128]{2,1,0:T(8,128)(2,1)S(1)} %collective-permute-done.8.refs_6_.refs_7_.refs_8_.refs_9_), channel_id=1, source_target_pairs={{0,1},{1,0},{2,3},{3,2},{4,5},{5,4},{6,7},{7,6}} | collective-permute-start | bytes 786440 | tf_op jit(solution)/shard_map/ppermute | solution.py:201
  52.7 0.0 collective-permute-done
  52.7 2.7 %collective-permute-start.17 = (bf16[4,256,128]{2,1,0:T(8,128)(2,1)S(1)}, bf16[4,256,128]{2,1,0:T(8,128)(2,1)S(1)}, u32[]{:S(2)}, u32[]{:S(2)}) collective-permute-start(bf16[4,256,128]{2,1,0:T(8,128)(2,1)S(1)} %get-tuple-element.11), channel_id=1, source_target_pairs={{1,4},{3,6},{4,1},{6,3}} | collective-permute-start | bytes 786440 | tf_op jit(solution)/shard_map/ppermute | solution.py:199
  55.4 0.0 collective-permute-done.2.refs_3_
  55.4 1.3 %collective-permute-start.13 = (bf16[4,256,128]{2,1,0:T(8,128)(2,1)S(1)}, bf16[4,256,128]{2,1,0:T(8,128)(2,1)S(1)}, u32[]{:S(2)}, u32[]{:S(2)}) collective-permute-start(bf16[4,256,128]{2,1,0:T(8,128)(2,1)S(1)} %get-tuple-element.11), channel_id=1, source_target_pairs={{0,4},{2,6},{5,1},{7,3}} | collective-permute-start | bytes 786440 | tf_op jit(solution)/shard_map/ppermute | solution.py:198
  56.7 0.0 copy-done
  56.7 0.2 shard_map.18.refs_10_
  56.9 0.0 collective-permute-done.12.refs_7_.refs_9_.refs_11_.refs_13_
  56.9 16.1 %collective-permute-start.11 = (bf16[4,256,128]{2,1,0:T(8,128)(2,1)}, bf16[4,256,128]{2,1,0:T(8,128)(2,1)S(1)}, u32[]{:S(2)}, u32[]{:S(2)}) collective-permute-start(bf16[4,256,128]{2,1,0:T(8,128)(2,1)} %collective-permute-done.7.refs_6_.refs_7_.refs_8_), channel_id=1, source_target_pairs={{0,1},{1,0},{2,3},{3,2},{4,5},{5,4},{6,7},{7,6}} | collective-permute-start | bytes 786440 | tf_op jit(solution)/shard_map/ppermute | solution.py:201
  73.0 0.0 collective-permute-done.4.refs_5_
  73.0 0.0 copy-start.1
  73.0 0.0 collective-permute-start.10
  73.1 3.3 %collective-permute-done.3.refs_4_ = bf16[16,256,128]{2,1,0:T(8,128)(2,1)S(1)} collective-permute-done((bf16[16,256,128]{2,1,0:T(8,128)(2,1)}, bf16[16,256,128]{2,1,0:T(8,128)(2,1)S(1)}, u32[]{:S(2)}, u32[]{:S(2)}) %collective-permute-start.3) | collective-permute-done | bytes 1048608 | tf_op jit(solution)/shard_map/ppermute | solution.py:189
  76.3 0.0 copy-start.2
  76.3 0.0 collective-permute-start.9
  76.3 0.7 collective-permute-done.17.refs_9_.refs_12_.refs_15_.refs_18_
  77.0 2.7 %collective-permute-start.18 = (bf16[4,256,128]{2,1,0:T(8,128)(2,1)S(1)}, bf16[4,256,128]{2,1,0:T(8,128)(2,1)S(1)}, u32[]{:S(2)}, u32[]{:S(2)}) collective-permute-start(bf16[4,256,128]{2,1,0:T(8,128)(2,1)S(1)} %get-tuple-element.10), channel_id=1, source_target_pairs={{1,4},{3,6},{4,1},{6,3}} | collective-permute-start | bytes 786440 | tf_op jit(solution)/shard_map/ppermute | solution.py:199
  79.7 0.0 collective-permute-done.13.refs_8_.refs_10_.refs_12_.refs_14_
  79.7 1.3 %collective-permute-start.14 = (bf16[4,256,128]{2,1,0:T(8,128)(2,1)S(1)}, bf16[4,256,128]{2,1,0:T(8,128)(2,1)S(1)}, u32[]{:S(2)}, u32[]{:S(2)}) collective-permute-start(bf16[4,256,128]{2,1,0:T(8,128)(2,1)S(1)} %get-tuple-element.10), channel_id=1, source_target_pairs={{0,4},{2,6},{5,1},{7,3}} | collective-permute-start | bytes 786440 | tf_op jit(solution)/shard_map/ppermute | solution.py:198
  81.0 8.8 %shard_map.19.refs_14_ = bf16[16,2,256,4096]{3,2,1,0:T(8,128)(2,1)} custom-call(bf16[16,2,256,128]{3,2,1,0:T(8,128)(2,1)} %bitcast.19, bf16[16,2,256,128]{3,2,1,0:T(8,128)(2,1)} %bitcast.1.refs_1_, bf16[16,256,128]{2,1,0:T(8,128)(2,1)S(1)} %collective-permute-done.1.refs_2_, ...), custom_call_target="tpu_custom_call", output_to_operand_aliasing={{}: (10, {})} | custom-call | flops 4966055936 | bytes 9699328 | tf_op jit(solution)/shard_map/pallas_call | solution.py:163
  89.9 0.0 copy-done.1
  89.9 0.0 collective-permute-done.11.refs_8_.refs_10_.refs_12_
  89.9 2.8 %collective-permute-start.19 = (bf16[4,256,128]{2,1,0:T(8,128)(2,1)S(1)}, bf16[4,256,128]{2,1,0:T(8,128)(2,1)S(1)}, u32[]{:S(2)}, u32[]{:S(2)}) collective-permute-start(bf16[4,256,128]{2,1,0:T(8,128)(2,1)S(1)} %get-tuple-element.9), channel_id=1, source_target_pairs={{1,4},{3,6},{4,1},{6,3}} | collective-permute-start | bytes 786440 | tf_op jit(solution)/shard_map/ppermute | solution.py:199
  92.7 0.0 collective-permute-done.18.refs_13_.refs_16_.refs_19_
  92.7 1.3 %collective-permute-start.15 = (bf16[4,256,128]{2,1,0:T(8,128)(2,1)S(1)}, bf16[4,256,128]{2,1,0:T(8,128)(2,1)S(1)}, u32[]{:S(2)}, u32[]{:S(2)}) collective-permute-start(bf16[4,256,128]{2,1,0:T(8,128)(2,1)S(1)} %get-tuple-element.9), channel_id=1, source_target_pairs={{0,4},{2,6},{5,1},{7,3}} | collective-permute-start | bytes 786440 | tf_op jit(solution)/shard_map/ppermute | solution.py:198
  94.0 0.0 collective-permute-done.14.refs_11_.refs_13_.refs_15_
  94.0 2.7 %collective-permute-start.20 = (bf16[4,256,128]{2,1,0:T(8,128)(2,1)S(1)}, bf16[4,256,128]{2,1,0:T(8,128)(2,1)S(1)}, u32[]{:S(2)}, u32[]{:S(2)}) collective-permute-start(bf16[4,256,128]{2,1,0:T(8,128)(2,1)S(1)} %get-tuple-element.8), channel_id=1, source_target_pairs={{1,4},{3,6},{4,1},{6,3}} | collective-permute-start | bytes 786440 | tf_op jit(solution)/shard_map/ppermute | solution.py:199
  96.8 0.0 copy-done.2
  96.8 10.3 %shard_map.20.refs_18_ = bf16[16,2,256,4096]{3,2,1,0:T(8,128)(2,1)} custom-call(bf16[16,2,256,128]{3,2,1,0:T(8,128)(2,1)} %bitcast.20, bf16[16,2,256,128]{3,2,1,0:T(8,128)(2,1)} %bitcast.1.refs_1_, bf16[16,256,128]{2,1,0:T(8,128)(2,1)S(1)} %collective-permute-done.1.refs_2_, ...), custom_call_target="tpu_custom_call", output_to_operand_aliasing={{}: (14, {})} | custom-call | flops 6039797760 | bytes 11796480 | tf_op jit(solution)/shard_map/pallas_call | solution.py:163
  107.1 0.0 collective-permute-done.10.refs_9_.refs_11_
  107.1 1.3 %collective-permute-start.16 = (bf16[4,256,128]{2,1,0:T(8,128)(2,1)S(1)}, bf16[4,256,128]{2,1,0:T(8,128)(2,1)S(1)}, u32[]{:S(2)}, u32[]{:S(2)}) collective-permute-start(bf16[4,256,128]{2,1,0:T(8,128)(2,1)S(1)} %get-tuple-element.8), channel_id=1, source_target_pairs={{0,4},{2,6},{5,1},{7,3}} | collective-permute-start | bytes 786440 | tf_op jit(solution)/shard_map/ppermute | solution.py:198
  108.4 0.0 collective-permute-done.19.refs_17_.refs_20_
  108.4 0.0 collective-permute-done.15.refs_14_.refs_16_
  108.4 9.6 %shard_map.21.refs_22_ = bf16[16,2,256,4096]{3,2,1,0:T(8,128)(2,1)} custom-call(bf16[16,2,256,128]{3,2,1,0:T(8,128)(2,1)} %bitcast.21, bf16[16,2,256,128]{3,2,1,0:T(8,128)(2,1)} %bitcast.1.refs_1_, bf16[16,256,128]{2,1,0:T(8,128)(2,1)S(1)} %collective-permute-done.1.refs_2_, ...), custom_call_target="tpu_custom_call", output_to_operand_aliasing={{}: (18, {})} | custom-call | flops 5234491392 | bytes 10223616 | tf_op jit(solution)/shard_map/pallas_call | solution.py:163
  118.0 0.0 collective-permute-done.9.refs_10_
  118.0 0.0 collective-permute-done.20.refs_21_
  118.1 0.0 collective-permute-done.16.refs_17_
  118.1 5.6 %shard_map.22 = bf16[16,2,256,4096]{3,2,1,0:T(8,128)(2,1)} custom-call(bf16[16,2,256,128]{3,2,1,0:T(8,128)(2,1)} %bitcast.22, bf16[16,2,256,128]{3,2,1,0:T(8,128)(2,1)} %bitcast.1.refs_1_, bf16[16,256,128]{2,1,0:T(8,128)(2,1)S(1)} %collective-permute-done.1.refs_2_, ...), custom_call_target="tpu_custom_call", output_to_operand_aliasing={{}: (22, {})} | custom-call | flops 2013265920 | bytes 3932160 | tf_op jit(solution)/shard_map/pallas_call | solution.py:163
Async XLA Ops:
  0.0 56.7 %copy-start = (bf16[8192,128]{1,0:T(8,128)(2,1)S(1)}, bf16[8192,128]{1,0:T(8,128)(2,1)}, u32[]{:S(2)}) copy-start(bf16[8192,128]{1,0:T(8,128)(2,1)} %param.1) | copy-start | bytes 6291460
  3.1 31.7 %collective-permute-start.1 = (bf16[16,256,128]{2,1,0:T(8,128)(2,1)S(1)}, bf16[16,256,128]{2,1,0:T(8,128)(2,1)S(1)}, u32[]{:S(2)}, u32[]{:S(2)}) collective-permute-start(bf16[16,256,128]{2,1,0:T(8,128)(2,1)S(1)} %get-tuple-element.7), channel_id=1, source_target_pairs={{0,2},{1,3},{2,0},{3,1},{4,6},{5,7},{6,4},{7,5}} | collective-permute-start | bytes 3145736 | tf_op jit(solution)/shard_map/ppermute | solution.py:188
  5.1 47.5 %collective-permute-start = (bf16[8192,128]{1,0:T(8,128)(2,1)}, bf16[8192,128]{1,0:T(8,128)(2,1)}, u32[]{:S(2)}, u32[]{:S(2)}) collective-permute-start(bf16[8192,128]{1,0:T(8,128)(2,1)} %param.1), channel_id=1, source_target_pairs={{0,1},{1,0},{2,3},{3,2},{4,5},{5,4},{6,7},{7,6}} | collective-permute-start | bytes 6291464 | tf_op jit(solution)/shard_map/ppermute | solution.py:187
  7.0 26.6 %collective-permute-start.8 = (bf16[4,256,128]{2,1,0:T(8,128)(2,1)S(1)}, bf16[4,256,128]{2,1,0:T(8,128)(2,1)S(1)}, u32[]{:S(2)}, u32[]{:S(2)}) collective-permute-start(bf16[4,256,128]{2,1,0:T(8,128)(2,1)S(1)} %get-tuple-element.12), channel_id=1, source_target_pairs={{0,2},{1,3},{2,0},{3,1},{4,6},{5,7},{6,4},{7,5}} | collective-permute-start | bytes 786440 | tf_op jit(solution)/shard_map/ppermute | solution.py:194
  7.0 39.5 %collective-permute-start.7 = (bf16[4,256,128]{2,1,0:T(8,128)(2,1)}, bf16[4,256,128]{2,1,0:T(8,128)(2,1)}, u32[]{:S(2)}, u32[]{:S(2)}) collective-permute-start(bf16[4,256,128]{2,1,0:T(8,128)(2,1)} %get-tuple-element.13), channel_id=1, source_target_pairs={{0,2},{1,3},{2,0},{3,1},{4,6},{5,7},{6,4},{7,5}} | collective-permute-start | bytes 786440 | tf_op jit(solution)/shard_map/ppermute | solution.py:194
  8.5 41.1 %collective-permute-start.6 = (bf16[4,256,128]{2,1,0:T(8,128)(2,1)}, bf16[4,256,128]{2,1,0:T(8,128)(2,1)}, u32[]{:S(2)}, u32[]{:S(2)}) collective-permute-start(bf16[4,256,128]{2,1,0:T(8,128)(2,1)} %get-tuple-element.14), channel_id=1, source_target_pairs={{0,2},{1,3},{2,0},{3,1},{4,6},{5,7},{6,4},{7,5}} | collective-permute-start | bytes 786440 | tf_op jit(solution)/shard_map/ppermute | solution.py:194
  33.6 17.3 %collective-permute-start.5 = (bf16[4,256,128]{2,1,0:T(8,128)(2,1)}, bf16[4,256,128]{2,1,0:T(8,128)(2,1)}, u32[]{:S(2)}, u32[]{:S(2)}) collective-permute-start(bf16[4,256,128]{2,1,0:T(8,128)(2,1)} %get-tuple-element.15), channel_id=1, source_target_pairs={{0,2},{1,3},{2,0},{3,1},{4,6},{5,7},{6,4},{7,5}} | collective-permute-start | bytes 786440 | tf_op jit(solution)/shard_map/ppermute | solution.py:194
  34.8 20.6 %collective-permute-start.2 = (bf16[16,256,128]{2,1,0:T(8,128)(2,1)S(1)}, bf16[16,256,128]{2,1,0:T(8,128)(2,1)}, u32[]{:S(2)}, u32[]{:S(2)}) collective-permute-start(bf16[16,256,128]{2,1,0:T(8,128)(2,1)S(1)} %collective-permute-done.1.refs_2_), channel_id=1, source_target_pairs={{0,1},{1,0},{2,3},{3,2},{4,5},{5,4},{6,7},{7,6}} | collective-permute-start | bytes 3145736 | tf_op jit(solution)/shard_map/ppermute | solution.py:195
  46.5 26.5 %collective-permute-start.4 = (bf16[16,256,128]{2,1,0:T(8,128)(2,1)}, bf16[16,256,128]{2,1,0:T(8,128)(2,1)S(1)}, u32[]{:S(2)}, u32[]{:S(2)}) collective-permute-start(bf16[16,256,128]{2,1,0:T(8,128)(2,1)} %get-tuple-element.6), channel_id=1, source_target_pairs={{1,4},{3,6},{4,1},{6,3}} | collective-permute-start | bytes 3145736 | tf_op jit(solution)/shard_map/ppermute | solution.py:190
  49.5 26.8 %collective-permute-start.3 = (bf16[16,256,128]{2,1,0:T(8,128)(2,1)}, bf16[16,256,128]{2,1,0:T(8,128)(2,1)S(1)}, u32[]{:S(2)}, u32[]{:S(2)}) collective-permute-start(bf16[16,256,128]{2,1,0:T(8,128)(2,1)} %get-tuple-element.6), channel_id=1, source_target_pairs={{0,4},{2,6},{5,1},{7,3}} | collective-permute-start | bytes 3145736 | tf_op jit(solution)/shard_map/ppermute | solution.py:189
  51.0 6.0 %collective-permute-start.12 = (bf16[4,256,128]{2,1,0:T(8,128)(2,1)S(1)}, bf16[4,256,128]{2,1,0:T(8,128)(2,1)S(1)}, u32[]{:S(2)}, u32[]{:S(2)}) collective-permute-start(bf16[4,256,128]{2,1,0:T(8,128)(2,1)S(1)} %collective-permute-done.8.refs_6_.refs_7_.refs_8_.refs_9_), channel_id=1, source_target_pairs={{0,1},{1,0},{2,3},{3,2},{4,5},{5,4},{6,7},{7,6}} | collective-permute-start | bytes 786440 | tf_op jit(solution)/shard_map/ppermute | solution.py:201
  52.7 24.3 %collective-permute-start.17 = (bf16[4,256,128]{2,1,0:T(8,128)(2,1)S(1)}, bf16[4,256,128]{2,1,0:T(8,128)(2,1)S(1)}, u32[]{:S(2)}, u32[]{:S(2)}) collective-permute-start(bf16[4,256,128]{2,1,0:T(8,128)(2,1)S(1)} %get-tuple-element.11), channel_id=1, source_target_pairs={{1,4},{3,6},{4,1},{6,3}} | collective-permute-start | bytes 786440 | tf_op jit(solution)/shard_map/ppermute | solution.py:199
  55.4 24.3 %collective-permute-start.13 = (bf16[4,256,128]{2,1,0:T(8,128)(2,1)S(1)}, bf16[4,256,128]{2,1,0:T(8,128)(2,1)S(1)}, u32[]{:S(2)}, u32[]{:S(2)}) collective-permute-start(bf16[4,256,128]{2,1,0:T(8,128)(2,1)S(1)} %get-tuple-element.11), channel_id=1, source_target_pairs={{0,4},{2,6},{5,1},{7,3}} | collective-permute-start | bytes 786440 | tf_op jit(solution)/shard_map/ppermute | solution.py:198
  56.9 33.0 %collective-permute-start.11 = (bf16[4,256,128]{2,1,0:T(8,128)(2,1)}, bf16[4,256,128]{2,1,0:T(8,128)(2,1)S(1)}, u32[]{:S(2)}, u32[]{:S(2)}) collective-permute-start(bf16[4,256,128]{2,1,0:T(8,128)(2,1)} %collective-permute-done.7.refs_6_.refs_7_.refs_8_), channel_id=1, source_target_pairs={{0,1},{1,0},{2,3},{3,2},{4,5},{5,4},{6,7},{7,6}} | collective-permute-start | bytes 786440 | tf_op jit(solution)/shard_map/ppermute | solution.py:201
  73.0 16.9 %copy-start.1 = (bf16[16,256,128]{2,1,0:T(8,128)(2,1)}, bf16[16,256,128]{2,1,0:T(8,128)(2,1)S(1)}, u32[]{:S(2)}) copy-start(bf16[16,256,128]{2,1,0:T(8,128)(2,1)S(1)} %collective-permute-done.4.refs_5_) | copy-start | bytes 3145732
  73.0 34.1 %collective-permute-start.10 = (bf16[4,256,128]{2,1,0:T(8,128)(2,1)}, bf16[4,256,128]{2,1,0:T(8,128)(2,1)S(1)}, u32[]{:S(2)}, u32[]{:S(2)}) collective-permute-start(bf16[4,256,128]{2,1,0:T(8,128)(2,1)} %collective-permute-done.6.refs_6_.refs_7_), channel_id=1, source_target_pairs={{0,1},{1,0},{2,3},{3,2},{4,5},{5,4},{6,7},{7,6}} | collective-permute-start | bytes 786440 | tf_op jit(solution)/shard_map/ppermute | solution.py:201
  76.3 20.5 %copy-start.2 = (bf16[16,256,128]{2,1,0:T(8,128)(2,1)}, bf16[16,256,128]{2,1,0:T(8,128)(2,1)S(1)}, u32[]{:S(2)}) copy-start(bf16[16,256,128]{2,1,0:T(8,128)(2,1)S(1)} %collective-permute-done.3.refs_4_) | copy-start | bytes 3145732
  76.3 41.7 %collective-permute-start.9 = (bf16[4,256,128]{2,1,0:T(8,128)(2,1)}, bf16[4,256,128]{2,1,0:T(8,128)(2,1)S(1)}, u32[]{:S(2)}, u32[]{:S(2)}) collective-permute-start(bf16[4,256,128]{2,1,0:T(8,128)(2,1)} %collective-permute-done.5.refs_6_), channel_id=1, source_target_pairs={{0,1},{1,0},{2,3},{3,2},{4,5},{5,4},{6,7},{7,6}} | collective-permute-start | bytes 786440 | tf_op jit(solution)/shard_map/ppermute | solution.py:201
  77.0 15.8 %collective-permute-start.18 = (bf16[4,256,128]{2,1,0:T(8,128)(2,1)S(1)}, bf16[4,256,128]{2,1,0:T(8,128)(2,1)S(1)}, u32[]{:S(2)}, u32[]{:S(2)}) collective-permute-start(bf16[4,256,128]{2,1,0:T(8,128)(2,1)S(1)} %get-tuple-element.10), channel_id=1, source_target_pairs={{1,4},{3,6},{4,1},{6,3}} | collective-permute-start | bytes 786440 | tf_op jit(solution)/shard_map/ppermute | solution.py:199
  79.7 14.3 %collective-permute-start.14 = (bf16[4,256,128]{2,1,0:T(8,128)(2,1)S(1)}, bf16[4,256,128]{2,1,0:T(8,128)(2,1)S(1)}, u32[]{:S(2)}, u32[]{:S(2)}) collective-permute-start(bf16[4,256,128]{2,1,0:T(8,128)(2,1)S(1)} %get-tuple-element.10), channel_id=1, source_target_pairs={{0,4},{2,6},{5,1},{7,3}} | collective-permute-start | bytes 786440 | tf_op jit(solution)/shard_map/ppermute | solution.py:198
  89.9 18.5 %collective-permute-start.19 = (bf16[4,256,128]{2,1,0:T(8,128)(2,1)S(1)}, bf16[4,256,128]{2,1,0:T(8,128)(2,1)S(1)}, u32[]{:S(2)}, u32[]{:S(2)}) collective-permute-start(bf16[4,256,128]{2,1,0:T(8,128)(2,1)S(1)} %get-tuple-element.9), channel_id=1, source_target_pairs={{1,4},{3,6},{4,1},{6,3}} | collective-permute-start | bytes 786440 | tf_op jit(solution)/shard_map/ppermute | solution.py:199
  92.7 15.7 %collective-permute-start.15 = (bf16[4,256,128]{2,1,0:T(8,128)(2,1)S(1)}, bf16[4,256,128]{2,1,0:T(8,128)(2,1)S(1)}, u32[]{:S(2)}, u32[]{:S(2)}) collective-permute-start(bf16[4,256,128]{2,1,0:T(8,128)(2,1)S(1)} %get-tuple-element.9), channel_id=1, source_target_pairs={{0,4},{2,6},{5,1},{7,3}} | collective-permute-start | bytes 786440 | tf_op jit(solution)/shard_map/ppermute | solution.py:198
  94.0 24.0 %collective-permute-start.20 = (bf16[4,256,128]{2,1,0:T(8,128)(2,1)S(1)}, bf16[4,256,128]{2,1,0:T(8,128)(2,1)S(1)}, u32[]{:S(2)}, u32[]{:S(2)}) collective-permute-start(bf16[4,256,128]{2,1,0:T(8,128)(2,1)S(1)} %get-tuple-element.8), channel_id=1, source_target_pairs={{1,4},{3,6},{4,1},{6,3}} | collective-permute-start | bytes 786440 | tf_op jit(solution)/shard_map/ppermute | solution.py:199
  107.1 11.0 %collective-permute-start.16 = (bf16[4,256,128]{2,1,0:T(8,128)(2,1)S(1)}, bf16[4,256,128]{2,1,0:T(8,128)(2,1)S(1)}, u32[]{:S(2)}, u32[]{:S(2)}) collective-permute-start(bf16[4,256,128]{2,1,0:T(8,128)(2,1)S(1)} %get-tuple-element.8), channel_id=1, source_target_pairs={{0,4},{2,6},{5,1},{7,3}} | collective-permute-start | bytes 786440 | tf_op jit(solution)/shard_map/ppermute | solution.py:198

commit v2 on v0

v2 whole, which is shorter than its diff:
```python
import functools
import jax
import jax.numpy as jnp
from jax import lax
from jax.experimental import pallas as pl
from jax.experimental.pallas import tpu as pltpu
from jax.sharding import PartitionSpec as P

BLOCK = 256
K_DIM = 512
PIECE = 128
PIECES = K_DIM // PIECE
NM = 16
CH = 4
NC = NM // CH
NBUF = 3
TILE = CH * BLOCK
JOBS = [(i, j) for j in range(NC) for i in range(j, NC)]


def positions():
    y = lax.axis_index('row')
    col = lax.axis_index('col')
    return y, col // 2, col % 2, col


def chunk(c):
    return pl.ds(c * CH, CH)


def panel(ref, lead, first, count):
    parts = [ref[(*lead, p, pl.ds(first, count))].reshape(count * BLOCK, PIECE) for p in range(PIECES)]
    return jnp.concatenate(parts, axis=1)


def dot_t(rows, cols):
    return lax.dot_general(rows, cols, (((1,), (1,)), ((), ())), preferred_element_type=jnp.float32)


def full_tile(out, row_ref, row_lead, i, col_ref, col_lead, j):
    prod = dot_t(panel(row_ref, row_lead, i * CH, CH), panel(col_ref, col_lead, j * CH, CH))
    out[...] = prod.astype(jnp.bfloat16).reshape(CH, BLOCK, TILE)


def diag_tile(out, row_ref, row_lead, col_ref, col_lead, j, row_blk, col_blk):
    for q in range(CH):
        prod = dot_t(panel(row_ref, row_lead, j * CH + q, CH - q), panel(col_ref, col_lead, j * CH + q, 1))
        row_id = lax.broadcasted_iota(jnp.int32, (BLOCK, BLOCK), 0) + row_blk * BLOCK
        col_id = lax.broadcasted_iota(jnp.int32, (BLOCK, BLOCK), 1) + col_blk * BLOCK
        lanes = slice(q * BLOCK, (q + 1) * BLOCK)
        out[q, :, lanes] = jnp.where(row_id >= col_id, prod[:BLOCK], 0.0).astype(jnp.bfloat16)
        if q + 1 < CH:
            out[q + 1:, :, lanes] = prod[BLOCK:].astype(jnp.bfloat16).reshape(CH - q - 1, BLOCK, BLOCK)
        if q:
            out[:q, :, lanes] = jnp.zeros((q, BLOCK, BLOCK), jnp.bfloat16)


def gather_kernel(a_ref, sc_ref, o_ref, t_ref, lsem, d_send, d_recv, x_send, x_recv, r_send, r_recv, y_send, y_recv):
    y, x, k, col = positions()
    other_parity = k != y
    side = jnp.where(other_parity, 1, 0)
    slot = jnp.where(k == y, 0, 1)
    partner = (0, y, 2 * x + 1 - k)
    x_peer = (0, y, 2 * (1 - x) + k)
    y_peer = (0, 1 - y, 2 * x + y)

    barrier = pltpu.get_barrier_semaphore()
    for dev in (partner, x_peer, (0, 1 - y, 2 * x), (0, 1 - y, 2 * x + 1)):
        pl.semaphore_signal(barrier, inc=1, device_id=dev, device_id_type=pl.DeviceIdType.MESH)
    pl.semaphore_wait(barrier, 4)

    def remote(src, dst, send, recv, dev):
        return pltpu.make_async_remote_copy(src, dst, send, recv, device_id=dev, device_id_type=pl.DeviceIdType.MESH)

    def x_copy(n):
        c = n % NC
        if n < NC:
            return remote(a_ref.at[chunk(c), 1 - x], sc_ref.at[0, 2, chunk(c)], x_send.at[n], x_recv.at[n], x_peer)
        return remote(a_ref.at[chunk(c), x], o_ref.at[2, chunk(c)], x_send.at[n], x_recv.at[n], x_peer)

    def relay_copy(n):
        c = n % NC
        if n < NC:
            return remote(sc_ref.at[0, 2, chunk(c)], sc_ref.at[0, 3, chunk(c)], r_send.at[n], r_recv.at[n], partner)
        return remote(o_ref.at[2, chunk(c)], o_ref.at[3, chunk(c)], r_send.at[n], r_recv.at[n], partner)

    def y0_copy(s):
        return remote(a_ref.at[:, x], sc_ref.at[1, s], y_send.at[0], y_recv.at[s, 0], y_peer)

    def y2_copy(s, c):
        return remote(sc_ref.at[0, 2, chunk(c)], sc_ref.at[1, 2 + s, chunk(c)], y_send.at[1 + c], y_recv.at[s, 1 + c], y_peer)

    d_copies = [remote(a_ref.at[:, x], sc_ref.at[0, 1], d_send.at[0], d_recv.at[0], partner),
                remote(a_ref.at[:, 1 - x], o_ref.at[1], d_send.at[1], d_recv.at[1], partner)]
    l_copies = [pltpu.make_async_copy(a_ref.at[:, x], sc_ref.at[0, 0], lsem.at[0]),
                pltpu.make_async_copy(a_ref.at[:, 1 - x], o_ref.at[0], lsem.at[1])]

    for n in range(2 * NC):
        x_copy(n).start()
    y0_copy(slot).start()
    for cp in d_copies + l_copies:
        cp.start()

    for c in range(NC):
        x_copy(c).wait_recv()
        relay_copy(c).start()
        y2_copy(slot, c).start()
    l_copies[0].wait()
    d_copies[0].wait_recv()
    for c in range(NC):
        relay_copy(c).wait_recv()

    row_blk = 2 * x + y
    for c in range(NC):
        x_copy(NC + c).wait_recv()
        relay_copy(NC + c).start()

        @pl.when(other_parity)
        def _():
            for s in range(2):
                if c == 0:
                    y0_copy(s).wait_recv()
                y2_copy(s, c).wait_recv()

        base = JOBS.index((c, c))
        diag_tile(t_ref.at[base], sc_ref, (0,), sc_ref, (side,), c, row_blk, col)

        def body(i, _):
            full_tile(t_ref.at[base + i - c], sc_ref, (0,), i, sc_ref, (side,), c)
            return 0
        if c + 1 < NC:
            lax.fori_loop(c + 1, NC, body, 0)

    l_copies[1].wait()
    d_copies[1].wait_recv()
    for c in range(NC):
        relay_copy(NC + c).wait_recv()
    for n in range(2 * NC):
        x_copy(n).wait_send()
        relay_copy(n).wait_send()
    for cp in d_copies:
        cp.wait_send()
    y0_copy(slot).wait_send()
    for c in range(NC):
        y2_copy(slot, c).wait_send()


def lookup(n, values):
    out = jnp.int32(values[-1])
    for m in range(len(values) - 2, -1, -1):
        out = jnp.where(n == m, jnp.int32(values[m]), out)
    return out


def write_kernel(sc_ref, o_ref, t_ref, c_ref, zbuf, obuf, tsem, zsem, osem):
    y, x, k, col = positions()
    side = jnp.where(k != y, 1, 0)

    def dest(i, j, s):
        return c_ref.at[pl.ds(i * CH, CH), s, :, pl.ds(pl.multiple_of(j * TILE, TILE), TILE)]

    t_copies = [pltpu.make_async_copy(t_ref.at[n], dest(i, j, x), tsem) for n, (i, j) in enumerate(JOBS)]
    for cp in t_copies:
        cp.start()
    zbuf[...] = jnp.zeros_like(zbuf)
    z_copies = [pltpu.make_async_copy(zbuf, dest(i, j, s), zsem) for i in range(NC) for j in range(i + 1, NC) for s in range(2)]
    for cp in z_copies:
        cp.start()

    def out_copy(b, i, j):
        return pltpu.make_async_copy(obuf.at[b], dest(i, j, 1 - x), osem.at[b])

    def body(n, _):
        i = lookup(n, [v[0] for v in JOBS])
        j = lookup(n, [v[1] for v in JOBS])
        b = lax.rem(n, NBUF)

        @pl.when(n >= NBUF)
        def _():
            out_copy(b, i, j).wait()

        @pl.when(i != j)
        def _():
            full_tile(obuf.at[b], o_ref, (), i, sc_ref, (side,), j)

        @pl.when(i == j)
        def _():
            diag_tile(obuf.at[b], o_ref, (), sc_ref, (side,), j, 2 * (1 - x) + y, col)
        out_copy(b, i, j).start()
        return 0

    lax.fori_loop(0, len(JOBS), body, 0)
    for b in range(NBUF):
        out_copy(b, 0, 0).wait()
    for cp in t_copies + z_copies:
        cp.wait()


def solution(mesh):
    def local_fn(a):
        a4 = pltpu.with_memory_space_constraint(a.reshape(NM, 2, BLOCK, PIECE), pltpu.HBM)
        any_spec = pl.BlockSpec(memory_space=pl.ANY)
        vmem = pl.BlockSpec(memory_space=pltpu.VMEM)
        dma = pltpu.SemaphoreType.DMA
        half_flops = 136 * 2 * BLOCK * BLOCK * K_DIM
        sc, o, t = pl.pallas_call(
            gather_kernel,
            out_shape=[pltpu.VMEM((2, PIECES, NM, BLOCK, PIECE), jnp.bfloat16),
                       pltpu.VMEM((PIECES, NM, BLOCK, PIECE), jnp.bfloat16),
                       pltpu.VMEM((len(JOBS), CH, BLOCK, TILE), jnp.bfloat16)],
            in_specs=[pl.BlockSpec(memory_space=pltpu.HBM)],
            out_specs=[vmem] * 3,
            scratch_shapes=[dma((2,)), dma((2,)), dma((2,)), dma((2 * NC,)), dma((2 * NC,)), dma((2 * NC,)), dma((2 * NC,)),
                            dma((1 + NC,)), dma((2, 1 + NC))],
            compiler_params=pltpu.CompilerParams(collective_id=0, has_side_effects=True, vmem_limit_bytes=8 * 1024 * 1024),
            cost_estimate=pl.CostEstimate(flops=half_flops, bytes_accessed=2 << 20, transcendentals=0),
        )(a4)
        c = pl.pallas_call(
            write_kernel,
            out_shape=jax.ShapeDtypeStruct((NM, 2, BLOCK, NM * BLOCK), jnp.bfloat16),
            in_specs=[vmem] * 3,
            out_specs=any_spec,
            scratch_shapes=[pltpu.VMEM((CH, BLOCK, TILE), jnp.bfloat16),
                            pltpu.VMEM((NBUF, CH, BLOCK, TILE), jnp.bfloat16),
                            dma(()), dma(()), dma((NBUF,))],
            compiler_params=pltpu.CompilerParams(vmem_limit_bytes=20 * 1024 * 1024),
            cost_estimate=pl.CostEstimate(flops=half_flops, bytes_accessed=64 << 20, transcendentals=0),
        )(sc, o, t)
        return c.reshape(2 * NM * BLOCK, NM * BLOCK)

    spec = P(('batch', 'row'), 'col')
    return jax.shard_map(local_fn, mesh=mesh, in_specs=(spec,), out_specs=spec, check_vma=False)
```

time: 307 us -> 77.3 us (0.25)
  waiting for transfers between devices: 150 us -> 0 us
  local copies, waits for them, and re-layouts: 99.4 us -> 0 us
  Pallas kernels: 0 us -> 77.2 us
  matrix products: 37.4 us -> 0 us
  between operations: 13.6 us -> 0.01 us
  starting transfers between devices: 4.94 us -> 0 us
    all_to_all x1 -> x0, waiting for transfers between devices: 90.8 us -> none  [local_fn(): swapped = lax.all_to_all(grouped, 'col', 1, 3, tiled=True)]
    pallas_call x0 -> x2, Pallas kernels: none -> 77.2 us  [the longest x1 52.4 us: local_fn(): pl.pallas_call(gather_kernel, out_shape=[pltpu.VMEM((2, PIECES, NM, BLOCK...]
    all_gather x2 -> x0, waiting for transfers between devices: 57.9 us -> none  [the longest x1 57.9 us: local_fn(): lax.all_gather(a_local.reshape(local_rows // BLOCK, BLOCK, m_local), 'row...]
    slice x26 -> x0, local copies, waits for them, and re-layouts: 47.8 us -> none  [the longest x14 47.8 us: lower_part(): col_panel[:col_width]]
    unnamed x29 -> x0, local copies, waits for them, and re-layouts: 39.1 us -> none
    dot_general x8 -> x0, matrix products: 37.4 us -> none  [lower_part(): lax.dot_general(row_panel[first_blk * BLOCK:last_blk * BLOCK], col_panel[...]
    all_to_all x1 -> x0, local copies, waits for them, and re-layouts: 7.83 us -> none  [local_fn(): swapped = lax.all_to_all(grouped, 'col', 1, 3, tiled=True)]
    all_to_all x1 -> x0, starting transfers between devices: 4.9 us -> none  [local_fn(): swapped = lax.all_to_all(grouped, 'col', 1, 3, tiled=True)]
  transfers between devices with their start and end apart: 3 -> 0, of which waited for: 2 -> 0; matrix products, arithmetic and copies ran while one was open for 22% -> 0% of each run, Pallas kernels for 0% -> 0%
where the time goes in v2:
time: 77.3 us; the launch traced here: 77.2 us
  Pallas kernels  77.2 us (100%)
    pallas_call x1, Pallas kernels, local_fn(): pl.pallas_call(gather_kernel, out_shape=[pltpu.VMEM((2, PIECES, NM, BLOCK...  52.4 us
    pallas_call x1, Pallas kernels, local_fn(): pl.pallas_call(write_kernel, out_shape=jax.ShapeDtypeStruct((NM, 2, BLOCK...  24.8 us

profile of v2, /device:TPU:0, one launch (start us, length us, event | category | flops | bytes accessed | tf_op | source)
XLA Modules:
  0.0 77.2 jit_solution(885221119857356775)
XLA Ops:
  0.0 52.4 %shard_map.17 = (bf16[2,4,16,256,128]{4,3,2,1,0:T(8,128)(2,1)S(1)}, bf16[4,16,256,128]{3,2,1,0:T(8,128)(2,1)S(1)}, bf16[10,4,256,1024]{3,2,1,0:T(8,128)(2,1)S(1)}) custom-call(bf16[16,2,256,128]{3,2,1,0:T(8,128)(2,1)} %bitcast.2), custom_call_target="tpu_custom_call" | custom-call | flops 9126805504 | bytes 2097152 | tf_op jit(solution)/shard_map/pallas_call | solution.py:206
  52.4 24.8 %shard_map.18 = bf16[16,2,256,4096]{3,2,1,0:T(8,128)(2,1)} custom-call(bf16[2,4,16,256,128]{4,3,2,1,0:T(8,128)(2,1)S(1)} %get-tuple-element.8.sc_ref, bf16[4,16,256,128]{3,2,1,0:T(8,128)(2,1)S(1)} %get-tuple-element.9.o_ref, bf16[10,4,256,1024]{3,2,1,0:T(8,128)(2,1)S(1)} %get-tuple-element.10.t_ref), custom_call_target="tpu_custom_call" | custom-call | flops 9126805504 | bytes 67108864 | tf_op jit(solution)/shard_map/pallas_call | solution.py:218

commit v3 on v2

--- a/solution.py
+++ b/solution.py
@@ -13,7 +13,8 @@
 NM = 16
 CH = 4
 NC = NM // CH
-NBUF = 3
+NBUF = 5
+LEAD = 3
 TILE = CH * BLOCK
 JOBS = [(i, j) for j in range(NC) for i in range(j, NC)]
 
@@ -160,12 +161,10 @@
         return c_ref.at[pl.ds(i * CH, CH), s, :, pl.ds(pl.multiple_of(j * TILE, TILE), TILE)]
 
     t_copies = [pltpu.make_async_copy(t_ref.at[n], dest(i, j, x), tsem) for n, (i, j) in enumerate(JOBS)]
-    for cp in t_copies:
+    for cp in t_copies[:LEAD]:
         cp.start()
     zbuf[...] = jnp.zeros_like(zbuf)
     z_copies = [pltpu.make_async_copy(zbuf, dest(i, j, s), zsem) for i in range(NC) for j in range(i + 1, NC) for s in range(2)]
-    for cp in z_copies:
-        cp.start()
 
     def out_copy(b, i, j):
         return pltpu.make_async_copy(obuf.at[b], dest(i, j, 1 - x), osem.at[b])
@@ -187,9 +186,18 @@
         def _():
             diag_tile(obuf.at[b], o_ref, (), sc_ref, (side,), j, 2 * (1 - x) + y, col)
         out_copy(b, i, j).start()
+
+        @pl.when(n + LEAD < len(JOBS))
+        def _():
+            m = jnp.minimum(n + LEAD, len(JOBS) - 1)
+            ti = lookup(m, [v[0] for v in JOBS])
+            tj = lookup(m, [v[1] for v in JOBS])
+            pltpu.make_async_copy(t_ref.at[m], dest(ti, tj, x), tsem).start()
         return 0
 
     lax.fori_loop(0, len(JOBS), body, 0)
+    for cp in z_copies:
+        cp.start()
     for b in range(NBUF):
         out_copy(b, 0, 0).wait()
     for cp in t_copies + z_copies:

time: 77.3 us -> 73.6 us (0.952)
  Pallas kernels: 77.2 us -> 73.5 us
    pallas_call x1, Pallas kernels: 24.8 us -> 21.1 us  [local_fn(): pl.pallas_call(write_kernel, out_shape=jax.ShapeDtypeStruct((NM, 2, BLOCK...]
where the time goes in v3:
time: 73.6 us; the launch traced here: 73.5 us
  Pallas kernels  73.5 us (100%)
    pallas_call x1, Pallas kernels, local_fn(): pl.pallas_call(gather_kernel, out_shape=[pltpu.VMEM((2, PIECES, NM, BLOCK...  52.4 us
    pallas_call x1, Pallas kernels, local_fn(): pl.pallas_call(write_kernel, out_shape=jax.ShapeDtypeStruct((NM, 2, BLOCK...  21.1 us

profile of v3, /device:TPU:0, one launch (start us, length us, event | category | flops | bytes accessed | tf_op | source)
XLA Modules:
  0.0 73.5 jit_solution(15472581295523958740)
XLA Ops:
  0.0 52.4 %shard_map.17 = (bf16[2,4,16,256,128]{4,3,2,1,0:T(8,128)(2,1)S(1)}, bf16[4,16,256,128]{3,2,1,0:T(8,128)(2,1)S(1)}, bf16[10,4,256,1024]{3,2,1,0:T(8,128)(2,1)S(1)}) custom-call(bf16[16,2,256,128]{3,2,1,0:T(8,128)(2,1)} %bitcast.2), custom_call_target="tpu_custom_call" | custom-call | flops 9126805504 | bytes 2097152 | tf_op jit(solution)/shard_map/pallas_call | solution.py:214
  52.4 21.1 %shard_map.18 = bf16[16,2,256,4096]{3,2,1,0:T(8,128)(2,1)} custom-call(bf16[2,4,16,256,128]{4,3,2,1,0:T(8,128)(2,1)S(1)} %get-tuple-element.8.sc_ref, bf16[4,16,256,128]{3,2,1,0:T(8,128)(2,1)S(1)} %get-tuple-element.9.o_ref, bf16[10,4,256,1024]{3,2,1,0:T(8,128)(2,1)S(1)} %get-tuple-element.10.t_ref), custom_call_target="tpu_custom_call" | custom-call | flops 9126805504 | bytes 67108864 | tf_op jit(solution)/shard_map/pallas_call | solution.py:226

commit v4 on v3

v4 whole, which is shorter than its diff:
```python
import functools
import jax
import jax.numpy as jnp
from jax import lax
from jax.experimental import pallas as pl
from jax.experimental.pallas import tpu as pltpu
from jax.sharding import PartitionSpec as P

BLOCK = 256
K_DIM = 512
PIECE = 128
PIECES = K_DIM // PIECE
NM = 16
CH = 4
NC = NM // CH
NBUF = 5
LEAD = 3
TILE = CH * BLOCK
JOBS = [(i, j) for j in range(NC) for i in range(j, NC)]


def positions():
    y = lax.axis_index('row')
    col = lax.axis_index('col')
    return y, col // 2, col % 2, col


def chunk(c):
    return pl.ds(c * CH, CH)


def panel(ref, lead, first, count):
    parts = [ref[(*lead, p, pl.ds(first, count))].reshape(count * BLOCK, PIECE) for p in range(PIECES)]
    return jnp.concatenate(parts, axis=1)


def dot_t(rows, cols):
    return lax.dot_general(rows, cols, (((1,), (1,)), ((), ())), preferred_element_type=jnp.float32)


def full_tile(out, row_ref, row_lead, i, col_ref, col_lead, j):
    prod = dot_t(panel(row_ref, row_lead, i * CH, CH), panel(col_ref, col_lead, j * CH, CH))
    out[...] = prod.astype(jnp.bfloat16).reshape(CH, BLOCK, TILE)


def diag_tile(out, row_ref, row_lead, col_ref, col_lead, j, row_blk, col_blk):
    for q in range(CH):
        prod = dot_t(panel(row_ref, row_lead, j * CH + q, CH - q), panel(col_ref, col_lead, j * CH + q, 1))
        row_id = lax.broadcasted_iota(jnp.int32, (BLOCK, BLOCK), 0) + row_blk * BLOCK
        col_id = lax.broadcasted_iota(jnp.int32, (BLOCK, BLOCK), 1) + col_blk * BLOCK
        lanes = slice(q * BLOCK, (q + 1) * BLOCK)
        out[q, :, lanes] = jnp.where(row_id >= col_id, prod[:BLOCK], 0.0).astype(jnp.bfloat16)
        if q + 1 < CH:
            out[q + 1:, :, lanes] = prod[BLOCK:].astype(jnp.bfloat16).reshape(CH - q - 1, BLOCK, BLOCK)


MESH_ID = pl.DeviceIdType.MESH


def remote(src, dst, send, recv, dev):
    return pltpu.make_async_remote_copy(src, dst, send, recv, device_id=dev, device_id_type=MESH_ID)


def signal(sem, devices):
    for dev in devices:
        pl.semaphore_signal(sem, inc=1, device_id=dev, device_id_type=MESH_ID)


def first_kernel(a_ref, sc_ref, token_ref, x_send, x_recv, y_send, y_recv):
    y, x, k, _ = positions()
    token_ref[...] = jnp.zeros_like(token_ref)

    @pl.when(k != y)
    def _():
        x_peer = (0, y, 2 * (1 - x) + k)
        y_peer = (0, 1 - y, 2 * x + y)
        barrier = pltpu.get_barrier_semaphore()
        signal(barrier, (x_peer, y_peer))
        pl.semaphore_wait(barrier, 2)
        xc = remote(a_ref.at[:, 1 - x], sc_ref.at[0, 2], x_send, x_recv, x_peer)
        yc = remote(a_ref.at[:, x], sc_ref.at[1, 1], y_send, y_recv, y_peer)
        xc.start()
        yc.start()
        xc.wait()
        yc.wait()


def zero_kernel(token_ref, c_ref, done_ref, zbuf, sem):
    zbuf[...] = jnp.zeros_like(zbuf)
    done_ref[...] = jnp.zeros_like(done_ref)
    copies = []
    for s in range(2):
        for i in range(NC):
            for j in range(i + 1, NC):
                copies.append(pltpu.make_async_copy(zbuf, c_ref.at[chunk(i), s, :, pl.ds(j * TILE, TILE)], sem))
            for q in range(1, CH):
                copies.append(pltpu.make_async_copy(
                    zbuf.at[pl.ds(0, q), :, pl.ds(0, BLOCK)],
                    c_ref.at[pl.ds(i * CH, q), s, :, pl.ds((i * CH + q) * BLOCK, BLOCK)], sem))
    for cp in copies:
        cp.start()
    for cp in copies:
        cp.wait()


def gather_kernel(a_ref, sc_in, token_ref, sc_ref, o_ref, t_ref, yb, join, lsem, d_send, d_recv, x_send, x_recv, r_send, r_recv,
                  y_send, y_recv, b_send, b_recv):
    y, x, k, col = positions()
    late = k != y
    side = jnp.where(late, 1, 0)
    partner = (0, y, 2 * x + 1 - k)
    x_peer = (0, y, 2 * (1 - x) + k)
    y_early = (0, 1 - y, 2 * x + 1 - y)
    y_late = (0, 1 - y, 2 * x + y)

    def x_copy(n):
        c = n % NC
        if n < NC:
            return remote(a_ref.at[chunk(c), 1 - x], sc_ref.at[0, 2, chunk(c)], x_send.at[n], x_recv.at[n], x_peer)
        return remote(a_ref.at[chunk(c), x], o_ref.at[2, chunk(c)], x_send.at[n], x_recv.at[n], x_peer)

    def relay_copy(n):
        c = n % NC
        if n < NC:
            return remote(sc_ref.at[0, 2, chunk(c)], sc_ref.at[0, 3, chunk(c)], r_send.at[n], r_recv.at[n], partner)
        return remote(o_ref.at[2, chunk(c)], o_ref.at[3, chunk(c)], r_send.at[n], r_recv.at[n], partner)

    def y_copy(s, c):
        return remote(sc_ref.at[0, 2, chunk(c)], sc_ref.at[1, 2 + s, chunk(c)], y_send.at[c], y_recv.at[s, c], y_late)

    yb_copy = remote(a_ref.at[:, x], yb, b_send.at[0], b_recv.at[0], y_early)
    yb_relay = remote(yb, sc_ref.at[1, 0], b_send.at[1], b_recv.at[1], partner)
    d_copies = [remote(a_ref.at[:, x], sc_ref.at[0, 1], d_send.at[0], d_recv.at[0], partner),
                remote(a_ref.at[:, 1 - x], o_ref.at[1], d_send.at[1], d_recv.at[1], partner)]
    l_copies = [pltpu.make_async_copy(a_ref.at[:, x], sc_ref.at[0, 0], lsem.at[0]),
                pltpu.make_async_copy(a_ref.at[:, 1 - x], o_ref.at[0], lsem.at[1])]
    for cp in l_copies:
        cp.start()
    barrier = pltpu.get_barrier_semaphore()

    @pl.when(jnp.logical_not(late))
    def _():
        signal(barrier, (x_peer, y_early, partner, y_late))
        pl.semaphore_wait(barrier, 2)
        for n in range(2 * NC):
            x_copy(n).start()
        yb_copy.start()
        pl.semaphore_wait(join, 2)
        d_copies[0].start()
        for c in range(NC):
            x_copy(c).wait_recv()
            y_copy(0, c).start()
            relay_copy(c).start()
        yb_copy.wait_recv()
        yb_relay.start()
        d_copies[1].start()

    @pl.when(late)
    def _():
        signal(barrier, (x_peer, y_late))
        pl.semaphore_wait(barrier, 4)
        signal(join, (partner, y_early))
        for n in range(NC, 2 * NC):
            x_copy(n).start()
        for c in range(NC):
            y_copy(1, c).start()
        for c in range(NC):
            relay_copy(c).start()
        for cp in d_copies:
            cp.start()

    l_copies[0].wait()
    d_copies[0].wait_recv()
    for c in range(NC):
        relay_copy(c).wait_recv()

    row_blk = 2 * x + y
    for c in range(NC):
        x_copy(NC + c).wait_recv()
        relay_copy(NC + c).start()

        @pl.when(late)
        def _():
            if c == 0:
                yb_relay.wait_recv()
            for s in range(2):
                y_copy(s, c).wait_recv()

        base = JOBS.index((c, c))
        diag_tile(t_ref.at[base], sc_ref, (0,), sc_ref, (side,), c, row_blk, col)

        def body(i, _):
            full_tile(t_ref.at[base + i - c], sc_ref, (0,), i, sc_ref, (side,), c)
            return 0
        if c + 1 < NC:
            lax.fori_loop(c + 1, NC, body, 0)

    l_copies[1].wait()
    d_copies[1].wait_recv()
    for c in range(NC):
        relay_copy(NC + c).wait_recv()
    for n in range(2 * NC):
        relay_copy(n).wait_send()
    for n in range(NC, 2 * NC):
        x_copy(n).wait_send()
    for cp in d_copies:
        cp.wait_send()
    for c in range(NC):
        y_copy(0, c).wait_send()

    @pl.when(jnp.logical_not(late))
    def _():
        for n in range(NC):
            x_copy(n).wait_send()
        yb_copy.wait_send()
        yb_relay.wait_send()


def lookup(n, values):
    out = jnp.int32(values[-1])
    for m in range(len(values) - 2, -1, -1):
        out = jnp.where(n == m, jnp.int32(values[m]), out)
    return out


def write_kernel(sc_ref, o_ref, t_ref, c_in, c_ref, obuf, tsem, osem):
    y, x, k, col = positions()
    side = jnp.where(k != y, 1, 0)

    def job(n):
        return lookup(n, [v[0] for v in JOBS]), lookup(n, [v[1] for v in JOBS])

    def put(src, i, j, s, sem, act):
        @pl.when(i != j)
        def _():
            act(pltpu.make_async_copy(src, c_ref.at[pl.ds(i * CH, CH), s, :, pl.ds(pl.multiple_of(j * TILE, TILE), TILE)], sem))

        @pl.when(i == j)
        def _():
            for q in range(CH):
                act(pltpu.make_async_copy(
                    src.at[pl.ds(q, CH - q), :, pl.ds(q * BLOCK, BLOCK)],
                    c_ref.at[pl.ds(i * CH + q, CH - q), s, :, pl.ds(pl.multiple_of(j * TILE + q * BLOCK, BLOCK), BLOCK)], sem))

    def put_panel(n, act):
        i, j = job(n)
        put(t_ref.at[n], i, j, x, tsem, act)

    def put_job(n, act):
        i, j = job(n)
        b = lax.rem(n, NBUF)
        put(obuf.at[b], i, j, 1 - x, osem.at[b], act)

    def start(cp):
        cp.start()

    def wait(cp):
        cp.wait()

    for n in range(LEAD):
        put_panel(jnp.int32(n), start)

    def body(n, _):
        i, j = job(n)
        b = lax.rem(n, NBUF)

        @pl.when(n >= NBUF)
        def _():
            put_job(n - NBUF, wait)

        @pl.when(i != j)
        def _():
            full_tile(obuf.at[b], o_ref, (), i, sc_ref, (side,), j)

        @pl.when(i == j)
        def _():
            diag_tile(obuf.at[b], o_ref, (), sc_ref, (side,), j, 2 * (1 - x) + y, col)
        put_job(n, start)

        @pl.when(n + LEAD < len(JOBS))
        def _():
            put_panel(jnp.minimum(n + LEAD, len(JOBS) - 1), start)
        return 0

    lax.fori_loop(0, len(JOBS), body, 0)

    def drain(n, _):
        put_panel(n, wait)

        @pl.when(n >= len(JOBS) - NBUF)
        def _():
            put_job(n, wait)
        return 0
    lax.fori_loop(0, len(JOBS), drain, 0)


def solution(mesh):
    def local_fn(a):
        a4 = pltpu.with_memory_space_constraint(a.reshape(NM, 2, BLOCK, PIECE), pltpu.HBM)
        any_spec = pl.BlockSpec(memory_space=pl.ANY)
        hbm = pl.BlockSpec(memory_space=pltpu.HBM)
        vmem = pl.BlockSpec(memory_space=pltpu.VMEM)
        dma = pltpu.SemaphoreType.DMA
        half_flops = 136 * 2 * BLOCK * BLOCK * K_DIM
        panels = pltpu.VMEM((2, PIECES, NM, BLOCK, PIECE), jnp.bfloat16)
        token = jax.ShapeDtypeStruct((8, 128), jnp.float32)
        sc, first = pl.pallas_call(
            first_kernel,
            out_shape=[panels, token],
            in_specs=[hbm],
            out_specs=[vmem, vmem],
            scratch_shapes=[dma(())] * 4,
            compiler_params=pltpu.CompilerParams(collective_id=0, has_side_effects=True, vmem_limit_bytes=2 * 1024 * 1024),
        )(a4)
        c, zeroed = pl.pallas_call(
            zero_kernel,
            out_shape=[jax.ShapeDtypeStruct((NM, 2, BLOCK, NM * BLOCK), jnp.bfloat16), token],
            in_specs=[any_spec],
            out_specs=[any_spec, vmem],
            scratch_shapes=[pltpu.VMEM((CH, BLOCK, TILE), jnp.bfloat16), dma(())],
            compiler_params=pltpu.CompilerParams(vmem_limit_bytes=4 * 1024 * 1024),
            cost_estimate=pl.CostEstimate(flops=half_flops, bytes_accessed=30 << 20, transcendentals=0),
        )(first)
        sc, o, t = pl.pallas_call(
            gather_kernel,
            out_shape=[panels,
                       pltpu.VMEM((PIECES, NM, BLOCK, PIECE), jnp.bfloat16),
                       pltpu.VMEM((len(JOBS), CH, BLOCK, TILE), jnp.bfloat16)],
            in_specs=[hbm, vmem, any_spec],
            out_specs=[vmem] * 3,
            input_output_aliases={1: 0},
            scratch_shapes=[pltpu.VMEM((NM, BLOCK, PIECE), jnp.bfloat16), pltpu.SemaphoreType.REGULAR,
                            dma((2,)), dma((2,)), dma((2,)), dma((2 * NC,)), dma((2 * NC,)), dma((2 * NC,)), dma((2 * NC,)),
                            dma((NC,)), dma((2, NC)), dma((2,)), dma((2,))],
            compiler_params=pltpu.CompilerParams(collective_id=1, has_side_effects=True, vmem_limit_bytes=8 * 1024 * 1024),
            cost_estimate=pl.CostEstimate(flops=half_flops, bytes_accessed=2 << 20, transcendentals=0),
        )(a4, sc, zeroed)
        c = pl.pallas_call(
            write_kernel,
            out_shape=jax.ShapeDtypeStruct((NM, 2, BLOCK, NM * BLOCK), jnp.bfloat16),
            in_specs=[vmem] * 3 + [any_spec],
            out_specs=any_spec,
            input_output_aliases={3: 0},
            scratch_shapes=[pltpu.VMEM((NBUF, CH, BLOCK, TILE), jnp.bfloat16), dma(()), dma((NBUF,))],
            compiler_params=pltpu.CompilerParams(vmem_limit_bytes=20 * 1024 * 1024),
            cost_estimate=pl.CostEstimate(flops=half_flops, bytes_accessed=34 << 20, transcendentals=0),
        )(sc, o, t, c)
        return c.reshape(2 * NM * BLOCK, NM * BLOCK)

    spec = P(('batch', 'row'), 'col')
    return jax.shard_map(local_fn, mesh=mesh, in_specs=(spec,), out_specs=spec, check_vma=False)
```

time: 73.6 us -> 69.6 us (0.946)
  the two profiles are of different devices: /device:TPU:0 before, /device:TPU:1 now
where the time goes in v4:
time: 69.6 us; the launch traced here: 69.5 us
  Pallas kernels  69.5 us (100%)
    pallas_call x1, Pallas kernels, local_fn(): pl.pallas_call(gather_kernel, out_shape=[panels, pltpu.VMEM((PIECES, NM,...  27 us
    pallas_call x1, Pallas kernels, local_fn(): pl.pallas_call(first_kernel, out_shape=[panels, token], in_specs=[hbm], o...  18.9 us
    pallas_call x1, Pallas kernels, local_fn(): pl.pallas_call(write_kernel, out_shape=jax.ShapeDtypeStruct((NM, 2, BLOCK...  13.3 us
    pallas_call x1, Pallas kernels, local_fn(): pl.pallas_call(zero_kernel, out_shape=[jax.ShapeDtypeStruct((NM, 2, BLOCK...  10.3 us

profile of v4, /device:TPU:1, one launch (start us, length us, event | category | flops | bytes accessed | tf_op | source)
XLA Modules:
  0.0 69.5 jit_solution(9576603822379798288)
XLA Ops:
  0.0 18.9 %shard_map.17 = (bf16[2,4,16,256,128]{4,3,2,1,0:T(8,128)(2,1)S(1)}, f32[8,128]{1,0:T(8,128)S(1)}) custom-call(bf16[16,2,256,128]{3,2,1,0:T(8,128)(2,1)} %bitcast.2), custom_call_target="tpu_custom_call" | custom-call | tf_op jit(solution)/shard_map/pallas_call | solution.py:307
  18.9 10.3 %shard_map.18 = (bf16[16,2,256,4096]{3,2,1,0:T(8,128)(2,1)}, f32[8,128]{1,0:T(8,128)S(1)}) custom-call(f32[8,128]{1,0:T(8,128)S(1)} %get-tuple-element.13.token_ref), custom_call_target="tpu_custom_call" | custom-call | flops 9126805504 | bytes 31457280 | tf_op jit(solution)/shard_map/pallas_call | solution.py:315
  29.2 27.0 %shard_map.19 = (bf16[2,4,16,256,128]{4,3,2,1,0:T(8,128)(2,1)S(1)}, bf16[4,16,256,128]{3,2,1,0:T(8,128)(2,1)S(1)}, bf16[10,4,256,1024]{3,2,1,0:T(8,128)(2,1)S(1)}) custom-call(bf16[16,2,256,128]{3,2,1,0:T(8,128)(2,1)} %bitcast.3, bf16[2,4,16,256,128]{4,3,2,1,0:T(8,128)(2,1)S(1)} %get-tuple-element.12.sc_in, ...), custom_call_target="tpu_custom_call", output_to_operand_aliasing={{0}: (1, {})} | custom-call | flops 9126805504 | bytes 2097152 | tf_op jit(solution)/shard_map/pallas_call | solution.py:324
  56.2 13.3 %shard_map.20 = bf16[16,2,256,4096]{3,2,1,0:T(8,128)(2,1)} custom-call(bf16[2,4,16,256,128]{4,3,2,1,0:T(8,128)(2,1)S(1)} %get-tuple-element.15.sc_ref, bf16[4,16,256,128]{3,2,1,0:T(8,128)(2,1)S(1)} %get-tuple-element.16.o_ref, bf16[10,4,256,1024]{3,2,1,0:T(8,128)(2,1)S(1)} %get-tuple-element.17.t_ref, ...), custom_call_target="tpu_custom_call", output_to_operand_aliasing={{}: (3, {})} | custom-call | flops 9126805504 | bytes 35651584 | tf_op jit(solution)/shard_map/pallas_call | solution.py:338

commit v5 on v4

--- a/solution.py
+++ b/solution.py
@@ -14,9 +14,15 @@
 CH = 4
 NC = NM // CH
 NBUF = 5
-LEAD = 3
+LEAD = 4
 TILE = CH * BLOCK
 JOBS = [(i, j) for j in range(NC) for i in range(j, NC)]
+NA = 3
+NR = 2
+O_ORDER = (3, 0, 1, 2)
+EXTRA = [(3, 0), (3, 1)]
+LATER = [job for job in JOBS if job not in EXTRA]
+PANELS = [(i, j, 0) for i, j in JOBS] + [(i, j, 1) for i, j in EXTRA]
 
 
 def positions():
@@ -77,8 +83,9 @@
         barrier = pltpu.get_barrier_semaphore()
         signal(barrier, (x_peer, y_peer))
         pl.semaphore_wait(barrier, 2)
-        xc = remote(a_ref.at[:, 1 - x], sc_ref.at[0, 2], x_send, x_recv, x_peer)
-        yc = remote(a_ref.at[:, x], sc_ref.at[1, 1], y_send, y_recv, y_peer)
+        part = pl.ds(0, NA * CH)
+        xc = remote(a_ref.at[part, 1 - x], sc_ref.at[0, 2, part], x_send, x_recv, x_peer)
+        yc = remote(a_ref.at[part, x], sc_ref.at[1, 1, part], y_send, y_recv, y_peer)
         xc.start()
         yc.start()
         xc.wait()
@@ -103,15 +110,17 @@
         cp.wait()
 
 
-def gather_kernel(a_ref, sc_in, token_ref, sc_ref, o_ref, t_ref, yb, join, lsem, d_send, d_recv, x_send, x_recv, r_send, r_recv,
-                  y_send, y_recv, b_send, b_recv):
+def gather_kernel(a_ref, sc_in, token_ref, sc_ref, o_ref, t_ref, yb, yr, join, lsem, d_send, d_recv, x_send, x_recv, r_send, r_recv,
+                  y_send, y_recv, b_send, b_recv, q_send, q_recv, u_send, u_recv):
     y, x, k, col = positions()
     late = k != y
+    early = k == y
     side = jnp.where(late, 1, 0)
     partner = (0, y, 2 * x + 1 - k)
     x_peer = (0, y, 2 * (1 - x) + k)
     y_early = (0, 1 - y, 2 * x + 1 - y)
     y_late = (0, 1 - y, 2 * x + y)
+    tail = pl.ds(NA * CH, (NC - NA) * CH)
 
     def x_copy(n):
         c = n % NC
@@ -128,8 +137,15 @@
     def y_copy(s, c):
         return remote(sc_ref.at[0, 2, chunk(c)], sc_ref.at[1, 2 + s, chunk(c)], y_send.at[c], y_recv.at[s, c], y_late)
 
+    def yr_copy(c):
+        return remote(sc_ref.at[0, 2, chunk(c)], yr.at[chunk(c)], q_send.at[c], q_recv.at[c], y_early)
+
+    def yr_relay(c):
+        return remote(yr.at[chunk(c)], sc_ref.at[1, 2, chunk(c)], y_send.at[c], y_recv.at[0, c], partner)
+
     yb_copy = remote(a_ref.at[:, x], yb, b_send.at[0], b_recv.at[0], y_early)
     yb_relay = remote(yb, sc_ref.at[1, 0], b_send.at[1], b_recv.at[1], partner)
+    u_copy = remote(a_ref.at[tail, x], sc_ref.at[1, 1, tail], u_send, u_recv, y_late)
     d_copies = [remote(a_ref.at[:, x], sc_ref.at[0, 1], d_send.at[0], d_recv.at[0], partner),
                 remote(a_ref.at[:, 1 - x], o_ref.at[1], d_send.at[1], d_recv.at[1], partner)]
     l_copies = [pltpu.make_async_copy(a_ref.at[:, x], sc_ref.at[0, 0], lsem.at[0]),
@@ -138,21 +154,28 @@
         cp.start()
     barrier = pltpu.get_barrier_semaphore()
 
-    @pl.when(jnp.logical_not(late))
+    @pl.when(early)
     def _():
         signal(barrier, (x_peer, y_early, partner, y_late))
         pl.semaphore_wait(barrier, 2)
-        for n in range(2 * NC):
+        for n in list(range(NC)) + [NC + c for c in O_ORDER]:
             x_copy(n).start()
         yb_copy.start()
+        for c in range(NR):
+            x_copy(c).wait_recv()
+            yr_copy(c).start()
         pl.semaphore_wait(join, 2)
         d_copies[0].start()
         for c in range(NC):
-            x_copy(c).wait_recv()
-            y_copy(0, c).start()
+            if c >= NR:
+                x_copy(c).wait_recv()
+                y_copy(0, c).start()
             relay_copy(c).start()
         yb_copy.wait_recv()
         yb_relay.start()
+        for c in range(NR):
+            yr_copy(c).wait_recv()
+            yr_relay(c).start()
         d_copies[1].start()
 
     @pl.when(late)
@@ -160,14 +183,19 @@
         signal(barrier, (x_peer, y_late))
         pl.semaphore_wait(barrier, 4)
         signal(join, (partner, y_early))
-        for n in range(NC, 2 * NC):
+        for n in list(range(NA, NC)) + [NC + c for c in O_ORDER]:
             x_copy(n).start()
-        for c in range(NC):
+        for c in range(NA):
             y_copy(1, c).start()
-        for c in range(NC):
+        u_copy.start()
+        for c in range(NA):
             relay_copy(c).start()
         for cp in d_copies:
             cp.start()
+        for c in range(NA, NC):
+            x_copy(c).wait_recv()
+            relay_copy(c).start()
+            y_copy(1, c).start()
 
     l_copies[0].wait()
     d_copies[0].wait_recv()
@@ -176,13 +204,22 @@
 
     row_blk = 2 * x + y
     for c in range(NC):
-        x_copy(NC + c).wait_recv()
-        relay_copy(NC + c).start()
+        x_copy(NC + O_ORDER[c]).wait_recv()
+        relay_copy(NC + O_ORDER[c]).start()
+        if c == NC - 2:
+            l_copies[1].wait()
+            d_copies[1].wait_recv()
+            relay_copy(NC + O_ORDER[0]).wait_recv()
+        if c >= NC - 2:
+            m = c - (NC - 2)
+            full_tile(t_ref.at[len(JOBS) + m], o_ref, (), EXTRA[m][0], sc_ref, (side,), EXTRA[m][1])
 
         @pl.when(late)
         def _():
             if c == 0:
                 yb_relay.wait_recv()
+            if c == NA:
+                u_copy.wait_recv()
             for s in range(2):
                 y_copy(s, c).wait_recv()
 
@@ -195,23 +232,27 @@
         if c + 1 < NC:
             lax.fori_loop(c + 1, NC, body, 0)
 
-    l_copies[1].wait()
-    d_copies[1].wait_recv()
-    for c in range(NC):
+    for c in O_ORDER[1:]:
         relay_copy(NC + c).wait_recv()
     for n in range(2 * NC):
         relay_copy(n).wait_send()
-    for n in range(NC, 2 * NC):
+    for n in range(NA, 2 * NC):
         x_copy(n).wait_send()
     for cp in d_copies:
         cp.wait_send()
     for c in range(NC):
         y_copy(0, c).wait_send()
 
-    @pl.when(jnp.logical_not(late))
-    def _():
-        for n in range(NC):
+    @pl.when(late)
+    def _():
+        u_copy.wait_send()
+
+    @pl.when(early)
+    def _():
+        for n in range(NA):
             x_copy(n).wait_send()
+        for c in range(NR):
+            yr_copy(c).wait_send()
         yb_copy.wait_send()
         yb_relay.wait_send()
 
@@ -227,8 +268,8 @@
     y, x, k, col = positions()
     side = jnp.where(k != y, 1, 0)
 
-    def job(n):
-        return lookup(n, [v[0] for v in JOBS]), lookup(n, [v[1] for v in JOBS])
+    def pick(n, values):
+        return [lookup(n, column) for column in zip(*values)]
 
     def put(src, i, j, s, sem, act):
         @pl.when(i != j)
@@ -243,11 +284,11 @@
                     c_ref.at[pl.ds(i * CH + q, CH - q), s, :, pl.ds(pl.multiple_of(j * TILE + q * BLOCK, BLOCK), BLOCK)], sem))
 
     def put_panel(n, act):
-        i, j = job(n)
-        put(t_ref.at[n], i, j, x, tsem, act)
+        i, j, cls = pick(n, PANELS)
+        put(t_ref.at[n], i, j, jnp.where(cls == 0, x, 1 - x), tsem, act)
 
     def put_job(n, act):
-        i, j = job(n)
+        i, j = pick(n, LATER)
         b = lax.rem(n, NBUF)
         put(obuf.at[b], i, j, 1 - x, osem.at[b], act)
 
@@ -261,7 +302,7 @@
         put_panel(jnp.int32(n), start)
 
     def body(n, _):
-        i, j = job(n)
+        i, j = pick(n, LATER)
         b = lax.rem(n, NBUF)
 
         @pl.when(n >= NBUF)
@@ -277,21 +318,21 @@
             diag_tile(obuf.at[b], o_ref, (), sc_ref, (side,), j, 2 * (1 - x) + y, col)
         put_job(n, start)
 
-        @pl.when(n + LEAD < len(JOBS))
-        def _():
-            put_panel(jnp.minimum(n + LEAD, len(JOBS) - 1), start)
+        @pl.when(n + LEAD < len(PANELS))
+        def _():
+            put_panel(jnp.minimum(n + LEAD, len(PANELS) - 1), start)
         return 0
 
-    lax.fori_loop(0, len(JOBS), body, 0)
+    lax.fori_loop(0, len(LATER), body, 0)
 
     def drain(n, _):
         put_panel(n, wait)
 
-        @pl.when(n >= len(JOBS) - NBUF)
-        def _():
-            put_job(n, wait)
+        @pl.when(jnp.logical_and(n >= len(LATER) - NBUF, n < len(LATER)))
+        def _():
+            put_job(jnp.minimum(n, len(LATER) - 1), wait)
         return 0
-    lax.fori_loop(0, len(JOBS), drain, 0)
+    lax.fori_loop(0, len(PANELS), drain, 0)
 
 
 def solution(mesh):
@@ -325,13 +366,14 @@
             gather_kernel,
             out_shape=[panels,
                        pltpu.VMEM((PIECES, NM, BLOCK, PIECE), jnp.bfloat16),
-                       pltpu.VMEM((len(JOBS), CH, BLOCK, TILE), jnp.bfloat16)],
+                       pltpu.VMEM((len(PANELS), CH, BLOCK, TILE), jnp.bfloat16)],
             in_specs=[hbm, vmem, any_spec],
             out_specs=[vmem] * 3,
             input_output_aliases={1: 0},
-            scratch_shapes=[pltpu.VMEM((NM, BLOCK, PIECE), jnp.bfloat16), pltpu.SemaphoreType.REGULAR,
+            scratch_shapes=[pltpu.VMEM((NM, BLOCK, PIECE), jnp.bfloat16), pltpu.VMEM((NR * CH, BLOCK, PIECE), jnp.bfloat16),
+                            pltpu.SemaphoreType.REGULAR,
                             dma((2,)), dma((2,)), dma((2,)), dma((2 * NC,)), dma((2 * NC,)), dma((2 * NC,)), dma((2 * NC,)),
-                            dma((NC,)), dma((2, NC)), dma((2,)), dma((2,))],
+                            dma((NC,)), dma((2, NC)), dma((2,)), dma((2,)), dma((NR,)), dma((NR,)), dma(()), dma(())],
             compiler_params=pltpu.CompilerParams(collective_id=1, has_side_effects=True, vmem_limit_bytes=8 * 1024 * 1024),
             cost_estimate=pl.CostEstimate(flops=half_flops, bytes_accessed=2 << 20, transcendentals=0),
         )(a4, sc, zeroed)
@@ -342,7 +384,7 @@
             out_specs=any_spec,
             input_output_aliases={3: 0},
             scratch_shapes=[pltpu.VMEM((NBUF, CH, BLOCK, TILE), jnp.bfloat16), dma(()), dma((NBUF,))],
-            compiler_params=pltpu.CompilerParams(vmem_limit_bytes=20 * 1024 * 1024),
+            compiler_params=pltpu.CompilerParams(vmem_limit_bytes=15 * 1024 * 1024),
             cost_estimate=pl.CostEstimate(flops=half_flops, bytes_accessed=34 << 20, transcendentals=0),
         )(sc, o, t, c)
         return c.reshape(2 * NM * BLOCK, NM * BLOCK)

time: 69.6 us -> 66.7 us (0.958)
  the two profiles are of different devices: /device:TPU:1 before, /device:TPU:0 now
where the time goes in v5:
time: 66.7 us; the launch traced here: 66.3 us
  Pallas kernels  66.3 us (99%)
    pallas_call x1, Pallas kernels, local_fn(): pl.pallas_call(gather_kernel, out_shape=[panels, pltpu.VMEM((PIECES, NM,...  44.3 us
    pallas_call x1, Pallas kernels, local_fn(): pl.pallas_call(write_kernel, out_shape=jax.ShapeDtypeStruct((NM, 2, BLOCK...  11.6 us
    pallas_call x1, Pallas kernels, local_fn(): pl.pallas_call(zero_kernel, out_shape=[jax.ShapeDtypeStruct((NM, 2, BLOCK...  10.3 us

profile of v5, /device:TPU:0, one launch (start us, length us, event | category | flops | bytes accessed | tf_op | source)
XLA Modules:
  0.0 66.3 jit_solution(13707379456362450102)
XLA Ops:
  0.0 10.3 %shard_map.18 = (bf16[16,2,256,4096]{3,2,1,0:T(8,128)(2,1)}, f32[8,128]{1,0:T(8,128)S(1)}) custom-call(f32[8,128]{1,0:T(8,128)S(1)} %get-tuple-element.13.token_ref), custom_call_target="tpu_custom_call" | custom-call | flops 9126805504 | bytes 31457280 | tf_op jit(solution)/shard_map/pallas_call | solution.py:356
  10.4 44.3 %shard_map.19 = (bf16[2,4,16,256,128]{4,3,2,1,0:T(8,128)(2,1)S(1)}, bf16[4,16,256,128]{3,2,1,0:T(8,128)(2,1)S(1)}, bf16[12,4,256,1024]{3,2,1,0:T(8,128)(2,1)S(1)}) custom-call(bf16[16,2,256,128]{3,2,1,0:T(8,128)(2,1)} %bitcast.3, bf16[2,4,16,256,128]{4,3,2,1,0:T(8,128)(2,1)S(1)} %get-tuple-element.12.sc_in, ...), custom_call_target="tpu_custom_call", output_to_operand_aliasing={{0}: (1, {})} | custom-call | flops 9126805504 | bytes 2097152 | tf_op jit(solution)/shard_map/pallas_call | solution.py:365
  54.7 11.6 %shard_map.20 = bf16[16,2,256,4096]{3,2,1,0:T(8,128)(2,1)} custom-call(bf16[2,4,16,256,128]{4,3,2,1,0:T(8,128)(2,1)S(1)} %get-tuple-element.15.sc_ref, bf16[4,16,256,128]{3,2,1,0:T(8,128)(2,1)S(1)} %get-tuple-element.16.o_ref, bf16[12,4,256,1024]{3,2,1,0:T(8,128)(2,1)S(1)} %get-tuple-element.17.t_ref, ...), custom_call_target="tpu_custom_call", output_to_operand_aliasing={{}: (3, {})} | custom-call | flops 9126805504 | bytes 35651584 | tf_op jit(solution)/shard_map/pallas_call | solution.py:380
  (1 shorter events, 0.0 us)

commit v6 on v5

--- a/solution.py
+++ b/solution.py
@@ -17,7 +17,7 @@
 LEAD = 4
 TILE = CH * BLOCK
 JOBS = [(i, j) for j in range(NC) for i in range(j, NC)]
-NA = 3
+NA = 14
 NR = 2
 O_ORDER = (3, 0, 1, 2)
 EXTRA = [(3, 0), (3, 1)]
@@ -83,7 +83,7 @@
         barrier = pltpu.get_barrier_semaphore()
         signal(barrier, (x_peer, y_peer))
         pl.semaphore_wait(barrier, 2)
-        part = pl.ds(0, NA * CH)
+        part = pl.ds(0, NA)
         xc = remote(a_ref.at[part, 1 - x], sc_ref.at[0, 2, part], x_send, x_recv, x_peer)
         yc = remote(a_ref.at[part, x], sc_ref.at[1, 1, part], y_send, y_recv, y_peer)
         xc.start()
@@ -111,7 +111,7 @@
 
 
 def gather_kernel(a_ref, sc_in, token_ref, sc_ref, o_ref, t_ref, yb, yr, join, lsem, d_send, d_recv, x_send, x_recv, r_send, r_recv,
-                  y_send, y_recv, b_send, b_recv, q_send, q_recv, u_send, u_recv):
+                  y_send, y_recv, b_send, b_recv, q_send, q_recv, u_send, u_recv, v_send, v_recv):
     y, x, k, col = positions()
     late = k != y
     early = k == y
@@ -120,7 +120,7 @@
     x_peer = (0, y, 2 * (1 - x) + k)
     y_early = (0, 1 - y, 2 * x + 1 - y)
     y_late = (0, 1 - y, 2 * x + y)
-    tail = pl.ds(NA * CH, (NC - NA) * CH)
+    tail = pl.ds(NA, NM - NA)
 
     def x_copy(n):
         c = n % NC
@@ -145,6 +145,7 @@
 
     yb_copy = remote(a_ref.at[:, x], yb, b_send.at[0], b_recv.at[0], y_early)
     yb_relay = remote(yb, sc_ref.at[1, 0], b_send.at[1], b_recv.at[1], partner)
+    x_tail = remote(a_ref.at[tail, 1 - x], sc_ref.at[0, 2, tail], v_send, v_recv, x_peer)
     u_copy = remote(a_ref.at[tail, x], sc_ref.at[1, 1, tail], u_send, u_recv, y_late)
     d_copies = [remote(a_ref.at[:, x], sc_ref.at[0, 1], d_send.at[0], d_recv.at[0], partner),
                 remote(a_ref.at[:, 1 - x], o_ref.at[1], d_send.at[1], d_recv.at[1], partner)]
@@ -183,19 +184,19 @@
         signal(barrier, (x_peer, y_late))
         pl.semaphore_wait(barrier, 4)
         signal(join, (partner, y_early))
-        for n in list(range(NA, NC)) + [NC + c for c in O_ORDER]:
-            x_copy(n).start()
-        for c in range(NA):
+        x_tail.start()
+        for c in O_ORDER:
+            x_copy(NC + c).start()
+        for c in range(NC - 1):
             y_copy(1, c).start()
         u_copy.start()
-        for c in range(NA):
+        for c in range(NC - 1):
             relay_copy(c).start()
         for cp in d_copies:
             cp.start()
-        for c in range(NA, NC):
-            x_copy(c).wait_recv()
-            relay_copy(c).start()
-            y_copy(1, c).start()
+        x_tail.wait_recv()
+        relay_copy(NC - 1).start()
+        y_copy(1, NC - 1).start()
 
     l_copies[0].wait()
     d_copies[0].wait_recv()
@@ -218,7 +219,7 @@
         def _():
             if c == 0:
                 yb_relay.wait_recv()
-            if c == NA:
+            if c == NC - 1:
                 u_copy.wait_recv()
             for s in range(2):
                 y_copy(s, c).wait_recv()
@@ -236,7 +237,7 @@
         relay_copy(NC + c).wait_recv()
     for n in range(2 * NC):
         relay_copy(n).wait_send()
-    for n in range(NA, 2 * NC):
+    for n in range(NC, 2 * NC):
         x_copy(n).wait_send()
     for cp in d_copies:
         cp.wait_send()
@@ -246,10 +247,11 @@
     @pl.when(late)
     def _():
         u_copy.wait_send()
+        x_tail.wait_send()
 
     @pl.when(early)
     def _():
-        for n in range(NA):
+        for n in range(NC):
             x_copy(n).wait_send()
         for c in range(NR):
             yr_copy(c).wait_send()
@@ -373,7 +375,7 @@
             scratch_shapes=[pltpu.VMEM((NM, BLOCK, PIECE), jnp.bfloat16), pltpu.VMEM((NR * CH, BLOCK, PIECE), jnp.bfloat16),
                             pltpu.SemaphoreType.REGULAR,
                             dma((2,)), dma((2,)), dma((2,)), dma((2 * NC,)), dma((2 * NC,)), dma((2 * NC,)), dma((2 * NC,)),
-                            dma((NC,)), dma((2, NC)), dma((2,)), dma((2,)), dma((NR,)), dma((NR,)), dma(()), dma(())],
+                            dma((NC,)), dma((2, NC)), dma((2,)), dma((2,)), dma((NR,)), dma((NR,))] + [dma(())] * 4,
             compiler_params=pltpu.CompilerParams(collective_id=1, has_side_effects=True, vmem_limit_bytes=8 * 1024 * 1024),
             cost_estimate=pl.CostEstimate(flops=half_flops, bytes_accessed=2 << 20, transcendentals=0),
         )(a4, sc, zeroed)

time: 66.7 us -> 65.3 us (0.979)
  Pallas kernels: 66.3 us -> 64.9 us
    pallas_call x1, Pallas kernels: 44.3 us -> 42.9 us  [local_fn(): pl.pallas_call(gather_kernel, out_shape=[panels, pltpu.VMEM((PIECES, NM,...]
where the time goes in v6:
time: 65.3 us; the launch traced here: 64.9 us
  Pallas kernels  64.9 us (99%)
    pallas_call x1, Pallas kernels, local_fn(): pl.pallas_call(gather_kernel, out_shape=[panels, pltpu.VMEM((PIECES, NM,...  42.9 us
    pallas_call x1, Pallas kernels, local_fn(): pl.pallas_call(write_kernel, out_shape=jax.ShapeDtypeStruct((NM, 2, BLOCK...  11.6 us
    pallas_call x1, Pallas kernels, local_fn(): pl.pallas_call(zero_kernel, out_shape=[jax.ShapeDtypeStruct((NM, 2, BLOCK...  10.3 us

profile of v6, /device:TPU:0, one launch (start us, length us, event | category | flops | bytes accessed | tf_op | source)
XLA Modules:
  0.0 64.9 jit_solution(4874731964701283667)
XLA Ops:
  0.0 10.3 %shard_map.18 = (bf16[16,2,256,4096]{3,2,1,0:T(8,128)(2,1)}, f32[8,128]{1,0:T(8,128)S(1)}) custom-call(f32[8,128]{1,0:T(8,128)S(1)} %get-tuple-element.13.token_ref), custom_call_target="tpu_custom_call" | custom-call | flops 9126805504 | bytes 31457280 | tf_op jit(solution)/shard_map/pallas_call | solution.py:358
  10.4 42.9 %shard_map.19 = (bf16[2,4,16,256,128]{4,3,2,1,0:T(8,128)(2,1)S(1)}, bf16[4,16,256,128]{3,2,1,0:T(8,128)(2,1)S(1)}, bf16[12,4,256,1024]{3,2,1,0:T(8,128)(2,1)S(1)}) custom-call(bf16[16,2,256,128]{3,2,1,0:T(8,128)(2,1)} %bitcast.3, bf16[2,4,16,256,128]{4,3,2,1,0:T(8,128)(2,1)S(1)} %get-tuple-element.12.sc_in, ...), custom_call_target="tpu_custom_call", output_to_operand_aliasing={{0}: (1, {})} | custom-call | flops 9126805504 | bytes 2097152 | tf_op jit(solution)/shard_map/pallas_call | solution.py:367
  53.3 11.6 %shard_map.20 = bf16[16,2,256,4096]{3,2,1,0:T(8,128)(2,1)} custom-call(bf16[2,4,16,256,128]{4,3,2,1,0:T(8,128)(2,1)S(1)} %get-tuple-element.15.sc_ref, bf16[4,16,256,128]{3,2,1,0:T(8,128)(2,1)S(1)} %get-tuple-element.16.o_ref, bf16[12,4,256,1024]{3,2,1,0:T(8,128)(2,1)S(1)} %get-tuple-element.17.t_ref, ...), custom_call_target="tpu_custom_call", output_to_operand_aliasing={{}: (3, {})} | custom-call | flops 9126805504 | bytes 35651584 | tf_op jit(solution)/shard_map/pallas_call | solution.py:382
  (1 shorter events, 0.0 us)

commit v7 on v6

--- a/solution.py
+++ b/solution.py
@@ -17,12 +17,15 @@
 LEAD = 4
 TILE = CH * BLOCK
 JOBS = [(i, j) for j in range(NC) for i in range(j, NC)]
-NA = 14
+LAST = (NC - 1, NC - 1)
+NOW = [job for job in JOBS if job != LAST]
+NAX, NAY = 15, 14
 NR = 2
-O_ORDER = (3, 0, 1, 2)
+O_PARTS = ((12, 4), (0, 4), (4, 4), (8, 3), (11, 1))
+NX = NC + len(O_PARTS)
 EXTRA = [(3, 0), (3, 1)]
 LATER = [job for job in JOBS if job not in EXTRA]
-PANELS = [(i, j, 0) for i, j in JOBS] + [(i, j, 1) for i, j in EXTRA]
+PANELS = [(i, j, 0) for i, j in NOW] + [(i, j, 1) for i, j in EXTRA]
 
 
 def positions():
@@ -83,9 +86,9 @@
         barrier = pltpu.get_barrier_semaphore()
         signal(barrier, (x_peer, y_peer))
         pl.semaphore_wait(barrier, 2)
-        part = pl.ds(0, NA)
-        xc = remote(a_ref.at[part, 1 - x], sc_ref.at[0, 2, part], x_send, x_recv, x_peer)
-        yc = remote(a_ref.at[part, x], sc_ref.at[1, 1, part], y_send, y_recv, y_peer)
+        px, py = pl.ds(0, NAX), pl.ds(0, NAY)
+        xc = remote(a_ref.at[px, 1 - x], sc_ref.at[0, 2, px], x_send, x_recv, x_peer)
+        yc = remote(a_ref.at[py, x], sc_ref.at[1, 1, py], y_send, y_recv, y_peer)
         xc.start()
         yc.start()
         xc.wait()
@@ -120,19 +123,19 @@
     x_peer = (0, y, 2 * (1 - x) + k)
     y_early = (0, 1 - y, 2 * x + 1 - y)
     y_late = (0, 1 - y, 2 * x + y)
-    tail = pl.ds(NA, NM - NA)
+    tx, ty = pl.ds(NAX, NM - NAX), pl.ds(NAY, NM - NAY)
 
     def x_copy(n):
-        c = n % NC
         if n < NC:
-            return remote(a_ref.at[chunk(c), 1 - x], sc_ref.at[0, 2, chunk(c)], x_send.at[n], x_recv.at[n], x_peer)
-        return remote(a_ref.at[chunk(c), x], o_ref.at[2, chunk(c)], x_send.at[n], x_recv.at[n], x_peer)
+            return remote(a_ref.at[chunk(n), 1 - x], sc_ref.at[0, 2, chunk(n)], x_send.at[n], x_recv.at[n], x_peer)
+        part = pl.ds(*O_PARTS[n - NC])
+        return remote(a_ref.at[part, x], o_ref.at[2, part], x_send.at[n], x_recv.at[n], x_peer)
 
     def relay_copy(n):
-        c = n % NC
         if n < NC:
-            return remote(sc_ref.at[0, 2, chunk(c)], sc_ref.at[0, 3, chunk(c)], r_send.at[n], r_recv.at[n], partner)
-        return remote(o_ref.at[2, chunk(c)], o_ref.at[3, chunk(c)], r_send.at[n], r_recv.at[n], partner)
+            return remote(sc_ref.at[0, 2, chunk(n)], sc_ref.at[0, 3, chunk(n)], r_send.at[n], r_recv.at[n], partner)
+        part = pl.ds(*O_PARTS[n - NC])
+        return remote(o_ref.at[2, part], o_ref.at[3, part], r_send.at[n], r_recv.at[n], partner)
 
     def y_copy(s, c):
         return remote(sc_ref.at[0, 2, chunk(c)], sc_ref.at[1, 2 + s, chunk(c)], y_send.at[c], y_recv.at[s, c], y_late)
@@ -145,8 +148,8 @@
 
     yb_copy = remote(a_ref.at[:, x], yb, b_send.at[0], b_recv.at[0], y_early)
     yb_relay = remote(yb, sc_ref.at[1, 0], b_send.at[1], b_recv.at[1], partner)
-    x_tail = remote(a_ref.at[tail, 1 - x], sc_ref.at[0, 2, tail], v_send, v_recv, x_peer)
-    u_copy = remote(a_ref.at[tail, x], sc_ref.at[1, 1, tail], u_send, u_recv, y_late)
+    x_tail = remote(a_ref.at[tx, 1 - x], sc_ref.at[0, 2, tx], v_send, v_recv, x_peer)
+    u_copy = remote(a_ref.at[ty, x], sc_ref.at[1, 1, ty], u_send, u_recv, y_late)
     d_copies = [remote(a_ref.at[:, x], sc_ref.at[0, 1], d_send.at[0], d_recv.at[0], partner),
                 remote(a_ref.at[:, 1 - x], o_ref.at[1], d_send.at[1], d_recv.at[1], partner)]
     l_copies = [pltpu.make_async_copy(a_ref.at[:, x], sc_ref.at[0, 0], lsem.at[0]),
@@ -159,7 +162,7 @@
     def _():
         signal(barrier, (x_peer, y_early, partner, y_late))
         pl.semaphore_wait(barrier, 2)
-        for n in list(range(NC)) + [NC + c for c in O_ORDER]:
+        for n in range(NX):
             x_copy(n).start()
         yb_copy.start()
         for c in range(NR):
@@ -185,8 +188,8 @@
         pl.semaphore_wait(barrier, 4)
         signal(join, (partner, y_early))
         x_tail.start()
-        for c in O_ORDER:
-            x_copy(NC + c).start()
+        for n in range(NC, NX):
+            x_copy(n).start()
         for c in range(NC - 1):
             y_copy(1, c).start()
         u_copy.start()
@@ -205,15 +208,9 @@
 
     row_blk = 2 * x + y
     for c in range(NC):
-        x_copy(NC + O_ORDER[c]).wait_recv()
-        relay_copy(NC + O_ORDER[c]).start()
-        if c == NC - 2:
-            l_copies[1].wait()
-            d_copies[1].wait_recv()
-            relay_copy(NC + O_ORDER[0]).wait_recv()
-        if c >= NC - 2:
-            m = c - (NC - 2)
-            full_tile(t_ref.at[len(JOBS) + m], o_ref, (), EXTRA[m][0], sc_ref, (side,), EXTRA[m][1])
+        for n in ([c] if c < NC - 1 else range(c, len(O_PARTS))):
+            x_copy(NC + n).wait_recv()
+            relay_copy(NC + n).start()
 
         @pl.when(late)
         def _():
@@ -224,20 +221,27 @@
             for s in range(2):
                 y_copy(s, c).wait_recv()
 
-        base = JOBS.index((c, c))
-        diag_tile(t_ref.at[base], sc_ref, (0,), sc_ref, (side,), c, row_blk, col)
-
-        def body(i, _):
-            full_tile(t_ref.at[base + i - c], sc_ref, (0,), i, sc_ref, (side,), c)
-            return 0
-        if c + 1 < NC:
+        if c < NC - 1:
+            base = NOW.index((c, c))
+            diag_tile(t_ref.at[base], sc_ref, (0,), sc_ref, (side,), c, row_blk, col)
+
+            def body(i, _):
+                full_tile(t_ref.at[base + i - c], sc_ref, (0,), i, sc_ref, (side,), c)
+                return 0
             lax.fori_loop(c + 1, NC, body, 0)
-
-    for c in O_ORDER[1:]:
-        relay_copy(NC + c).wait_recv()
-    for n in range(2 * NC):
+        if c == 1:
+            l_copies[1].wait()
+            d_copies[1].wait_recv()
+            relay_copy(NC).wait_recv()
+        if c in (1, 2):
+            i, j = EXTRA[c - 1]
+            full_tile(t_ref.at[len(NOW) + c - 1], o_ref, (), i, sc_ref, (side,), j)
+
+    for n in range(1, len(O_PARTS)):
+        relay_copy(NC + n).wait_recv()
+    for n in range(NX):
         relay_copy(n).wait_send()
-    for n in range(NC, 2 * NC):
+    for n in range(NC, NX):
         x_copy(n).wait_send()
     for cp in d_copies:
         cp.wait_send()
@@ -326,15 +330,20 @@
         return 0
 
     lax.fori_loop(0, len(LATER), body, 0)
+    last_slot = len(LATER) % NBUF
+    put_job(jnp.int32(len(LATER) - NBUF), wait)
+    diag_tile(obuf.at[last_slot], sc_ref, (0,), sc_ref, (side,), LAST[1], 2 * x + y, col)
+    put(obuf.at[last_slot], jnp.int32(LAST[0]), jnp.int32(LAST[1]), x, osem.at[last_slot], start)
 
     def drain(n, _):
         put_panel(n, wait)
 
-        @pl.when(jnp.logical_and(n >= len(LATER) - NBUF, n < len(LATER)))
+        @pl.when(jnp.logical_and(n > len(LATER) - NBUF, n < len(LATER)))
         def _():
             put_job(jnp.minimum(n, len(LATER) - 1), wait)
         return 0
     lax.fori_loop(0, len(PANELS), drain, 0)
+    put(obuf.at[last_slot], jnp.int32(LAST[0]), jnp.int32(LAST[1]), x, osem.at[last_slot], wait)
 
 
 def solution(mesh):
@@ -374,7 +383,7 @@
             input_output_aliases={1: 0},
             scratch_shapes=[pltpu.VMEM((NM, BLOCK, PIECE), jnp.bfloat16), pltpu.VMEM((NR * CH, BLOCK, PIECE), jnp.bfloat16),
                             pltpu.SemaphoreType.REGULAR,
-                            dma((2,)), dma((2,)), dma((2,)), dma((2 * NC,)), dma((2 * NC,)), dma((2 * NC,)), dma((2 * NC,)),
+                            dma((2,)), dma((2,)), dma((2,)), dma((NX,)), dma((NX,)), dma((NX,)), dma((NX,)),
                             dma((NC,)), dma((2, NC)), dma((2,)), dma((2,)), dma((NR,)), dma((NR,))] + [dma(())] * 4,
             compiler_params=pltpu.CompilerParams(collective_id=1, has_side_effects=True, vmem_limit_bytes=8 * 1024 * 1024),
             cost_estimate=pl.CostEstimate(flops=half_flops, bytes_accessed=2 << 20, transcendentals=0),

time: 65.3 us -> 65.5 us (level)
  no operation moved by 1% of the time
where the time goes in v7:
time: 65.5 us; the launch traced here: 65.4 us
  Pallas kernels  65.4 us (100%)
    pallas_call x1, Pallas kernels, local_fn(): pl.pallas_call(gather_kernel, out_shape=[panels, pltpu.VMEM((PIECES, NM,...  43.4 us
    pallas_call x1, Pallas kernels, local_fn(): pl.pallas_call(write_kernel, out_shape=jax.ShapeDtypeStruct((NM, 2, BLOCK...  11.6 us
    pallas_call x1, Pallas kernels, local_fn(): pl.pallas_call(zero_kernel, out_shape=[jax.ShapeDtypeStruct((NM, 2, BLOCK...  10.3 us

profile of v7, /device:TPU:0, one launch (start us, length us, event | category | flops | bytes accessed | tf_op | source)
XLA Modules:
  0.0 65.4 jit_solution(9754879860683513733)
XLA Ops:
  0.0 10.3 %shard_map.18 = (bf16[16,2,256,4096]{3,2,1,0:T(8,128)(2,1)}, f32[8,128]{1,0:T(8,128)S(1)}) custom-call(f32[8,128]{1,0:T(8,128)S(1)} %get-tuple-element.13.token_ref), custom_call_target="tpu_custom_call" | custom-call | flops 9126805504 | bytes 31457280 | tf_op jit(solution)/shard_map/pallas_call | solution.py:367
  10.4 43.4 %shard_map.19 = (bf16[2,4,16,256,128]{4,3,2,1,0:T(8,128)(2,1)S(1)}, bf16[4,16,256,128]{3,2,1,0:T(8,128)(2,1)S(1)}, bf16[11,4,256,1024]{3,2,1,0:T(8,128)(2,1)S(1)}) custom-call(bf16[16,2,256,128]{3,2,1,0:T(8,128)(2,1)} %bitcast.3, bf16[2,4,16,256,128]{4,3,2,1,0:T(8,128)(2,1)S(1)} %get-tuple-element.12.sc_in, ...), custom_call_target="tpu_custom_call", output_to_operand_aliasing={{0}: (1, {})} | custom-call | flops 9126805504 | bytes 2097152 | tf_op jit(solution)/shard_map/pallas_call | solution.py:376
  53.8 11.6 %shard_map.20 = bf16[16,2,256,4096]{3,2,1,0:T(8,128)(2,1)} custom-call(bf16[2,4,16,256,128]{4,3,2,1,0:T(8,128)(2,1)S(1)} %get-tuple-element.15.sc_ref, bf16[4,16,256,128]{3,2,1,0:T(8,128)(2,1)S(1)} %get-tuple-element.16.o_ref, bf16[11,4,256,1024]{3,2,1,0:T(8,128)(2,1)S(1)} %get-tuple-element.17.t_ref, ...), custom_call_target="tpu_custom_call", output_to_operand_aliasing={{}: (3, {})} | custom-call | flops 9126805504 | bytes 35651584 | tf_op jit(solution)/shard_map/pallas_call | solution.py:391
  (1 shorter events, 0.0 us)

commit v8 on v7

--- a/solution.py
+++ b/solution.py
@@ -133,13 +133,22 @@
 
     def relay_copy(n):
         if n < NC:
-            return remote(sc_ref.at[0, 2, chunk(n)], sc_ref.at[0, 3, chunk(n)], r_send.at[n], r_recv.at[n], partner)
+            return s_relay(n)
         part = pl.ds(*O_PARTS[n - NC])
         return remote(o_ref.at[2, part], o_ref.at[3, part], r_send.at[n], r_recv.at[n], partner)
 
     def y_copy(s, c):
         return remote(sc_ref.at[0, 2, chunk(c)], sc_ref.at[1, 2 + s, chunk(c)], y_send.at[c], y_recv.at[s, c], y_late)
 
+    def s_relay(c):
+        return remote(sc_ref.at[0, 2, chunk(c)], sc_ref.at[0, 3, chunk(c)], r_send.at[c], r_recv.at[c], partner)
+
+    def s_copy(c):
+        return remote(a_ref.at[chunk(c), x], sc_ref.at[0, 1, chunk(c)], d_send.at[c], d_recv.at[c], partner)
+
+    def yb_relay(c):
+        return remote(yb.at[chunk(c)], sc_ref.at[1, 0, chunk(c)], b_send.at[1 + c], b_recv.at[1 + c], partner)
+
     def yr_copy(c):
         return remote(sc_ref.at[0, 2, chunk(c)], yr.at[chunk(c)], q_send.at[c], q_recv.at[c], y_early)
 
@@ -147,11 +156,9 @@
         return remote(yr.at[chunk(c)], sc_ref.at[1, 2, chunk(c)], y_send.at[c], y_recv.at[0, c], partner)
 
     yb_copy = remote(a_ref.at[:, x], yb, b_send.at[0], b_recv.at[0], y_early)
-    yb_relay = remote(yb, sc_ref.at[1, 0], b_send.at[1], b_recv.at[1], partner)
     x_tail = remote(a_ref.at[tx, 1 - x], sc_ref.at[0, 2, tx], v_send, v_recv, x_peer)
     u_copy = remote(a_ref.at[ty, x], sc_ref.at[1, 1, ty], u_send, u_recv, y_late)
-    d_copies = [remote(a_ref.at[:, x], sc_ref.at[0, 1], d_send.at[0], d_recv.at[0], partner),
-                remote(a_ref.at[:, 1 - x], o_ref.at[1], d_send.at[1], d_recv.at[1], partner)]
+    o_copy = remote(a_ref.at[:, 1 - x], o_ref.at[1], d_send.at[NC], d_recv.at[NC], partner)
     l_copies = [pltpu.make_async_copy(a_ref.at[:, x], sc_ref.at[0, 0], lsem.at[0]),
                 pltpu.make_async_copy(a_ref.at[:, 1 - x], o_ref.at[0], lsem.at[1])]
     for cp in l_copies:
@@ -169,18 +176,21 @@
             x_copy(c).wait_recv()
             yr_copy(c).start()
         pl.semaphore_wait(join, 2)
-        d_copies[0].start()
         for c in range(NC):
             if c >= NR:
                 x_copy(c).wait_recv()
-                y_copy(0, c).start()
+            s_copy(c).start()
             relay_copy(c).start()
-        yb_copy.wait_recv()
-        yb_relay.start()
-        for c in range(NR):
-            yr_copy(c).wait_recv()
-            yr_relay(c).start()
-        d_copies[1].start()
+            if c == 0:
+                yb_copy.wait_recv()
+                yb_relay(c).start()
+        for c in range(NC):
+            if c < NR:
+                yr_copy(c).wait_recv()
+                yr_relay(c).start()
+            if c + 1 < NC:
+                yb_relay(c + 1).start()
+        o_copy.start()
 
     @pl.when(late)
     def _():
@@ -193,29 +203,40 @@
         for c in range(NC - 1):
             y_copy(1, c).start()
         u_copy.start()
-        for c in range(NC - 1):
-            relay_copy(c).start()
-        for cp in d_copies:
-            cp.start()
+        for c in range(NC):
+            s_copy(c).start()
+            if c < NC - 1:
+                relay_copy(c).start()
+        o_copy.start()
         x_tail.wait_recv()
         relay_copy(NC - 1).start()
         y_copy(1, NC - 1).start()
 
+    def rows_ready(i):
+        s_copy(i).wait_recv()
+        s_relay(i).wait_recv()
+
+    def o_step(n):
+        x_copy(NC + n).wait_recv()
+        relay_copy(NC + n).start()
+
     l_copies[0].wait()
-    d_copies[0].wait_recv()
-    for c in range(NC):
-        relay_copy(c).wait_recv()
-
+    rows_ready(0)
     row_blk = 2 * x + y
     for c in range(NC):
-        for n in ([c] if c < NC - 1 else range(c, len(O_PARTS))):
-            x_copy(NC + n).wait_recv()
-            relay_copy(NC + n).start()
+        if c < NC - 1:
+            o_step(c)
+        else:
+            o_step(len(O_PARTS) - 1)
+
+        @pl.when(early)
+        def _():
+            if c < NC - NR:
+                y_copy(0, NR + c).start()
 
         @pl.when(late)
         def _():
-            if c == 0:
-                yb_relay.wait_recv()
+            yb_relay(c).wait_recv()
             if c == NC - 1:
                 u_copy.wait_recv()
             for s in range(2):
@@ -226,13 +247,17 @@
             diag_tile(t_ref.at[base], sc_ref, (0,), sc_ref, (side,), c, row_blk, col)
 
             def body(i, _):
+                if c == 0:
+                    rows_ready(i)
                 full_tile(t_ref.at[base + i - c], sc_ref, (0,), i, sc_ref, (side,), c)
                 return 0
             lax.fori_loop(c + 1, NC, body, 0)
         if c == 1:
             l_copies[1].wait()
-            d_copies[1].wait_recv()
+            o_copy.wait_recv()
             relay_copy(NC).wait_recv()
+        if c == 2:
+            o_step(c + 1)
         if c in (1, 2):
             i, j = EXTRA[c - 1]
             full_tile(t_ref.at[len(NOW) + c - 1], o_ref, (), i, sc_ref, (side,), j)
@@ -243,10 +268,10 @@
         relay_copy(n).wait_send()
     for n in range(NC, NX):
         x_copy(n).wait_send()
-    for cp in d_copies:
-        cp.wait_send()
     for c in range(NC):
+        s_copy(c).wait_send()
         y_copy(0, c).wait_send()
+    o_copy.wait_send()
 
     @pl.when(late)
     def _():
@@ -260,7 +285,8 @@
         for c in range(NR):
             yr_copy(c).wait_send()
         yb_copy.wait_send()
-        yb_relay.wait_send()
+        for c in range(NC):
+            yb_relay(c).wait_send()
 
 
 def lookup(n, values):
@@ -383,8 +409,8 @@
             input_output_aliases={1: 0},
             scratch_shapes=[pltpu.VMEM((NM, BLOCK, PIECE), jnp.bfloat16), pltpu.VMEM((NR * CH, BLOCK, PIECE), jnp.bfloat16),
                             pltpu.SemaphoreType.REGULAR,
-                            dma((2,)), dma((2,)), dma((2,)), dma((NX,)), dma((NX,)), dma((NX,)), dma((NX,)),
-                            dma((NC,)), dma((2, NC)), dma((2,)), dma((2,)), dma((NR,)), dma((NR,))] + [dma(())] * 4,
+                            dma((2,)), dma((NC + 1,)), dma((NC + 1,)), dma((NX,)), dma((NX,)), dma((NX,)), dma((NX,)),
+                            dma((NC,)), dma((2, NC)), dma((NC + 1,)), dma((NC + 1,)), dma((NR,)), dma((NR,))] + [dma(())] * 4,
             compiler_params=pltpu.CompilerParams(collective_id=1, has_side_effects=True, vmem_limit_bytes=8 * 1024 * 1024),
             cost_estimate=pl.CostEstimate(flops=half_flops, bytes_accessed=2 << 20, transcendentals=0),
         )(a4, sc, zeroed)

time: 65.5 us -> 65.5 us (level)
  no operation moved by 1% of the time
where the time goes in v8:
time: 65.5 us; the launch traced here: 65.4 us
  Pallas kernels  65.4 us (100%)
    pallas_call x1, Pallas kernels, local_fn(): pl.pallas_call(gather_kernel, out_shape=[panels, pltpu.VMEM((PIECES, NM,...  43.5 us
    pallas_call x1, Pallas kernels, local_fn(): pl.pallas_call(write_kernel, out_shape=jax.ShapeDtypeStruct((NM, 2, BLOCK...  11.6 us
    pallas_call x1, Pallas kernels, local_fn(): pl.pallas_call(zero_kernel, out_shape=[jax.ShapeDtypeStruct((NM, 2, BLOCK...  10.3 us

profile of v8, /device:TPU:0, one launch (start us, length us, event | category | flops | bytes accessed | tf_op | source)
XLA Modules:
  0.0 65.4 jit_solution(3169475940007448924)
XLA Ops:
  0.0 10.3 %shard_map.18 = (bf16[16,2,256,4096]{3,2,1,0:T(8,128)(2,1)}, f32[8,128]{1,0:T(8,128)S(1)}) custom-call(f32[8,128]{1,0:T(8,128)S(1)} %get-tuple-element.13.token_ref), custom_call_target="tpu_custom_call" | custom-call | flops 9126805504 | bytes 31457280 | tf_op jit(solution)/shard_map/pallas_call | solution.py:393
  10.4 43.5 %shard_map.19 = (bf16[2,4,16,256,128]{4,3,2,1,0:T(8,128)(2,1)S(1)}, bf16[4,16,256,128]{3,2,1,0:T(8,128)(2,1)S(1)}, bf16[11,4,256,1024]{3,2,1,0:T(8,128)(2,1)S(1)}) custom-call(bf16[16,2,256,128]{3,2,1,0:T(8,128)(2,1)} %bitcast.3, bf16[2,4,16,256,128]{4,3,2,1,0:T(8,128)(2,1)S(1)} %get-tuple-element.12.sc_in, ...), custom_call_target="tpu_custom_call", output_to_operand_aliasing={{0}: (1, {})} | custom-call | flops 9126805504 | bytes 2097152 | tf_op jit(solution)/shard_map/pallas_call | solution.py:402
  53.9 11.6 %shard_map.20 = bf16[16,2,256,4096]{3,2,1,0:T(8,128)(2,1)} custom-call(bf16[2,4,16,256,128]{4,3,2,1,0:T(8,128)(2,1)S(1)} %get-tuple-element.15.sc_ref, bf16[4,16,256,128]{3,2,1,0:T(8,128)(2,1)S(1)} %get-tuple-element.16.o_ref, bf16[11,4,256,1024]{3,2,1,0:T(8,128)(2,1)S(1)} %get-tuple-element.17.t_ref, ...), custom_call_target="tpu_custom_call", output_to_operand_aliasing={{}: (3, {})} | custom-call | flops 9126805504 | bytes 35651584 | tf_op jit(solution)/shard_map/pallas_call | solution.py:417
  (1 shorter events, 0.0 us)

commit v9 on v8

--- a/solution.py
+++ b/solution.py
@@ -127,7 +127,8 @@
 
     def x_copy(n):
         if n < NC:
-            return remote(a_ref.at[chunk(n), 1 - x], sc_ref.at[0, 2, chunk(n)], x_send.at[n], x_recv.at[n], x_peer)
+            part = pl.ds(n * NM // 2, NM // 2)
+            return remote(a_ref.at[part, 1 - x], sc_ref.at[0, 2, part], x_send.at[n], x_recv.at[n], x_peer)
         part = pl.ds(*O_PARTS[n - NC])
         return remote(a_ref.at[part, x], o_ref.at[2, part], x_send.at[n], x_recv.at[n], x_peer)
 
@@ -149,12 +150,11 @@
     def yb_relay(c):
         return remote(yb.at[chunk(c)], sc_ref.at[1, 0, chunk(c)], b_send.at[1 + c], b_recv.at[1 + c], partner)
 
-    def yr_copy(c):
-        return remote(sc_ref.at[0, 2, chunk(c)], yr.at[chunk(c)], q_send.at[c], q_recv.at[c], y_early)
-
     def yr_relay(c):
         return remote(yr.at[chunk(c)], sc_ref.at[1, 2, chunk(c)], y_send.at[c], y_recv.at[0, c], partner)
 
+    yr_part = pl.ds(0, NR * CH)
+    yr_copy = remote(sc_ref.at[0, 2, yr_part], yr, q_send, q_recv, y_early)
     yb_copy = remote(a_ref.at[:, x], yb, b_send.at[0], b_recv.at[0], y_early)
     x_tail = remote(a_ref.at[tx, 1 - x], sc_ref.at[0, 2, tx], v_send, v_recv, x_peer)
     u_copy = remote(a_ref.at[ty, x], sc_ref.at[1, 1, ty], u_send, u_recv, y_late)
@@ -169,24 +169,24 @@
     def _():
         signal(barrier, (x_peer, y_early, partner, y_late))
         pl.semaphore_wait(barrier, 2)
-        for n in range(NX):
+        for n in (0, 1, *range(NC, NX)):
             x_copy(n).start()
         yb_copy.start()
-        for c in range(NR):
-            x_copy(c).wait_recv()
-            yr_copy(c).start()
+        x_copy(0).wait_recv()
+        yr_copy.start()
         pl.semaphore_wait(join, 2)
         for c in range(NC):
-            if c >= NR:
-                x_copy(c).wait_recv()
+            if c == NR:
+                x_copy(1).wait_recv()
             s_copy(c).start()
             relay_copy(c).start()
             if c == 0:
                 yb_copy.wait_recv()
                 yb_relay(c).start()
         for c in range(NC):
+            if c == 0:
+                yr_copy.wait_recv()
             if c < NR:
-                yr_copy(c).wait_recv()
                 yr_relay(c).start()
             if c + 1 < NC:
                 yb_relay(c + 1).start()
@@ -280,10 +280,9 @@
 
     @pl.when(early)
     def _():
-        for n in range(NC):
+        for n in range(2):
             x_copy(n).wait_send()
-        for c in range(NR):
-            yr_copy(c).wait_send()
+        yr_copy.wait_send()
         yb_copy.wait_send()
         for c in range(NC):
             yb_relay(c).wait_send()
@@ -410,7 +409,7 @@
             scratch_shapes=[pltpu.VMEM((NM, BLOCK, PIECE), jnp.bfloat16), pltpu.VMEM((NR * CH, BLOCK, PIECE), jnp.bfloat16),
                             pltpu.SemaphoreType.REGULAR,
                             dma((2,)), dma((NC + 1,)), dma((NC + 1,)), dma((NX,)), dma((NX,)), dma((NX,)), dma((NX,)),
-                            dma((NC,)), dma((2, NC)), dma((NC + 1,)), dma((NC + 1,)), dma((NR,)), dma((NR,))] + [dma(())] * 4,
+                            dma((NC,)), dma((2, NC)), dma((NC + 1,)), dma((NC + 1,)), dma(()), dma(())] + [dma(())] * 4,
             compiler_params=pltpu.CompilerParams(collective_id=1, has_side_effects=True, vmem_limit_bytes=8 * 1024 * 1024),
             cost_estimate=pl.CostEstimate(flops=half_flops, bytes_accessed=2 << 20, transcendentals=0),
         )(a4, sc, zeroed)

time: 65.5 us -> 65.5 us (level)
  no operation moved by 1% of the time
where the time goes in v9:
time: 65.5 us; the launch traced here: 65.4 us
  Pallas kernels  65.4 us (100%)
    pallas_call x1, Pallas kernels, local_fn(): pl.pallas_call(gather_kernel, out_shape=[panels, pltpu.VMEM((PIECES, NM,...  43.5 us
    pallas_call x1, Pallas kernels, local_fn(): pl.pallas_call(write_kernel, out_shape=jax.ShapeDtypeStruct((NM, 2, BLOCK...  11.6 us
    pallas_call x1, Pallas kernels, local_fn(): pl.pallas_call(zero_kernel, out_shape=[jax.ShapeDtypeStruct((NM, 2, BLOCK...  10.3 us

profile of v9, /device:TPU:0, one launch (start us, length us, event | category | flops | bytes accessed | tf_op | source)
XLA Modules:
  0.0 65.4 jit_solution(15381082710181447903)
XLA Ops:
  0.0 10.3 %shard_map.18 = (bf16[16,2,256,4096]{3,2,1,0:T(8,128)(2,1)}, f32[8,128]{1,0:T(8,128)S(1)}) custom-call(f32[8,128]{1,0:T(8,128)S(1)} %get-tuple-element.13.token_ref), custom_call_target="tpu_custom_call" | custom-call | flops 9126805504 | bytes 31457280 | tf_op jit(solution)/shard_map/pallas_call | solution.py:392
  10.4 43.5 %shard_map.19 = (bf16[2,4,16,256,128]{4,3,2,1,0:T(8,128)(2,1)S(1)}, bf16[4,16,256,128]{3,2,1,0:T(8,128)(2,1)S(1)}, bf16[11,4,256,1024]{3,2,1,0:T(8,128)(2,1)S(1)}) custom-call(bf16[16,2,256,128]{3,2,1,0:T(8,128)(2,1)} %bitcast.3, bf16[2,4,16,256,128]{4,3,2,1,0:T(8,128)(2,1)S(1)} %get-tuple-element.12.sc_in, ...), custom_call_target="tpu_custom_call", output_to_operand_aliasing={{0}: (1, {})} | custom-call | flops 9126805504 | bytes 2097152 | tf_op jit(solution)/shard_map/pallas_call | solution.py:401
  53.9 11.6 %shard_map.20 = bf16[16,2,256,4096]{3,2,1,0:T(8,128)(2,1)} custom-call(bf16[2,4,16,256,128]{4,3,2,1,0:T(8,128)(2,1)S(1)} %get-tuple-element.15.sc_ref, bf16[4,16,256,128]{3,2,1,0:T(8,128)(2,1)S(1)} %get-tuple-element.16.o_ref, bf16[11,4,256,1024]{3,2,1,0:T(8,128)(2,1)S(1)} %get-tuple-element.17.t_ref, ...), custom_call_target="tpu_custom_call", output_to_operand_aliasing={{}: (3, {})} | custom-call | flops 9126805504 | bytes 35651584 | tf_op jit(solution)/shard_map/pallas_call | solution.py:416
  (1 shorter events, 0.0 us)

commit v10 on v9

--- a/solution.py
+++ b/solution.py
@@ -19,7 +19,7 @@
 JOBS = [(i, j) for j in range(NC) for i in range(j, NC)]
 LAST = (NC - 1, NC - 1)
 NOW = [job for job in JOBS if job != LAST]
-NAX, NAY = 15, 14
+NAX, NAY = 15, 15
 NR = 2
 O_PARTS = ((12, 4), (0, 4), (4, 4), (8, 3), (11, 1))
 NX = NC + len(O_PARTS)
@@ -95,7 +95,12 @@
         yc.wait()
 
 
-def zero_kernel(token_ref, c_ref, done_ref, zbuf, sem):
+def zero_kernel(token_ref, a_ref, sc_in, c_ref, done_ref, sc_ref, o_ref, zbuf, sem, lsem):
+    _, x, _, _ = positions()
+    loads = [pltpu.make_async_copy(a_ref.at[:, 1 - x], o_ref.at[0], lsem),
+             pltpu.make_async_copy(a_ref.at[:, x], sc_ref.at[0, 0], lsem)]
+    for cp in loads:
+        cp.start()
     zbuf[...] = jnp.zeros_like(zbuf)
     done_ref[...] = jnp.zeros_like(done_ref)
     copies = []
@@ -109,11 +114,11 @@
                     c_ref.at[pl.ds(i * CH, q), s, :, pl.ds((i * CH + q) * BLOCK, BLOCK)], sem))
     for cp in copies:
         cp.start()
-    for cp in copies:
+    for cp in copies + loads:
         cp.wait()
 
 
-def gather_kernel(a_ref, sc_in, token_ref, sc_ref, o_ref, t_ref, yb, yr, join, lsem, d_send, d_recv, x_send, x_recv, r_send, r_recv,
+def gather_kernel(sc_in, o_in, token_ref, sc_ref, o_ref, t_ref, yb, yr, join, d_send, d_recv, x_send, x_recv, r_send, r_recv,
                   y_send, y_recv, b_send, b_recv, q_send, q_recv, u_send, u_recv, v_send, v_recv):
     y, x, k, col = positions()
     late = k != y
@@ -128,9 +133,9 @@
     def x_copy(n):
         if n < NC:
             part = pl.ds(n * NM // 2, NM // 2)
-            return remote(a_ref.at[part, 1 - x], sc_ref.at[0, 2, part], x_send.at[n], x_recv.at[n], x_peer)
+            return remote(o_ref.at[0, part], sc_ref.at[0, 2, part], x_send.at[n], x_recv.at[n], x_peer)
         part = pl.ds(*O_PARTS[n - NC])
-        return remote(a_ref.at[part, x], o_ref.at[2, part], x_send.at[n], x_recv.at[n], x_peer)
+        return remote(sc_ref.at[0, 0, part], o_ref.at[2, part], x_send.at[n], x_recv.at[n], x_peer)
 
     def relay_copy(n):
         if n < NC:
@@ -145,7 +150,7 @@
         return remote(sc_ref.at[0, 2, chunk(c)], sc_ref.at[0, 3, chunk(c)], r_send.at[c], r_recv.at[c], partner)
 
     def s_copy(c):
-        return remote(a_ref.at[chunk(c), x], sc_ref.at[0, 1, chunk(c)], d_send.at[c], d_recv.at[c], partner)
+        return remote(sc_ref.at[0, 0, chunk(c)], sc_ref.at[0, 1, chunk(c)], d_send.at[c], d_recv.at[c], partner)
 
     def yb_relay(c):
         return remote(yb.at[chunk(c)], sc_ref.at[1, 0, chunk(c)], b_send.at[1 + c], b_recv.at[1 + c], partner)
@@ -155,14 +160,10 @@
 
     yr_part = pl.ds(0, NR * CH)
     yr_copy = remote(sc_ref.at[0, 2, yr_part], yr, q_send, q_recv, y_early)
-    yb_copy = remote(a_ref.at[:, x], yb, b_send.at[0], b_recv.at[0], y_early)
-    x_tail = remote(a_ref.at[tx, 1 - x], sc_ref.at[0, 2, tx], v_send, v_recv, x_peer)
-    u_copy = remote(a_ref.at[ty, x], sc_ref.at[1, 1, ty], u_send, u_recv, y_late)
-    o_copy = remote(a_ref.at[:, 1 - x], o_ref.at[1], d_send.at[NC], d_recv.at[NC], partner)
-    l_copies = [pltpu.make_async_copy(a_ref.at[:, x], sc_ref.at[0, 0], lsem.at[0]),
-                pltpu.make_async_copy(a_ref.at[:, 1 - x], o_ref.at[0], lsem.at[1])]
-    for cp in l_copies:
-        cp.start()
+    yb_copy = remote(sc_ref.at[0, 0], yb, b_send.at[0], b_recv.at[0], y_early)
+    x_tail = remote(o_ref.at[0, tx], sc_ref.at[0, 2, tx], v_send, v_recv, x_peer)
+    u_copy = remote(sc_ref.at[0, 0, ty], sc_ref.at[1, 1, ty], u_send, u_recv, y_late)
+    o_copy = remote(o_ref.at[0], o_ref.at[1], d_send.at[NC], d_recv.at[NC], partner)
     barrier = pltpu.get_barrier_semaphore()
 
     @pl.when(early)
@@ -220,7 +221,6 @@
         x_copy(NC + n).wait_recv()
         relay_copy(NC + n).start()
 
-    l_copies[0].wait()
     rows_ready(0)
     row_blk = 2 * x + y
     for c in range(NC):
@@ -253,7 +253,6 @@
                 return 0
             lax.fori_loop(c + 1, NC, body, 0)
         if c == 1:
-            l_copies[1].wait()
             o_copy.wait_recv()
             relay_copy(NC).wait_recv()
         if c == 2:
@@ -389,30 +388,31 @@
             scratch_shapes=[dma(())] * 4,
             compiler_params=pltpu.CompilerParams(collective_id=0, has_side_effects=True, vmem_limit_bytes=2 * 1024 * 1024),
         )(a4)
-        c, zeroed = pl.pallas_call(
+        rest = pltpu.VMEM((PIECES, NM, BLOCK, PIECE), jnp.bfloat16)
+        c, zeroed, sc, o = pl.pallas_call(
             zero_kernel,
-            out_shape=[jax.ShapeDtypeStruct((NM, 2, BLOCK, NM * BLOCK), jnp.bfloat16), token],
-            in_specs=[any_spec],
-            out_specs=[any_spec, vmem],
-            scratch_shapes=[pltpu.VMEM((CH, BLOCK, TILE), jnp.bfloat16), dma(())],
+            out_shape=[jax.ShapeDtypeStruct((NM, 2, BLOCK, NM * BLOCK), jnp.bfloat16), token, panels, rest],
+            in_specs=[any_spec, hbm, vmem],
+            out_specs=[any_spec, vmem, vmem, vmem],
+            input_output_aliases={2: 2},
+            scratch_shapes=[pltpu.VMEM((CH, BLOCK, TILE), jnp.bfloat16), dma(()), dma(())],
             compiler_params=pltpu.CompilerParams(vmem_limit_bytes=4 * 1024 * 1024),
             cost_estimate=pl.CostEstimate(flops=half_flops, bytes_accessed=30 << 20, transcendentals=0),
-        )(first)
+        )(first, a4, sc)
         sc, o, t = pl.pallas_call(
             gather_kernel,
-            out_shape=[panels,
-                       pltpu.VMEM((PIECES, NM, BLOCK, PIECE), jnp.bfloat16),
+            out_shape=[panels, rest,
                        pltpu.VMEM((len(PANELS), CH, BLOCK, TILE), jnp.bfloat16)],
-            in_specs=[hbm, vmem, any_spec],
+            in_specs=[vmem, vmem, any_spec],
             out_specs=[vmem] * 3,
-            input_output_aliases={1: 0},
+            input_output_aliases={0: 0, 1: 1},
             scratch_shapes=[pltpu.VMEM((NM, BLOCK, PIECE), jnp.bfloat16), pltpu.VMEM((NR * CH, BLOCK, PIECE), jnp.bfloat16),
                             pltpu.SemaphoreType.REGULAR,
-                            dma((2,)), dma((NC + 1,)), dma((NC + 1,)), dma((NX,)), dma((NX,)), dma((NX,)), dma((NX,)),
+                            dma((NC + 1,)), dma((NC + 1,)), dma((NX,)), dma((NX,)), dma((NX,)), dma((NX,)),
                             dma((NC,)), dma((2, NC)), dma((NC + 1,)), dma((NC + 1,)), dma(()), dma(())] + [dma(())] * 4,
             compiler_params=pltpu.CompilerParams(collective_id=1, has_side_effects=True, vmem_limit_bytes=8 * 1024 * 1024),
             cost_estimate=pl.CostEstimate(flops=half_flops, bytes_accessed=2 << 20, transcendentals=0),
-        )(a4, sc, zeroed)
+        )(sc, o, zeroed)
         c = pl.pallas_call(
             write_kernel,
             out_shape=jax.ShapeDtypeStruct((NM, 2, BLOCK, NM * BLOCK), jnp.bfloat16),

time: 65.5 us -> 65.5 us (level)
  no operation moved by 1% of the time
where the time goes in v10:
time: 65.5 us; the launch traced here: 65.4 us
  Pallas kernels  65.4 us (100%)
    pallas_call x1, Pallas kernels, local_fn(): pl.pallas_call(gather_kernel, out_shape=[panels, rest, pltpu.VMEM((len(PA...  43.3 us
    pallas_call x1, Pallas kernels, local_fn(): pl.pallas_call(write_kernel, out_shape=jax.ShapeDtypeStruct((NM, 2, BLOCK...  11.6 us
    pallas_call x1, Pallas kernels, local_fn(): pl.pallas_call(zero_kernel, out_shape=[jax.ShapeDtypeStruct((NM, 2, BLOCK...  10.5 us

profile of v10, /device:TPU:0, one launch (start us, length us, event | category | flops | bytes accessed | tf_op | source)
XLA Modules:
  0.0 65.4 jit_solution(13539058493770578530)
XLA Ops:
  0.0 10.5 %shard_map.18 = (bf16[16,2,256,4096]{3,2,1,0:T(8,128)(2,1)}, f32[8,128]{1,0:T(8,128)S(1)}, bf16[2,4,16,256,128]{4,3,2,1,0:T(8,128)(2,1)S(1)}, bf16[4,16,256,128]{3,2,1,0:T(8,128)(2,1)S(1)}) custom-call(f32[8,128]{1,0:T(8,128)S(1)} %get-tuple-element.14.token_ref, bf16[16,2,256,128]{3,2,1,0:T(8,128)(2,1)} %bitcast.3, ...), custom_call_target="tpu_custom_call", output_to_operand_aliasing={{2}: (2, {})} | custom-call | flops 9126805504 | bytes 31457280 | tf_op jit(solution)/shard_map/pallas_call | solution.py:392
  10.6 43.3 %shard_map.19 = (bf16[2,4,16,256,128]{4,3,2,1,0:T(8,128)(2,1)S(1)}, bf16[4,16,256,128]{3,2,1,0:T(8,128)(2,1)S(1)}, bf16[11,4,256,1024]{3,2,1,0:T(8,128)(2,1)S(1)}) custom-call(bf16[2,4,16,256,128]{4,3,2,1,0:T(8,128)(2,1)S(1)} %get-tuple-element.16.sc_in, ...), custom_call_target="tpu_custom_call", output_to_operand_aliasing={{0}: (0, {}), {1}: (1, {})} | custom-call | flops 9126805504 | bytes 2097152 | tf_op jit(solution)/shard_map/pallas_call | solution.py:402
  53.8 11.6 %shard_map.20 = bf16[16,2,256,4096]{3,2,1,0:T(8,128)(2,1)} custom-call(bf16[2,4,16,256,128]{4,3,2,1,0:T(8,128)(2,1)S(1)} %get-tuple-element.19.sc_ref, bf16[4,16,256,128]{3,2,1,0:T(8,128)(2,1)S(1)} %get-tuple-element.20.o_ref, bf16[11,4,256,1024]{3,2,1,0:T(8,128)(2,1)S(1)} %get-tuple-element.21.t_ref, ...), custom_call_target="tpu_custom_call", output_to_operand_aliasing={{}: (3, {})} | custom-call | flops 9126805504 | bytes 35651584 | tf_op jit(solution)/shard_map/pallas_call | solution.py:416
  (1 shorter events, 0.0 us)

commit v11 on v10

--- a/solution.py
+++ b/solution.py
@@ -231,8 +231,8 @@
 
         @pl.when(early)
         def _():
-            if c < NC - NR:
-                y_copy(0, NR + c).start()
+            if c in (0, 2):
+                y_copy(0, NR + c // 2).start()
 
         @pl.when(late)
         def _():
@@ -255,11 +255,10 @@
         if c == 1:
             o_copy.wait_recv()
             relay_copy(NC).wait_recv()
+            for m, (i, j) in enumerate(EXTRA):
+                full_tile(t_ref.at[len(NOW) + m], o_ref, (), i, sc_ref, (side,), j)
         if c == 2:
             o_step(c + 1)
-        if c in (1, 2):
-            i, j = EXTRA[c - 1]
-            full_tile(t_ref.at[len(NOW) + c - 1], o_ref, (), i, sc_ref, (side,), j)
 
     for n in range(1, len(O_PARTS)):
         relay_copy(NC + n).wait_recv()

time: 65.5 us -> 65.6 us (level)
  no operation moved by 1% of the time
where the time goes in v11:
time: 65.6 us; the launch traced here: 65.5 us
  Pallas kernels  65.4 us (100%)
    pallas_call x1, Pallas kernels, local_fn(): pl.pallas_call(gather_kernel, out_shape=[panels, rest, pltpu.VMEM((len(PA...  43.4 us
    pallas_call x1, Pallas kernels, local_fn(): pl.pallas_call(write_kernel, out_shape=jax.ShapeDtypeStruct((NM, 2, BLOCK...  11.6 us
    pallas_call x1, Pallas kernels, local_fn(): pl.pallas_call(zero_kernel, out_shape=[jax.ShapeDtypeStruct((NM, 2, BLOCK...  10.5 us

profile of v11, /device:TPU:0, one launch (start us, length us, event | category | flops | bytes accessed | tf_op | source)
XLA Modules:
  0.0 65.5 jit_solution(6989313124959110917)
XLA Ops:
  0.0 10.5 %shard_map.18 = (bf16[16,2,256,4096]{3,2,1,0:T(8,128)(2,1)}, f32[8,128]{1,0:T(8,128)S(1)}, bf16[2,4,16,256,128]{4,3,2,1,0:T(8,128)(2,1)S(1)}, bf16[4,16,256,128]{3,2,1,0:T(8,128)(2,1)S(1)}) custom-call(f32[8,128]{1,0:T(8,128)S(1)} %get-tuple-element.14.token_ref, bf16[16,2,256,128]{3,2,1,0:T(8,128)(2,1)} %bitcast.3, ...), custom_call_target="tpu_custom_call", output_to_operand_aliasing={{2}: (2, {})} | custom-call | flops 9126805504 | bytes 31457280 | tf_op jit(solution)/shard_map/pallas_call | solution.py:391
  10.6 43.4 %shard_map.19 = (bf16[2,4,16,256,128]{4,3,2,1,0:T(8,128)(2,1)S(1)}, bf16[4,16,256,128]{3,2,1,0:T(8,128)(2,1)S(1)}, bf16[11,4,256,1024]{3,2,1,0:T(8,128)(2,1)S(1)}) custom-call(bf16[2,4,16,256,128]{4,3,2,1,0:T(8,128)(2,1)S(1)} %get-tuple-element.16.sc_in, ...), custom_call_target="tpu_custom_call", output_to_operand_aliasing={{0}: (0, {}), {1}: (1, {})} | custom-call | flops 9126805504 | bytes 2097152 | tf_op jit(solution)/shard_map/pallas_call | solution.py:401
  53.9 11.6 %shard_map.20 = bf16[16,2,256,4096]{3,2,1,0:T(8,128)(2,1)} custom-call(bf16[2,4,16,256,128]{4,3,2,1,0:T(8,128)(2,1)S(1)} %get-tuple-element.19.sc_ref, bf16[4,16,256,128]{3,2,1,0:T(8,128)(2,1)S(1)} %get-tuple-element.20.o_ref, bf16[11,4,256,1024]{3,2,1,0:T(8,128)(2,1)S(1)} %get-tuple-element.21.t_ref, ...), custom_call_target="tpu_custom_call", output_to_operand_aliasing={{}: (3, {})} | custom-call | flops 9126805504 | bytes 35651584 | tf_op jit(solution)/shard_map/pallas_call | solution.py:415
  (1 shorter events, 0.0 us)

commit v12 on v11

--- a/solution.py
+++ b/solution.py
@@ -224,9 +224,7 @@
     rows_ready(0)
     row_blk = 2 * x + y
     for c in range(NC):
-        if c < NC - 1:
-            o_step(c)
-        else:
+        if c == NC - 1:
             o_step(len(O_PARTS) - 1)
 
         @pl.when(early)
@@ -252,6 +250,7 @@
                 full_tile(t_ref.at[base + i - c], sc_ref, (0,), i, sc_ref, (side,), c)
                 return 0
             lax.fori_loop(c + 1, NC, body, 0)
+            o_step(c)
         if c == 1:
             o_copy.wait_recv()
             relay_copy(NC).wait_recv()

time: 65.6 us -> 63.8 us (0.973)
  Pallas kernels: 65.4 us -> 63.7 us
    pallas_call x1, Pallas kernels: 43.4 us -> 41.6 us  [local_fn(): pl.pallas_call(gather_kernel, out_shape=[panels, rest, pltpu.VMEM((len(PA...]
where the time goes in v12:
time: 63.8 us; the launch traced here: 63.7 us
  Pallas kernels  63.7 us (100%)
    pallas_call x1, Pallas kernels, local_fn(): pl.pallas_call(gather_kernel, out_shape=[panels, rest, pltpu.VMEM((len(PA...  41.6 us
    pallas_call x1, Pallas kernels, local_fn(): pl.pallas_call(write_kernel, out_shape=jax.ShapeDtypeStruct((NM, 2, BLOCK...  11.6 us
    pallas_call x1, Pallas kernels, local_fn(): pl.pallas_call(zero_kernel, out_shape=[jax.ShapeDtypeStruct((NM, 2, BLOCK...  10.5 us

profile of v12, /device:TPU:0, one launch (start us, length us, event | category | flops | bytes accessed | tf_op | source)
XLA Modules:
  0.0 63.7 jit_solution(15014865912826917905)
XLA Ops:
  0.0 10.5 %shard_map.18 = (bf16[16,2,256,4096]{3,2,1,0:T(8,128)(2,1)}, f32[8,128]{1,0:T(8,128)S(1)}, bf16[2,4,16,256,128]{4,3,2,1,0:T(8,128)(2,1)S(1)}, bf16[4,16,256,128]{3,2,1,0:T(8,128)(2,1)S(1)}) custom-call(f32[8,128]{1,0:T(8,128)S(1)} %get-tuple-element.14.token_ref, bf16[16,2,256,128]{3,2,1,0:T(8,128)(2,1)} %bitcast.3, ...), custom_call_target="tpu_custom_call", output_to_operand_aliasing={{2}: (2, {})} | custom-call | flops 9126805504 | bytes 31457280 | tf_op jit(solution)/shard_map/pallas_call | solution.py:390
  10.6 41.6 %shard_map.19 = (bf16[2,4,16,256,128]{4,3,2,1,0:T(8,128)(2,1)S(1)}, bf16[4,16,256,128]{3,2,1,0:T(8,128)(2,1)S(1)}, bf16[11,4,256,1024]{3,2,1,0:T(8,128)(2,1)S(1)}) custom-call(bf16[2,4,16,256,128]{4,3,2,1,0:T(8,128)(2,1)S(1)} %get-tuple-element.16.sc_in, ...), custom_call_target="tpu_custom_call", output_to_operand_aliasing={{0}: (0, {}), {1}: (1, {})} | custom-call | flops 9126805504 | bytes 2097152 | tf_op jit(solution)/shard_map/pallas_call | solution.py:400
  52.1 11.6 %shard_map.20 = bf16[16,2,256,4096]{3,2,1,0:T(8,128)(2,1)} custom-call(bf16[2,4,16,256,128]{4,3,2,1,0:T(8,128)(2,1)S(1)} %get-tuple-element.19.sc_ref, bf16[4,16,256,128]{3,2,1,0:T(8,128)(2,1)S(1)} %get-tuple-element.20.o_ref, bf16[11,4,256,1024]{3,2,1,0:T(8,128)(2,1)S(1)} %get-tuple-element.21.t_ref, ...), custom_call_target="tpu_custom_call", output_to_operand_aliasing={{}: (3, {})} | custom-call | flops 9126805504 | bytes 35651584 | tf_op jit(solution)/shard_map/pallas_call | solution.py:414
  (1 shorter events, 0.0 us)

commit v13 on v12

--- a/solution.py
+++ b/solution.py
@@ -19,6 +19,7 @@
 JOBS = [(i, j) for j in range(NC) for i in range(j, NC)]
 LAST = (NC - 1, NC - 1)
 NOW = [job for job in JOBS if job != LAST]
+HEAD = 2
 NAX, NAY = 15, 15
 NR = 2
 O_PARTS = ((12, 4), (0, 4), (4, 4), (8, 3), (11, 1))
@@ -75,7 +76,7 @@
         pl.semaphore_signal(sem, inc=1, device_id=dev, device_id_type=MESH_ID)
 
 
-def first_kernel(a_ref, sc_ref, token_ref, x_send, x_recv, y_send, y_recv):
+def first_kernel(a_ref, sc_ref, token_ref, head, lsem, x_send, x_recv, y_send, y_recv):
     y, x, k, _ = positions()
     token_ref[...] = jnp.zeros_like(token_ref)
 
@@ -83,16 +84,25 @@
     def _():
         x_peer = (0, y, 2 * (1 - x) + k)
         y_peer = (0, 1 - y, 2 * x + y)
+        first = pl.ds(0, HEAD)
+        loads = [pltpu.make_async_copy(a_ref.at[first, 1 - x], head.at[0], lsem.at[0]),
+                 pltpu.make_async_copy(a_ref.at[first, x], head.at[1], lsem.at[1])]
+        for cp in loads:
+            cp.start()
         barrier = pltpu.get_barrier_semaphore()
         signal(barrier, (x_peer, y_peer))
         pl.semaphore_wait(barrier, 2)
-        px, py = pl.ds(0, NAX), pl.ds(0, NAY)
-        xc = remote(a_ref.at[px, 1 - x], sc_ref.at[0, 2, px], x_send, x_recv, x_peer)
-        yc = remote(a_ref.at[py, x], sc_ref.at[1, 1, py], y_send, y_recv, y_peer)
-        xc.start()
-        yc.start()
-        xc.wait()
-        yc.wait()
+        px, py = pl.ds(HEAD, NAX - HEAD), pl.ds(HEAD, NAY - HEAD)
+        sends = [remote(head.at[0], sc_ref.at[0, 2, first], x_send.at[0], x_recv.at[0], x_peer),
+                 remote(head.at[1], sc_ref.at[1, 1, first], y_send.at[0], y_recv.at[0], y_peer),
+                 remote(a_ref.at[px, 1 - x], sc_ref.at[0, 2, px], x_send.at[1], x_recv.at[1], x_peer),
+                 remote(a_ref.at[py, x], sc_ref.at[1, 1, py], y_send.at[1], y_recv.at[1], y_peer)]
+        for cp in loads:
+            cp.wait()
+        for cp in sends:
+            cp.start()
+        for cp in sends:
+            cp.wait()
 
 
 def zero_kernel(token_ref, a_ref, sc_in, c_ref, done_ref, sc_ref, o_ref, zbuf, sem, lsem):
@@ -383,7 +393,7 @@
             out_shape=[panels, token],
             in_specs=[hbm],
             out_specs=[vmem, vmem],
-            scratch_shapes=[dma(())] * 4,
+            scratch_shapes=[pltpu.VMEM((2, HEAD, BLOCK, PIECE), jnp.bfloat16)] + [dma((2,))] * 5,
             compiler_params=pltpu.CompilerParams(collective_id=0, has_side_effects=True, vmem_limit_bytes=2 * 1024 * 1024),
         )(a4)
         rest = pltpu.VMEM((PIECES, NM, BLOCK, PIECE), jnp.bfloat16)

time: 63.8 us -> 63.8 us (level)
  no operation moved by 1% of the time
where the time goes in v13:
time: 63.8 us; the launch traced here: 63.7 us
  Pallas kernels  63.7 us (100%)
    pallas_call x1, Pallas kernels, local_fn(): pl.pallas_call(gather_kernel, out_shape=[panels, rest, pltpu.VMEM((len(PA...  41.6 us
    pallas_call x1, Pallas kernels, local_fn(): pl.pallas_call(write_kernel, out_shape=jax.ShapeDtypeStruct((NM, 2, BLOCK...  11.6 us
    pallas_call x1, Pallas kernels, local_fn(): pl.pallas_call(zero_kernel, out_shape=[jax.ShapeDtypeStruct((NM, 2, BLOCK...  10.5 us

profile of v13, /device:TPU:0, one launch (start us, length us, event | category | flops | bytes accessed | tf_op | source)
XLA Modules:
  0.0 63.7 jit_solution(15131135588877546126)
XLA Ops:
  0.0 0.1 shard_map.17
  0.1 10.5 %shard_map.18 = (bf16[16,2,256,4096]{3,2,1,0:T(8,128)(2,1)}, f32[8,128]{1,0:T(8,128)S(1)}, bf16[2,4,16,256,128]{4,3,2,1,0:T(8,128)(2,1)S(1)}, bf16[4,16,256,128]{3,2,1,0:T(8,128)(2,1)S(1)}) custom-call(f32[8,128]{1,0:T(8,128)S(1)} %get-tuple-element.14.token_ref, bf16[16,2,256,128]{3,2,1,0:T(8,128)(2,1)} %bitcast.3, ...), custom_call_target="tpu_custom_call", output_to_operand_aliasing={{2}: (2, {})} | custom-call | flops 9126805504 | bytes 31457280 | tf_op jit(solution)/shard_map/pallas_call | solution.py:400
  10.6 41.6 %shard_map.19 = (bf16[2,4,16,256,128]{4,3,2,1,0:T(8,128)(2,1)S(1)}, bf16[4,16,256,128]{3,2,1,0:T(8,128)(2,1)S(1)}, bf16[11,4,256,1024]{3,2,1,0:T(8,128)(2,1)S(1)}) custom-call(bf16[2,4,16,256,128]{4,3,2,1,0:T(8,128)(2,1)S(1)} %get-tuple-element.16.sc_in, ...), custom_call_target="tpu_custom_call", output_to_operand_aliasing={{0}: (0, {}), {1}: (1, {})} | custom-call | flops 9126805504 | bytes 2097152 | tf_op jit(solution)/shard_map/pallas_call | solution.py:410
  52.2 11.6 %shard_map.20 = bf16[16,2,256,4096]{3,2,1,0:T(8,128)(2,1)} custom-call(bf16[2,4,16,256,128]{4,3,2,1,0:T(8,128)(2,1)S(1)} %get-tuple-element.19.sc_ref, bf16[4,16,256,128]{3,2,1,0:T(8,128)(2,1)S(1)} %get-tuple-element.20.o_ref, bf16[11,4,256,1024]{3,2,1,0:T(8,128)(2,1)S(1)} %get-tuple-element.21.t_ref, ...), custom_call_target="tpu_custom_call", output_to_operand_aliasing={{}: (3, {})} | custom-call | flops 9126805504 | bytes 35651584 | tf_op jit(solution)/shard_map/pallas_call | solution.py:424

commit v14 on v12

--- a/solution.py
+++ b/solution.py
@@ -14,7 +14,7 @@
 CH = 4
 NC = NM // CH
 NBUF = 5
-LEAD = 4
+LEAD = 5
 TILE = CH * BLOCK
 JOBS = [(i, j) for j in range(NC) for i in range(j, NC)]
 LAST = (NC - 1, NC - 1)
@@ -23,7 +23,7 @@
 NR = 2
 O_PARTS = ((12, 4), (0, 4), (4, 4), (8, 3), (11, 1))
 NX = NC + len(O_PARTS)
-EXTRA = [(3, 0), (3, 1)]
+EXTRA = [(3, 0), (3, 1), (3, 2)]
 LATER = [job for job in JOBS if job not in EXTRA]
 PANELS = [(i, j, 0) for i, j in NOW] + [(i, j, 1) for i, j in EXTRA]
 
@@ -254,10 +254,11 @@
         if c == 1:
             o_copy.wait_recv()
             relay_copy(NC).wait_recv()
-            for m, (i, j) in enumerate(EXTRA):
-                full_tile(t_ref.at[len(NOW) + m], o_ref, (), i, sc_ref, (side,), j)
         if c == 2:
             o_step(c + 1)
+        for m, (i, j) in enumerate(EXTRA):
+            if c == max(j, 1):
+                full_tile(t_ref.at[len(NOW) + m], o_ref, (), i, sc_ref, (side,), j)
 
     for n in range(1, len(O_PARTS)):
         relay_copy(NC + n).wait_recv()

time: 63.8 us -> 64.4 us (level)
  no operation moved by 1% of the time
where the time goes in v14:
time: 64.4 us; the launch traced here: 64.3 us
  Pallas kernels  64.2 us (100%)
    pallas_call x1, Pallas kernels, local_fn(): pl.pallas_call(gather_kernel, out_shape=[panels, rest, pltpu.VMEM((len(PA...  42.1 us
    pallas_call x1, Pallas kernels, local_fn(): pl.pallas_call(write_kernel, out_shape=jax.ShapeDtypeStruct((NM, 2, BLOCK...  11.6 us
    pallas_call x1, Pallas kernels, local_fn(): pl.pallas_call(zero_kernel, out_shape=[jax.ShapeDtypeStruct((NM, 2, BLOCK...  10.5 us

profile of v14, /device:TPU:0, one launch (start us, length us, event | category | flops | bytes accessed | tf_op | source)
XLA Modules:
  0.0 64.3 jit_solution(880228227731627919)
XLA Ops:
  0.0 10.5 %shard_map.18 = (bf16[16,2,256,4096]{3,2,1,0:T(8,128)(2,1)}, f32[8,128]{1,0:T(8,128)S(1)}, bf16[2,4,16,256,128]{4,3,2,1,0:T(8,128)(2,1)S(1)}, bf16[4,16,256,128]{3,2,1,0:T(8,128)(2,1)S(1)}) custom-call(f32[8,128]{1,0:T(8,128)S(1)} %get-tuple-element.14.token_ref, bf16[16,2,256,128]{3,2,1,0:T(8,128)(2,1)} %bitcast.3, ...), custom_call_target="tpu_custom_call", output_to_operand_aliasing={{2}: (2, {})} | custom-call | flops 9126805504 | bytes 31457280 | tf_op jit(solution)/shard_map/pallas_call | solution.py:391
  10.6 42.1 %shard_map.19 = (bf16[2,4,16,256,128]{4,3,2,1,0:T(8,128)(2,1)S(1)}, bf16[4,16,256,128]{3,2,1,0:T(8,128)(2,1)S(1)}, bf16[12,4,256,1024]{3,2,1,0:T(8,128)(2,1)S(1)}) custom-call(bf16[2,4,16,256,128]{4,3,2,1,0:T(8,128)(2,1)S(1)} %get-tuple-element.16.sc_in, ...), custom_call_target="tpu_custom_call", output_to_operand_aliasing={{0}: (0, {}), {1}: (1, {})} | custom-call | flops 9126805504 | bytes 2097152 | tf_op jit(solution)/shard_map/pallas_call | solution.py:401
  52.7 11.6 %shard_map.20 = bf16[16,2,256,4096]{3,2,1,0:T(8,128)(2,1)} custom-call(bf16[2,4,16,256,128]{4,3,2,1,0:T(8,128)(2,1)S(1)} %get-tuple-element.19.sc_ref, bf16[4,16,256,128]{3,2,1,0:T(8,128)(2,1)S(1)} %get-tuple-element.20.o_ref, bf16[12,4,256,1024]{3,2,1,0:T(8,128)(2,1)S(1)} %get-tuple-element.21.t_ref, ...), custom_call_target="tpu_custom_call", output_to_operand_aliasing={{}: (3, {})} | custom-call | flops 9126805504 | bytes 35651584 | tf_op jit(solution)/shard_map/pallas_call | solution.py:415
  (1 shorter events, 0.0 us)

commit v15 on v12

--- a/solution.py
+++ b/solution.py
@@ -199,8 +199,6 @@
         pl.semaphore_wait(barrier, 4)
         signal(join, (partner, y_early))
         x_tail.start()
-        for n in range(NC, NX):
-            x_copy(n).start()
         for c in range(NC - 1):
             y_copy(1, c).start()
         u_copy.start()
@@ -243,6 +241,11 @@
         if c < NC - 1:
             base = NOW.index((c, c))
             diag_tile(t_ref.at[base], sc_ref, (0,), sc_ref, (side,), c, row_blk, col)
+            if c == 0:
+                @pl.when(late)
+                def _():
+                    for n in range(NC, NX):
+                        x_copy(n).start()
 
             def body(i, _):
                 if c == 0:

time: 63.8 us -> 63.9 us (level)
  no operation moved by 1% of the time
where the time goes in v15:
time: 63.9 us; the launch traced here: 63.8 us
  Pallas kernels  63.8 us (100%)
    pallas_call x1, Pallas kernels, local_fn(): pl.pallas_call(gather_kernel, out_shape=[panels, rest, pltpu.VMEM((len(PA...  41.7 us
    pallas_call x1, Pallas kernels, local_fn(): pl.pallas_call(write_kernel, out_shape=jax.ShapeDtypeStruct((NM, 2, BLOCK...  11.6 us
    pallas_call x1, Pallas kernels, local_fn(): pl.pallas_call(zero_kernel, out_shape=[jax.ShapeDtypeStruct((NM, 2, BLOCK...  10.5 us

profile of v15, /device:TPU:0, one launch (start us, length us, event | category | flops | bytes accessed | tf_op | source)
XLA Modules:
  0.0 63.8 jit_solution(12618339492902487024)
XLA Ops:
  0.0 10.5 %shard_map.18 = (bf16[16,2,256,4096]{3,2,1,0:T(8,128)(2,1)}, f32[8,128]{1,0:T(8,128)S(1)}, bf16[2,4,16,256,128]{4,3,2,1,0:T(8,128)(2,1)S(1)}, bf16[4,16,256,128]{3,2,1,0:T(8,128)(2,1)S(1)}) custom-call(f32[8,128]{1,0:T(8,128)S(1)} %get-tuple-element.14.token_ref, bf16[16,2,256,128]{3,2,1,0:T(8,128)(2,1)} %bitcast.3, ...), custom_call_target="tpu_custom_call", output_to_operand_aliasing={{2}: (2, {})} | custom-call | flops 9126805504 | bytes 31457280 | tf_op jit(solution)/shard_map/pallas_call | solution.py:393
  10.6 41.7 %shard_map.19 = (bf16[2,4,16,256,128]{4,3,2,1,0:T(8,128)(2,1)S(1)}, bf16[4,16,256,128]{3,2,1,0:T(8,128)(2,1)S(1)}, bf16[11,4,256,1024]{3,2,1,0:T(8,128)(2,1)S(1)}) custom-call(bf16[2,4,16,256,128]{4,3,2,1,0:T(8,128)(2,1)S(1)} %get-tuple-element.16.sc_in, ...), custom_call_target="tpu_custom_call", output_to_operand_aliasing={{0}: (0, {}), {1}: (1, {})} | custom-call | flops 9126805504 | bytes 2097152 | tf_op jit(solution)/shard_map/pallas_call | solution.py:403
  52.3 11.6 %shard_map.20 = bf16[16,2,256,4096]{3,2,1,0:T(8,128)(2,1)} custom-call(bf16[2,4,16,256,128]{4,3,2,1,0:T(8,128)(2,1)S(1)} %get-tuple-element.19.sc_ref, bf16[4,16,256,128]{3,2,1,0:T(8,128)(2,1)S(1)} %get-tuple-element.20.o_ref, bf16[11,4,256,1024]{3,2,1,0:T(8,128)(2,1)S(1)} %get-tuple-element.21.t_ref, ...), custom_call_target="tpu_custom_call", output_to_operand_aliasing={{}: (3, {})} | custom-call | flops 9126805504 | bytes 35651584 | tf_op jit(solution)/shard_map/pallas_call | solution.py:417
  (1 shorter events, 0.0 us)

commit v16 on v12

--- a/solution.py
+++ b/solution.py
@@ -19,7 +19,7 @@
 JOBS = [(i, j) for j in range(NC) for i in range(j, NC)]
 LAST = (NC - 1, NC - 1)
 NOW = [job for job in JOBS if job != LAST]
-NAX, NAY = 15, 15
+NAX, NAY = 16, 16
 NR = 2
 O_PARTS = ((12, 4), (0, 4), (4, 4), (8, 3), (11, 1))
 NX = NC + len(O_PARTS)
@@ -119,7 +119,7 @@
 
 
 def gather_kernel(sc_in, o_in, token_ref, sc_ref, o_ref, t_ref, yb, yr, join, d_send, d_recv, x_send, x_recv, r_send, r_recv,
-                  y_send, y_recv, b_send, b_recv, q_send, q_recv, u_send, u_recv, v_send, v_recv):
+                  y_send, y_recv, b_send, b_recv, q_send, q_recv):
     y, x, k, col = positions()
     late = k != y
     early = k == y
@@ -128,7 +128,6 @@
     x_peer = (0, y, 2 * (1 - x) + k)
     y_early = (0, 1 - y, 2 * x + 1 - y)
     y_late = (0, 1 - y, 2 * x + y)
-    tx, ty = pl.ds(NAX, NM - NAX), pl.ds(NAY, NM - NAY)
 
     def x_copy(n):
         if n < NC:
@@ -161,8 +160,6 @@
     yr_part = pl.ds(0, NR * CH)
     yr_copy = remote(sc_ref.at[0, 2, yr_part], yr, q_send, q_recv, y_early)
     yb_copy = remote(sc_ref.at[0, 0], yb, b_send.at[0], b_recv.at[0], y_early)
-    x_tail = remote(o_ref.at[0, tx], sc_ref.at[0, 2, tx], v_send, v_recv, x_peer)
-    u_copy = remote(sc_ref.at[0, 0, ty], sc_ref.at[1, 1, ty], u_send, u_recv, y_late)
     o_copy = remote(o_ref.at[0], o_ref.at[1], d_send.at[NC], d_recv.at[NC], partner)
     barrier = pltpu.get_barrier_semaphore()
 
@@ -198,18 +195,15 @@
         signal(barrier, (x_peer, y_late))
         pl.semaphore_wait(barrier, 4)
         signal(join, (partner, y_early))
-        x_tail.start()
         for n in range(NC, NX):
             x_copy(n).start()
         for c in range(NC - 1):
             y_copy(1, c).start()
-        u_copy.start()
         for c in range(NC):
             s_copy(c).start()
             if c < NC - 1:
                 relay_copy(c).start()
         o_copy.start()
-        x_tail.wait_recv()
         relay_copy(NC - 1).start()
         y_copy(1, NC - 1).start()
 
@@ -235,8 +229,6 @@
         @pl.when(late)
         def _():
             yb_relay(c).wait_recv()
-            if c == NC - 1:
-                u_copy.wait_recv()
             for s in range(2):
                 y_copy(s, c).wait_recv()
 
@@ -269,11 +261,6 @@
         s_copy(c).wait_send()
         y_copy(0, c).wait_send()
     o_copy.wait_send()
-
-    @pl.when(late)
-    def _():
-        u_copy.wait_send()
-        x_tail.wait_send()
 
     @pl.when(early)
     def _():
@@ -407,7 +394,7 @@
             scratch_shapes=[pltpu.VMEM((NM, BLOCK, PIECE), jnp.bfloat16), pltpu.VMEM((NR * CH, BLOCK, PIECE), jnp.bfloat16),
                             pltpu.SemaphoreType.REGULAR,
                             dma((NC + 1,)), dma((NC + 1,)), dma((NX,)), dma((NX,)), dma((NX,)), dma((NX,)),
-                            dma((NC,)), dma((2, NC)), dma((NC + 1,)), dma((NC + 1,)), dma(()), dma(())] + [dma(())] * 4,
+                            dma((NC,)), dma((2, NC)), dma((NC + 1,)), dma((NC + 1,)), dma(()), dma(())],
             compiler_params=pltpu.CompilerParams(collective_id=1, has_side_effects=True, vmem_limit_bytes=8 * 1024 * 1024),
             cost_estimate=pl.CostEstimate(flops=half_flops, bytes_accessed=2 << 20, transcendentals=0),
         )(sc, o, zeroed)

time: 63.8 us -> 64.6 us (1.013)
  Pallas kernels: 63.7 us -> 64.5 us
    pallas_call x1, Pallas kernels: 41.6 us -> 42.4 us  [local_fn(): pl.pallas_call(gather_kernel, out_shape=[panels, rest, pltpu.VMEM((len(PA...]
where the time goes in v16:
time: 64.6 us; the launch traced here: 64.5 us
  Pallas kernels  64.5 us (100%)
    pallas_call x1, Pallas kernels, local_fn(): pl.pallas_call(gather_kernel, out_shape=[panels, rest, pltpu.VMEM((len(PA...  42.4 us
    pallas_call x1, Pallas kernels, local_fn(): pl.pallas_call(write_kernel, out_shape=jax.ShapeDtypeStruct((NM, 2, BLOCK...  11.6 us
    pallas_call x1, Pallas kernels, local_fn(): pl.pallas_call(zero_kernel, out_shape=[jax.ShapeDtypeStruct((NM, 2, BLOCK...  10.5 us

profile of v16, /device:TPU:0, one launch (start us, length us, event | category | flops | bytes accessed | tf_op | source)
XLA Modules:
  0.0 64.5 jit_solution(15124683859898963166)
XLA Ops:
  0.0 10.5 %shard_map.18 = (bf16[16,2,256,4096]{3,2,1,0:T(8,128)(2,1)}, f32[8,128]{1,0:T(8,128)S(1)}, bf16[2,4,16,256,128]{4,3,2,1,0:T(8,128)(2,1)S(1)}, bf16[4,16,256,128]{3,2,1,0:T(8,128)(2,1)S(1)}) custom-call(f32[8,128]{1,0:T(8,128)S(1)} %get-tuple-element.14.token_ref, bf16[16,2,256,128]{3,2,1,0:T(8,128)(2,1)} %bitcast.3, ...), custom_call_target="tpu_custom_call", output_to_operand_aliasing={{2}: (2, {})} | custom-call | flops 9126805504 | bytes 31457280 | tf_op jit(solution)/shard_map/pallas_call | solution.py:377
  10.6 42.4 %shard_map.19 = (bf16[2,4,16,256,128]{4,3,2,1,0:T(8,128)(2,1)S(1)}, bf16[4,16,256,128]{3,2,1,0:T(8,128)(2,1)S(1)}, bf16[11,4,256,1024]{3,2,1,0:T(8,128)(2,1)S(1)}) custom-call(bf16[2,4,16,256,128]{4,3,2,1,0:T(8,128)(2,1)S(1)} %get-tuple-element.16.sc_in, ...), custom_call_target="tpu_custom_call", output_to_operand_aliasing={{0}: (0, {}), {1}: (1, {})} | custom-call | flops 9126805504 | bytes 2097152 | tf_op jit(solution)/shard_map/pallas_call | solution.py:387
  52.9 11.6 %shard_map.20 = bf16[16,2,256,4096]{3,2,1,0:T(8,128)(2,1)} custom-call(bf16[2,4,16,256,128]{4,3,2,1,0:T(8,128)(2,1)S(1)} %get-tuple-element.19.sc_ref, bf16[4,16,256,128]{3,2,1,0:T(8,128)(2,1)S(1)} %get-tuple-element.20.o_ref, bf16[11,4,256,1024]{3,2,1,0:T(8,128)(2,1)S(1)} %get-tuple-element.21.t_ref, ...), custom_call_target="tpu_custom_call", output_to_operand_aliasing={{}: (3, {})} | custom-call | flops 9126805504 | bytes 35651584 | tf_op jit(solution)/shard_map/pallas_call | solution.py:401
  (1 shorter events, 0.0 us)

commit v17 on v12

--- a/solution.py
+++ b/solution.py
@@ -19,7 +19,7 @@
 JOBS = [(i, j) for j in range(NC) for i in range(j, NC)]
 LAST = (NC - 1, NC - 1)
 NOW = [job for job in JOBS if job != LAST]
-NAX, NAY = 15, 15
+NAX, NAY = 14, 14
 NR = 2
 O_PARTS = ((12, 4), (0, 4), (4, 4), (8, 3), (11, 1))
 NX = NC + len(O_PARTS)

time: 63.8 us -> 64.5 us (1.011)
  Pallas kernels: 63.7 us -> 64.4 us
    pallas_call x1, Pallas kernels: 41.6 us -> 42.3 us  [local_fn(): pl.pallas_call(gather_kernel, out_shape=[panels, rest, pltpu.VMEM((len(PA...]
where the time goes in v17:
time: 64.5 us; the launch traced here: 64.4 us
  Pallas kernels  64.4 us (100%)
    pallas_call x1, Pallas kernels, local_fn(): pl.pallas_call(gather_kernel, out_shape=[panels, rest, pltpu.VMEM((len(PA...  42.3 us
    pallas_call x1, Pallas kernels, local_fn(): pl.pallas_call(write_kernel, out_shape=jax.ShapeDtypeStruct((NM, 2, BLOCK...  11.6 us
    pallas_call x1, Pallas kernels, local_fn(): pl.pallas_call(zero_kernel, out_shape=[jax.ShapeDtypeStruct((NM, 2, BLOCK...  10.5 us

profile of v17, /device:TPU:0, one launch (start us, length us, event | category | flops | bytes accessed | tf_op | source)
XLA Modules:
  0.0 64.4 jit_solution(11742235219557038740)
XLA Ops:
  0.0 10.5 %shard_map.18 = (bf16[16,2,256,4096]{3,2,1,0:T(8,128)(2,1)}, f32[8,128]{1,0:T(8,128)S(1)}, bf16[2,4,16,256,128]{4,3,2,1,0:T(8,128)(2,1)S(1)}, bf16[4,16,256,128]{3,2,1,0:T(8,128)(2,1)S(1)}) custom-call(f32[8,128]{1,0:T(8,128)S(1)} %get-tuple-element.14.token_ref, bf16[16,2,256,128]{3,2,1,0:T(8,128)(2,1)} %bitcast.3, ...), custom_call_target="tpu_custom_call", output_to_operand_aliasing={{2}: (2, {})} | custom-call | flops 9126805504 | bytes 31457280 | tf_op jit(solution)/shard_map/pallas_call | solution.py:390
  10.6 42.3 %shard_map.19 = (bf16[2,4,16,256,128]{4,3,2,1,0:T(8,128)(2,1)S(1)}, bf16[4,16,256,128]{3,2,1,0:T(8,128)(2,1)S(1)}, bf16[11,4,256,1024]{3,2,1,0:T(8,128)(2,1)S(1)}) custom-call(bf16[2,4,16,256,128]{4,3,2,1,0:T(8,128)(2,1)S(1)} %get-tuple-element.16.sc_in, ...), custom_call_target="tpu_custom_call", output_to_operand_aliasing={{0}: (0, {}), {1}: (1, {})} | custom-call | flops 9126805504 | bytes 2097152 | tf_op jit(solution)/shard_map/pallas_call | solution.py:400
  52.8 11.6 %shard_map.20 = bf16[16,2,256,4096]{3,2,1,0:T(8,128)(2,1)} custom-call(bf16[2,4,16,256,128]{4,3,2,1,0:T(8,128)(2,1)S(1)} %get-tuple-element.19.sc_ref, bf16[4,16,256,128]{3,2,1,0:T(8,128)(2,1)S(1)} %get-tuple-element.20.o_ref, bf16[11,4,256,1024]{3,2,1,0:T(8,128)(2,1)S(1)} %get-tuple-element.21.t_ref, ...), custom_call_target="tpu_custom_call", output_to_operand_aliasing={{}: (3, {})} | custom-call | flops 9126805504 | bytes 35651584 | tf_op jit(solution)/shard_map/pallas_call | solution.py:414
  (1 shorter events, 0.0 us)
